TPU v7x, 512 devices: a 8x2x16 block of a 8x8x16 slice. The times are simulated.
512 devices in a mesh: grp: 2 (over y), ep: 16 (over z), tp: 8 (over x), mb: 2 (over core).
Axes of the slice: x: 8, y: 2, z: 16, core: 2. Of those that a mesh axis runs over, the one named last changes fastest.
The devices are a block of a 8x8x16 slice.
Arguments:
- hidden: bfloat16 [1024, 3584], P(('grp', 'ep', 'mb'), 'tp'), parts along dimension 0, may hold values from -12 to 12
- moe_gain: float32 [3584], P('tp'), may hold values from 0.1 to 1.9
- expert_ids: int32 [1024, 8], P(('grp', 'ep', 'mb')), parts along dimension 0, may hold values from 0 to 31, as said below
- slots: int32 [1024, 8], P(('grp', 'ep', 'mb')), parts along dimension 0, may hold values from 0 to 15, as said below
- affinity: float32 [1024, 8], P(('grp', 'ep', 'mb')), parts along dimension 0, may hold values from 0.05 to 1
- w_gate: bfloat16 [32, 3584, 1024], P(('ep', 'mb'), None, 'tp'), may hold values from -0.09375 to 0.09375
- w_up: bfloat16 [32, 3584, 1024], P(('ep', 'mb'), None, 'tp'), may hold values from -0.09375 to 0.09375
- w_down: bfloat16 [32, 1024, 3584], P(('ep', 'mb'), 'tp'), may hold values from -0.1875 to 0.1875
- attn_gain: float32 [3584], P('tp'), may hold values from 0.1 to 1.9
- w_dkv: bfloat16 [3584, 576], P('tp'), may hold values from -0.09375 to 0.09375
- kv_gain: float32 [512], replicated, may hold values from 0.1 to 1.9
- queries: bfloat16 [1024, 64, 576], P(('grp', 'ep', 'mb'), 'tp'), parts along dimension 0, may hold values from -36 to 36
- cache: bfloat16 [1024, 128, 576], P(('grp', 'ep', 'mb'), 'tp'), parts along dimension 0, may hold values from -4 to 4
- lengths: int32 [1024], P(('grp', 'ep', 'mb')), parts along dimension 0, may hold values from 2 to 128
Outputs:
- next_hidden: bfloat16 [1024, 3584], P(('grp', 'ep', 'mb'), 'tp'), parts along dimension 0
- latent_out: bfloat16 [1024, 64, 512], P(('grp', 'ep', 'mb'), 'tp'), parts along dimension 0
There are 2 independent parts, one for each index of `grp`. A program takes and returns all parts, laid end to end along the dimension named above; an argument that names none is the same for every part. Nothing has to cross between parts.
Inputs may be any that keep to these rules, and one draw needn't show every extreme that they name: `expert_ids`: each row names 8 different experts; in every draw some expert is named by every token. slots[t, k] is the rank of the choice (t, k) among the choices of the same expert made by the 16 tokens of one device; these ranks are distinct and run from 0 upward. A choice whose slot is 8 or more is dropped.
All inputs are finite; a program needn't handle non-finite values.
Results may differ from a plain program's by a relative error of at most 0.017.
Values may be sent and summed in bfloat16 or wider, within the bound.
No kernel may reach another device: no remote copies, remote signals or barrier semaphores. Data moves between devices by JAX's collectives and lax.ppermute only.
A program may use at most 128 MiB of HBM per device.

v0:
```python
import jax
import jax.numpy as jnp
from jax import lax
from jax.sharding import PartitionSpec as P

D = 3584
LAT = 512
CAP = 8


epsilon = 1e-06
route_scale = 2.5
score_scale = 192.0 ** (-0.5)


def sent_to_all(x, axis):
    copies = jnp.broadcast_to(x, (lax.axis_size(axis), *x.shape))
    return lax.all_to_all(copies, axis, split_axis=0, concat_axis=0, tiled=True)


def over_copies(x, axis):
    everything = sent_to_all(x, axis)
    return jnp.sum(everything, axis=0)


def joined_along(tiles, dim):
    tiles = jnp.moveaxis(tiles, 0, dim)
    lengths = tiles.shape
    return tiles.reshape(*lengths[:dim], lengths[dim] * lengths[dim + 1], *lengths[dim + 2 :])


def gathered_copies(x, axis, dim):
    tiles = sent_to_all(x, axis)
    return joined_along(tiles, dim)


def in_blocks(x, dim, peers):
    before, after = (x.shape[:dim], x.shape[dim + 1 :])
    return jnp.moveaxis(x.reshape(*before, peers, -1, *after), dim, 0)


def sum_at_owner(x, axis, dim):
    peers = lax.axis_size(axis)
    tiles = lax.all_to_all(in_blocks(x, dim, peers), axis, 0, 0, tiled=True)
    return jnp.sum(tiles.astype(jnp.float32), axis=0)


def taken_together(x, axis):
    everything = sent_to_all(x, axis)
    return jnp.sum(everything.astype(jnp.float32), axis=0)


def rope_rotate(rope_part, position):
    half_rope = rope_part.shape[-1] // 2
    inv_freq = 10000.0 ** (-jnp.arange(half_rope, dtype=jnp.float32) / half_rope)
    angles = position[:, None] * inv_freq[None, :]
    cos_table = jnp.cos(angles)
    sin_table = jnp.sin(angles)
    first_half = rope_part[:, :half_rope]
    second_half = rope_part[:, half_rope:]
    return jnp.concatenate(
        [
            first_half * cos_table - second_half * sin_table,
            first_half * sin_table + second_half * cos_table,
        ],
        1,
    )


def local(
    hidden,
    moe_gain,
    expert_ids,
    slots,
    affinity,
    w_gate,
    w_up,
    w_down,
    attn_gain,
    w_dkv,
    kv_gain,
    queries,
    cache,
    lengths,
):
    tok_rows, width = hidden.shape
    experts = lax.axis_size("ep") * lax.axis_size("mb")
    slot_rows = experts * CAP
    hidden_wide = hidden.astype(jnp.float32)
    square = over_copies(jnp.sum(hidden_wide * hidden_wide, -1), "tp")
    normed = (hidden_wide * lax.rsqrt(square[:, None] / D + epsilon) * moe_gain).astype(
        jnp.bfloat16
    )
    kept_rows = slots < CAP
    weight = (
        route_scale
        * affinity
        / jnp.sum(affinity, -1, keepdims=True)
        * kept_rows.astype(jnp.float32)
    )
    target = jnp.where(kept_rows, expert_ids * CAP + slots, -1)
    matches = target[None, :, :] == jnp.arange(slot_rows, dtype=jnp.int32)[:, None, None]
    dispatch = jnp.any(matches, 2).astype(jnp.bfloat16)
    combine = jnp.sum(jnp.where(matches, weight[None, :, :], 0.0), 2).T
    gate_weight = w_gate[0]
    up_weight = w_up[0]
    down_weight = w_down[0]
    send_rows = jnp.dot(dispatch, normed, preferred_element_type=jnp.float32).astype(jnp.bfloat16)
    arrived = lax.all_to_all(
        send_rows.reshape(experts, CAP, width),
        ("ep", "mb"),
        split_axis=0,
        concat_axis=0,
        tiled=True,
    )
    portion = gathered_copies(arrived, "tp", 2)
    columns = portion.shape[2]
    flattened = portion.reshape(slot_rows, columns)
    gate_act = jnp.dot(flattened, gate_weight, preferred_element_type=jnp.float32)
    up_act = jnp.dot(flattened, up_weight, preferred_element_type=jnp.float32)
    units = (jax.nn.silu(gate_act) * up_act).astype(jnp.bfloat16)
    partial_out = jnp.dot(units, down_weight, preferred_element_type=jnp.float32)
    summed = sum_at_owner(partial_out.reshape(experts, CAP, D).astype(jnp.bfloat16), "tp", 2)
    returned = (
        lax.all_to_all(
            summed.astype(jnp.bfloat16), ("ep", "mb"), split_axis=0, concat_axis=0, tiled=True
        )
        .astype(summed.dtype)
        .reshape(slot_rows, width)
    )
    moe_out = jnp.dot(combine, returned)
    next_hidden = (hidden_wide + moe_out).astype(jnp.bfloat16)
    next_wide = next_hidden.astype(jnp.float32)
    square_attn = over_copies(jnp.sum(next_wide * next_wide, -1), "tp")
    normed_attn = (next_wide * lax.rsqrt(square_attn[:, None] / D + epsilon) * attn_gain).astype(
        jnp.bfloat16
    )
    down_kv = taken_together(
        jnp.dot(normed_attn, w_dkv, preferred_element_type=jnp.float32).astype(jnp.bfloat16), "tp"
    ).astype(jnp.float32)
    latent_part = down_kv[:, :LAT]
    latent_part = (
        latent_part
        * lax.rsqrt(jnp.mean(latent_part * latent_part, -1, keepdims=True) + epsilon)
        * kv_gain
    )
    rope_part = rope_rotate(down_kv[:, LAT:], lengths.astype(jnp.float32))
    new_key = jnp.concatenate([latent_part, rope_part], 1).astype(jnp.bfloat16)
    own_score = (
        jnp.einsum("bhc,bc->bh", queries, new_key, preferred_element_type=jnp.float32) * score_scale
    )
    full_cache = lax.all_gather(cache, "tp", axis=1, tiled=True)
    position = jnp.arange(full_cache.shape[1], dtype=jnp.int32)
    live_mask = (position[None, :] < lengths[:, None])[:, None, :]
    scores = (
        jnp.einsum("bhc,bjc->bhj", queries, full_cache, preferred_element_type=jnp.float32)
        * score_scale
    )
    scores = jnp.where(live_mask, scores, -1e30)
    peak_all = jnp.maximum(jnp.max(scores, -1), own_score)
    prob_live = jnp.where(live_mask, jnp.exp(scores - peak_all[:, :, None]), 0.0)
    own_prob = jnp.exp(own_score - peak_all)
    denominator = jnp.sum(prob_live, -1) + own_prob
    numerator = jnp.einsum(
        "bhj,bjc->bhc",
        prob_live.astype(jnp.bfloat16),
        full_cache[:, :, :LAT],
        preferred_element_type=jnp.float32,
    )
    numerator = numerator + own_prob.astype(jnp.bfloat16).astype(jnp.float32)[:, :, None] * new_key[
        :, None, :LAT
    ].astype(jnp.float32)
    latent_out = (numerator / denominator[:, :, None]).astype(jnp.bfloat16)
    return (next_hidden, latent_out)


def solution(mesh):
    return jax.shard_map(
        local,
        mesh=mesh,
        in_specs=(
            P(("grp", "ep", "mb"), "tp"),
            P("tp"),
            P(("grp", "ep", "mb"), None),
            P(("grp", "ep", "mb"), None),
            P(("grp", "ep", "mb"), None),
            P(("ep", "mb"), None, "tp"),
            P(("ep", "mb"), None, "tp"),
            P(("ep", "mb"), "tp", None),
            P("tp"),
            P("tp", None),
            P(),
            P(("grp", "ep", "mb"), "tp", None),
            P(("grp", "ep", "mb"), "tp", None),
            P(("grp", "ep", "mb")),
        ),
        out_specs=(P(("grp", "ep", "mb"), "tp"), P(("grp", "ep", "mb"), "tp", None)),
        check_vma=False,
    )
```

profile of v0, /device:TPU:80, one launch (start us, length us, event | category | flops | bytes accessed | tf_op | source)
XLA Modules:
  0.0 303.1 jit_solution(17806892856432269811)
XLA Ops:
  7.2 0.9 fusion.36
  8.1 0.6 broadcast_in_dim.68
  8.7 7.3 %all-to-all-start = ((f32[8,1,16]{2,1,0:T(1,128)}), f32[8,1,16]{2,1,0:T(1,128)S(1)}, u32[]{:S(2)}, u32[]{:S(2)}) async-start(f32[8,1,16]{2,1,0:T(1,128)} %broadcast_in_dim.68), calls=%async_computation | async-start | bytes 8192 | tf_op jit(solution)/shard_map/all_to_all | solution.py:18
  16.0 0.7 add_select_fusion
  16.7 0.1 copy.32
  16.8 0.1 fusion.27
  16.9 6.7 %all-to-all-done = f32[8,1,16]{2,1,0:T(1,128)S(1)} async-done(((f32[8,1,16]{2,1,0:T(1,128)}), f32[8,1,16]{2,1,0:T(1,128)S(1)}, u32[]{:S(2)}, u32[]{:S(2)}) %all-to-all-start) | async-done | bytes 544 | tf_op jit(solution)/shard_map/all_to_all | solution.py:18
  23.7 1.1 convolution_convert_fusion.1
  24.8 0.1 copy.35
  24.9 66.2 %all_to_all.37 = bf16[32,8,448]{2,1,0:T(8,128)(2,1)S(1)} all-to-all(bf16[32,8,448]{2,1,0:T(8,128)(2,1)S(1)} %bitcast.44), channel_id=1, replica_groups=mesh['grp'=2,'ep'=16,'tp'=8,'mb'=2] {'ep','mb'}, dimensions={0} | all-to-all | bytes 458752 | tf_op jit(solution)/shard_map/all_to_all | solution.py:109
  91.1 0.2 broadcast_in_dim.69
  91.3 54.0 %all_to_all.38 = bf16[8,32,8,448]{3,2,1,0:T(8,128)(2,1)S(1)} all-to-all(bf16[8,32,8,448]{3,2,1,0:T(8,128)(2,1)S(1)} %broadcast_in_dim.69), channel_id=1, replica_groups=mesh['grp'=2,'ep'=16,'tp'=8,'mb'=2] {'tp'}, dimensions={0} | all-to-all | bytes 3670016 | tf_op jit(solution)/shard_map/all_to_all | solution.py:18
  145.4 3.1 %copy.36 = bf16[32,8,8,448]{3,2,1,0:T(8,128)(2,1)} copy(bf16[32,8,8,448]{3,1,0,2:T(8,128)(2,1)S(1)} %bitcast.43) | data formatting | bytes 3670016 | tf_op jit(solution)/shard_map/transpose | solution.py:27
  148.4 3.7 %reshape_reshape.3 = bf16[256,3584]{1,0:T(8,128)(2,1)S(1)} reshape(bf16[32,8,8,448]{3,2,1,0:T(8,128)(2,1)} %copy.36) | data formatting | bytes 3670016 | tf_op jit(solution)/shard_map/reshape;reshape | solution.py:118
  152.1 1.8 fusion.17
  154.0 3.6 %convolution_convert_fusion = bf16[32,8,3584]{2,1,0:T(8,128)(2,1)} fusion(bf16[1,128,3584]{2,1,0:T(8,128)(2,1)S(1)} %copy-done, bf16[256,3584]{1,0:T(8,128)(2,1)S(1)} %reshape_reshape.3, bf16[1,3584,128]{2,1,0:T(8,128)(2,1)} %param.20, f32[256,128]{1,0:T(8,128)S(1)} %fusion.17), kind=kOutput, calls=%fused_computation | convolution fusion | flops 470876160 | bytes 5636096 | tf_op jit(solution)/shard_map/dot_general | solution.py:122
  157.6 3.9 %reshape.83 = bf16[32,8,8,448]{3,2,1,0:T(8,128)(2,1)S(1)} reshape(bf16[32,8,3584]{2,1,0:T(8,128)(2,1)} %convolution_convert_fusion) | data formatting | bytes 3670016 | tf_op jit(solution)/shard_map/reshape | solution.py:39
  161.5 2.0 copy.44
  163.5 3.8 %all-to-all-start.3 = ((bf16[8,32,8,448]{3,2,1,0:T(8,128)(2,1)}), bf16[8,32,8,448]{3,2,1,0:T(8,128)(2,1)S(1)}, u32[]{:S(2)}, u32[]{:S(2)}) async-start(bf16[8,32,8,448]{3,2,1,0:T(8,128)(2,1)} %bitcast.42), calls=%async_computation.3 | async-start | bytes 4194304 | tf_op jit(solution)/shard_map/all_to_all | solution.py:44
  167.4 0.1 all-gather.2.cloned.1.call-start
  167.4 0.7 all-gather.2.cloned.1.call-update
  168.2 66.3 %all-to-all-done.3 = bf16[8,32,8,448]{3,2,1,0:T(8,128)(2,1)S(1)} async-done(((bf16[8,32,8,448]{3,2,1,0:T(8,128)(2,1)}), bf16[8,32,8,448]{3,2,1,0:T(8,128)(2,1)S(1)}, u32[]{:S(2)}, u32[]{:S(2)}) %all-to-all-start.3) | async-done | bytes 1835040 | tf_op jit(solution)/shard_map/all_to_all | solution.py:44
  234.5 1.1 reduce_sum.97
  235.6 4.8 %all-to-all-start.4 = ((bf16[32,8,448]{2,1,0:T(8,128)(2,1)}), bf16[32,8,448]{2,1,0:T(8,128)(2,1)S(1)}, u32[]{:S(2)}, u32[]{:S(2)}) async-start(bf16[32,8,448]{2,1,0:T(8,128)(2,1)} %reduce_sum.97), calls=%async_computation.4 | async-start | bytes 524288 | tf_op jit(solution)/shard_map/all_to_all | solution.py:125
  240.4 0.1 copy.33
  240.5 0.1 select_reduce_fusion
  240.6 0.1 iota_compare_fusion.1
  240.7 21.6 %all-to-all-done.4 = bf16[32,8,448]{2,1,0:T(8,128)(2,1)S(1)} async-done(((bf16[32,8,448]{2,1,0:T(8,128)(2,1)}), bf16[32,8,448]{2,1,0:T(8,128)(2,1)S(1)}, u32[]{:S(2)}, u32[]{:S(2)}) %all-to-all-start.4) | async-done | bytes 229408 | tf_op jit(solution)/shard_map/all_to_all | solution.py:125
  262.3 0.3 fusion.33
  262.6 0.6 broadcast_in_dim.72
  263.2 3.8 %all-to-all-start.5 = ((f32[8,1,16]{2,1,0:T(1,128)}), f32[8,1,16]{2,1,0:T(1,128)S(1)}, u32[]{:S(2)}, u32[]{:S(2)}) async-start(f32[8,1,16]{2,1,0:T(1,128)} %broadcast_in_dim.72), calls=%async_computation.5 | async-start | bytes 8192 | tf_op jit(solution)/shard_map/all_to_all | solution.py:18
  267.0 0.6 multiply_power_fusion
  267.6 0.5 convert_element_type.65
  268.1 6.5 %all-to-all-done.5 = f32[8,1,16]{2,1,0:T(1,128)S(1)} async-done(((f32[8,1,16]{2,1,0:T(1,128)}), f32[8,1,16]{2,1,0:T(1,128)S(1)}, u32[]{:S(2)}, u32[]{:S(2)}) %all-to-all-start.5) | async-done | bytes 544 | tf_op jit(solution)/shard_map/all_to_all | solution.py:18
  274.7 1.3 convolution_convert_fusion.2
  276.0 0.7 broadcast_in_dim.73
  276.7 4.2 %all-to-all-start.6 = ((bf16[8,16,576]{2,1,0:T(8,128)(2,1)}), bf16[8,16,576]{2,1,0:T(8,128)(2,1)}, u32[]{:S(2)}, u32[]{:S(2)}) async-start(bf16[8,16,576]{2,1,0:T(8,128)(2,1)} %broadcast_in_dim.73), calls=%async_computation.6 | async-start | bytes 327680 | tf_op jit(solution)/shard_map/all_to_all | solution.py:18
  280.9 0.0 all-gather.2.cloned.1.call-done
  280.9 3.5 %fusion.61 = (f32[16,8]{1,0:T(8,128)S(1)}, f32[16,8,128]{2,1,0:T(8,128)}) fusion(bf16[16,8,576]{2,1,0:T(8,128)(2,1)} %param.25, bf16[16,128,576]{2,1,0:T(8,128)(2,1)} %all-gather.2.cloned.1.call-done, pred[16,128]{1,0:T(8,128)(4,1)S(1)} %iota_compare_fusion.1), kind=kOutput, calls=%fused_computation.81 | convolution fusion | flops 18923392 | bytes 2574848 | tf_op jit(solution)/shard_map/bhc,bjc->bhj/dot_general | solution.py:156
  284.4 5.7 %all-to-all-done.6 = bf16[8,16,576]{2,1,0:T(8,128)(2,1)} async-done(((bf16[8,16,576]{2,1,0:T(8,128)(2,1)}), bf16[8,16,576]{2,1,0:T(8,128)(2,1)}, u32[]{:S(2)}, u32[]{:S(2)}) %all-to-all-start.6) | async-done | bytes 147488 | tf_op jit(solution)/shard_map/all_to_all | solution.py:18
  290.1 0.9 convert_reduce_fusion
  291.1 0.1 multiply_reduce_fusion
  291.2 0.1 fusion.60
  291.3 0.8 fusion.54
  292.1 0.1 maximum_bitcast_fusion
  292.2 1.1 fusion.31
  293.3 1.0 fusion.29
  294.3 1.9 fusion.8
  (27 shorter events, 0.2 us)
Async XLA Ops:
  7.2 146.8 %copy-start = (bf16[1,128,3584]{2,1,0:T(8,128)(2,1)S(1)}, bf16[1,128,3584]{2,1,0:T(8,128)(2,1)}, u32[]{:S(2)}) copy-start(bf16[1,128,3584]{2,1,0:T(8,128)(2,1)} %param.21) | copy-start | bytes 2752516
  8.7 14.9 %all-to-all-start = ((f32[8,1,16]{2,1,0:T(1,128)}), f32[8,1,16]{2,1,0:T(1,128)S(1)}, u32[]{:S(2)}, u32[]{:S(2)}) async-start(f32[8,1,16]{2,1,0:T(1,128)} %broadcast_in_dim.68), calls=%async_computation | async-start | bytes 8192 | tf_op jit(solution)/shard_map/all_to_all | solution.py:18
  163.5 71.0 %all-to-all-start.3 = ((bf16[8,32,8,448]{3,2,1,0:T(8,128)(2,1)}), bf16[8,32,8,448]{3,2,1,0:T(8,128)(2,1)S(1)}, u32[]{:S(2)}, u32[]{:S(2)}) async-start(bf16[8,32,8,448]{3,2,1,0:T(8,128)(2,1)} %bitcast.42), calls=%async_computation.3 | async-start | bytes 4194304 | tf_op jit(solution)/shard_map/all_to_all | solution.py:44
  167.3 73.0 %copy-start.5 = (f32[16,8]{0,1:T(8,128)S(1)}, f32[16,8]{0,1:T(8,128)}, u32[]{:S(2)}) copy-start(f32[16,8]{0,1:T(8,128)} %param.18) | copy-start | bytes 1540
  167.3 73.1 %copy-start.4 = (s32[16,8]{0,1:T(8,128)S(1)}, s32[16,8]{0,1:T(8,128)}, u32[]{:S(2)}) copy-start(s32[16,8]{0,1:T(8,128)} %param.17) | copy-start | bytes 1540
  167.3 73.3 %copy-start.8 = (s32[16]{0:T(128)S(1)}, s32[16]{0:T(128)}, u32[]{:S(2)}) copy-start(s32[16]{0:T(128)} %param.27) | copy-start | bytes 196
  167.4 95.0 %copy-start.2 = (bf16[16,448]{1,0:T(8,128)(2,1)S(1)}, bf16[16,448]{1,0:T(8,128)(2,1)}, u32[]{:S(2)}) copy-start(bf16[16,448]{1,0:T(8,128)(2,1)} %param.14) | copy-start | bytes 43012
  167.4 107.3 %copy-start.6 = (f32[448]{0:T(512)S(1)}, f32[448]{0:T(512)}, u32[]{:S(2)}) copy-start(f32[448]{0:T(512)} %param.22) | copy-start | bytes 5380
  167.4 113.5 %all-gather.2.cloned.1.call-start = ((), (), s32[]{:S(2)}) async-start(), calls=%async_computation.7 | async-start | bytes 2949120 | tf_op jit(solution)/shard_map/all_gather | solution.py:152
  235.6 26.7 %all-to-all-start.4 = ((bf16[32,8,448]{2,1,0:T(8,128)(2,1)}), bf16[32,8,448]{2,1,0:T(8,128)(2,1)S(1)}, u32[]{:S(2)}, u32[]{:S(2)}) async-start(bf16[32,8,448]{2,1,0:T(8,128)(2,1)} %reduce_sum.97), calls=%async_computation.4 | async-start | bytes 524288 | tf_op jit(solution)/shard_map/all_to_all | solution.py:125
  262.6 18.3 %copy-start.3 = (bf16[16,448]{1,0:T(8,128)(2,1)}, bf16[16,448]{1,0:T(8,128)(2,1)S(1)}, u32[]{:S(2)}) copy-start(bf16[16,448]{1,0:T(8,128)(2,1)S(1)} %get-tuple-element.9) | copy-start | bytes 43012
  263.2 11.4 %all-to-all-start.5 = ((f32[8,1,16]{2,1,0:T(1,128)}), f32[8,1,16]{2,1,0:T(1,128)S(1)}, u32[]{:S(2)}, u32[]{:S(2)}) async-start(f32[8,1,16]{2,1,0:T(1,128)} %broadcast_in_dim.72), calls=%async_computation.5 | async-start | bytes 8192 | tf_op jit(solution)/shard_map/all_to_all | solution.py:18
  274.7 16.5 %copy-start.7 = (f32[512]{0:T(512)S(1)}, f32[512]{0:T(512)}, u32[]{:S(2)}) copy-start(f32[512]{0:T(512)} %param.24) | copy-start | bytes 6148
  276.7 13.5 %all-to-all-start.6 = ((bf16[8,16,576]{2,1,0:T(8,128)(2,1)}), bf16[8,16,576]{2,1,0:T(8,128)(2,1)}, u32[]{:S(2)}, u32[]{:S(2)}) async-start(bf16[8,16,576]{2,1,0:T(8,128)(2,1)} %broadcast_in_dim.73), calls=%async_computation.6 | async-start | bytes 327680 | tf_op jit(solution)/shard_map/all_to_all | solution.py:18
  280.9 13.4 %copy-start.1 = (bf16[16,128,576]{2,1,0:T(8,128)(2,1)S(1)}, bf16[16,128,576]{2,1,0:T(8,128)(2,1)}, u32[]{:S(2)}) copy-start(bf16[16,128,576]{2,1,0:T(8,128)(2,1)} %all-gather.2.cloned.1.call-done) | copy-start | bytes 7077892
Sparse Core Ops, SparseCore 0:
  170.3 70.9 all-gather.1
where the time goes:
time: 304 us; the launch traced here: 303 us
  blocking collectives  120 us (39%)
  waiting for transfers between devices  108 us (36%)
  starting transfers between devices  24 us (8%)
  local copies, waits for them, and re-layouts  15.1 us (5%)
  matrix products  14.6 us (5%)
  between operations  14.3 us (5%)
  other arithmetic  7.28 us (2%)
    all_to_all x1, waiting for transfers between devices, sum_at_owner(): tiles = lax.all_to_all(in_blocks(x, dim, peers), axis, 0, 0, tiled=True)  66.3 us
    all_to_all x1, blocking collectives, local(): lax.all_to_all(send_rows.reshape(experts, CAP, width), ('ep', 'mb'), spli...  66.2 us
    all_to_all x1, blocking collectives, sent_to_all(): return lax.all_to_all(copies, axis, split_axis=0, concat_axis=0, tiled=True)  54 us
    all_to_all x1, waiting for transfers between devices, local(): lax.all_to_all(summed.astype(jnp.bfloat16), ('ep', 'mb'), split_axis=0, c...  21.6 us
    all_to_all x3, waiting for transfers between devices, sent_to_all(): return lax.all_to_all(copies, axis, split_axis=0, concat_axis=0, tiled=True)  19 us
    all_to_all x3, starting transfers between devices, sent_to_all(): return lax.all_to_all(copies, axis, split_axis=0, concat_axis=0, tiled=True)  15.3 us
  transfers between devices with their start and end apart: 6, of which 5 were waited for; matrix products, arithmetic and copies ran while one was open for 3% of the time, Pallas kernels for 0%

commit v1 on v0

v1 whole, which is shorter than its diff:
```python
import jax
import jax.numpy as jnp
from jax import lax
from jax.experimental import pallas as pl
from jax.experimental.pallas import tpu as pltpu
from jax.sharding import PartitionSpec as P

D = 3584
LAT = 512
CAP = 8
EXTRA = 8

epsilon = 1e-06
route_scale = 2.5
score_scale = 192.0 ** (-0.5)
f32 = jnp.float32
bf16 = jnp.bfloat16


def parts_of(x):
    hi = lax.reduce_precision(x, 8, 7)
    mid = lax.reduce_precision(x - hi, 8, 7)
    lo = x - hi - mid
    return hi.astype(bf16), mid.astype(bf16), lo.astype(bf16)


def rope_rotate(rope_part, position):
    half_rope = rope_part.shape[-1] // 2
    inv_freq = 10000.0 ** (-jnp.arange(half_rope, dtype=f32) / half_rope)
    angles = position[:, None] * inv_freq[None, :]
    cos_table = jnp.cos(angles)
    sin_table = jnp.sin(angles)
    first_half = rope_part[:, :half_rope]
    second_half = rope_part[:, half_rope:]
    return jnp.concatenate(
        [
            first_half * cos_table - second_half * sin_table,
            first_half * sin_table + second_half * cos_table,
        ],
        1,
    )


def expert_kernel(x_ref, wg_ref, wu_ref, wd_ref, o_ref, g_ref, u_ref):
    peers, padded, cols = x_ref.shape
    rows = padded - EXTRA
    square = jnp.zeros((rows, 1), f32)
    for j in range(peers):
        x = x_ref[j, :rows, :].astype(f32)
        square = square + jnp.sum(x * x, -1, keepdims=True)
    scale = lax.rsqrt(square / D + epsilon)
    for j in range(peers):
        x = x_ref[j, :rows, :].astype(f32)
        gain = jnp.sum(x_ref[j, rows:, :].astype(f32), 0, keepdims=True)
        normed = (x * scale * gain).astype(bf16)
        part = pl.ds(j * cols, cols)
        gate = jnp.dot(normed, wg_ref[part, :], preferred_element_type=f32)
        up = jnp.dot(normed, wu_ref[part, :], preferred_element_type=f32)
        if j == 0:
            g_ref[...] = gate
            u_ref[...] = up
        else:
            g_ref[...] += gate
            u_ref[...] += up
    gate = g_ref[...]
    units = (gate / (1.0 + jnp.exp(-gate)) * u_ref[...]).astype(bf16)
    for j in range(peers):
        o_ref[j] = jnp.dot(
            units, wd_ref[:, j * cols : (j + 1) * cols], preferred_element_type=f32
        ).astype(bf16)


def expert(x, w_gate, w_up, w_down):
    peers, padded, cols = x.shape
    rows = padded - EXTRA
    hid = w_gate.shape[1]
    vmem = pl.BlockSpec(memory_space=pltpu.VMEM)
    return pl.pallas_call(
        expert_kernel,
        out_shape=jax.ShapeDtypeStruct((peers, rows, cols), bf16),
        in_specs=[vmem] * 4,
        out_specs=vmem,
        scratch_shapes=[pltpu.VMEM((rows, hid), f32), pltpu.VMEM((rows, hid), f32)],
        compiler_params=pltpu.CompilerParams(vmem_limit_bytes=40 * 1024 * 1024),
        name="expert",
    )(x, w_gate, w_up, w_down)


def cached_attention(queries, cache, lengths):
    seqs, heads, keys = queries.shape
    peers = lax.axis_size("tp")
    own = seqs // peers
    span = cache.shape[1]
    both = jnp.concatenate([cache, queries], 1)
    moved = lax.all_to_all(
        both.reshape(peers, own, span + heads, keys), "tp", split_axis=0, concat_axis=0, tiled=True
    )
    full_cache = jnp.moveaxis(moved[:, :, :span], 0, 1).reshape(own, peers * span, keys)
    full_queries = jnp.moveaxis(moved[:, :, span:], 0, 1).reshape(own, peers * heads, keys)
    live_of = lax.dynamic_slice(lengths, (lax.axis_index("tp") * own,), (own,))
    position = jnp.arange(peers * span, dtype=jnp.int32)
    live = (position[None, :] < live_of[:, None])[:, None, :]
    scores = (
        jnp.einsum("bhc,bjc->bhj", full_queries, full_cache, preferred_element_type=f32)
        * score_scale
    )
    scores = jnp.where(live, scores, -1e30)
    peak = jnp.max(scores, -1)
    prob = jnp.where(live, jnp.exp(scores - peak[:, :, None]), 0.0)
    mass = jnp.sum(prob, -1)
    out = jnp.einsum(
        "bhj,bjc->bhc", prob.astype(bf16), full_cache[:, :, :LAT], preferred_element_type=f32
    )
    out = (out / mass[:, :, None]).astype(bf16)
    log_mass = peak + jnp.log(mass)
    tail = jnp.stack(parts_of(log_mass), -1)
    tail = jnp.pad(tail, ((0, 0), (0, 0), (0, 125)))
    back = jnp.concatenate([out, tail], -1).reshape(own, peers, heads, LAT + 128)
    back = lax.all_to_all(
        jnp.moveaxis(back, 1, 0), "tp", split_axis=0, concat_axis=0, tiled=True
    ).reshape(seqs, heads, LAT + 128)
    return back[:, :, :LAT].astype(f32), jnp.sum(back[:, :, LAT : LAT + 3].astype(f32), -1)


def local(
    hidden,
    moe_gain,
    expert_ids,
    slots,
    affinity,
    w_gate,
    w_up,
    w_down,
    attn_gain,
    w_dkv,
    kv_gain,
    queries,
    cache,
    lengths,
):
    tok_rows, width = hidden.shape
    experts = lax.axis_size("ep") * lax.axis_size("mb")
    slot_rows = experts * CAP
    hidden_wide = hidden.astype(f32)
    kept_rows = slots < CAP
    weight = (
        route_scale
        * affinity
        / jnp.sum(affinity, -1, keepdims=True)
        * kept_rows.astype(f32)
    )
    target = jnp.where(kept_rows, expert_ids * CAP + slots, -1)
    matches = target[None, :, :] == jnp.arange(slot_rows, dtype=jnp.int32)[:, None, None]
    dispatch = jnp.any(matches, 2).astype(bf16)
    combine = jnp.sum(jnp.where(matches, weight[None, :, :], 0.0), 2).T
    send_rows = jnp.dot(dispatch, hidden, preferred_element_type=f32).astype(bf16)
    arrived = lax.all_to_all(
        send_rows.reshape(experts, CAP, width),
        ("ep", "mb"),
        split_axis=0,
        concat_axis=0,
        tiled=True,
    ).reshape(slot_rows, width)
    gain_rows = jnp.pad(jnp.stack(parts_of(moe_gain)), ((0, EXTRA - 3), (0, 0)))
    portion = lax.all_gather(jnp.concatenate([arrived, gain_rows], 0), "tp")
    partial_out = expert(portion, w_gate[0], w_up[0], w_down[0])
    summed = lax.psum_scatter(partial_out, "tp")
    returned = lax.all_to_all(
        summed.reshape(experts, CAP, width),
        ("ep", "mb"),
        split_axis=0,
        concat_axis=0,
        tiled=True,
    ).reshape(slot_rows, width)
    moe_out = jnp.dot(combine, returned)
    next_hidden = (hidden_wide + moe_out).astype(bf16)
    next_wide = next_hidden.astype(f32)

    cached_out, cached_mass = cached_attention(queries, cache, lengths)

    keys = w_dkv.shape[1]
    down = jnp.dot(
        (next_wide * attn_gain).astype(bf16), w_dkv, preferred_element_type=f32
    )
    square = jnp.sum(next_wide * next_wide, -1, keepdims=True)
    small = jnp.concatenate([down, jnp.broadcast_to(square, (tok_rows, 64))], 1)
    peers = lax.axis_size("tp")
    shared = jnp.sum(
        lax.all_to_all(
            jnp.broadcast_to(small, (peers, *small.shape)),
            "tp",
            split_axis=0,
            concat_axis=0,
            tiled=True,
        ),
        0,
    )
    down_kv = shared[:, :keys] * lax.rsqrt(shared[:, keys : keys + 1] / D + epsilon)
    latent_part = down_kv[:, :LAT]
    latent_part = (
        latent_part
        * lax.rsqrt(jnp.mean(latent_part * latent_part, -1, keepdims=True) + epsilon)
        * kv_gain
    )
    rope_part = rope_rotate(down_kv[:, LAT:], lengths.astype(f32))
    new_key = jnp.concatenate([latent_part, rope_part], 1).astype(bf16)
    own_score = (
        jnp.einsum("bhc,bc->bh", queries, new_key, preferred_element_type=f32) * score_scale
    )
    peak_all = jnp.maximum(own_score, cached_mass)
    own_prob = jnp.exp(own_score - peak_all)
    cached_prob = jnp.exp(cached_mass - peak_all)
    share = 1.0 / (own_prob + cached_prob)
    latent_out = (
        cached_out * (cached_prob * share)[:, :, None]
        + new_key[:, None, :LAT].astype(f32) * (own_prob * share)[:, :, None]
    ).astype(bf16)
    return (next_hidden, latent_out)


def solution(mesh):
    return jax.shard_map(
        local,
        mesh=mesh,
        in_specs=(
            P(("grp", "ep", "mb"), "tp"),
            P("tp"),
            P(("grp", "ep", "mb"), None),
            P(("grp", "ep", "mb"), None),
            P(("grp", "ep", "mb"), None),
            P(("ep", "mb"), None, "tp"),
            P(("ep", "mb"), None, "tp"),
            P(("ep", "mb"), "tp", None),
            P("tp"),
            P("tp", None),
            P(),
            P(("grp", "ep", "mb"), "tp", None),
            P(("grp", "ep", "mb"), "tp", None),
            P(("grp", "ep", "mb")),
        ),
        out_specs=(P(("grp", "ep", "mb"), "tp"), P(("grp", "ep", "mb"), "tp", None)),
        check_vma=False,
    )
```

time: 304 us -> 246 us (0.81)
  blocking collectives: 120 us -> 0 us
  starting transfers between devices: 24 us -> 70.9 us
  waiting for transfers between devices: 108 us -> 142 us
  matrix products: 14.6 us -> 2.19 us
  local copies, waits for them, and re-layouts: 15.1 us -> 5.82 us
  Pallas kernels: 0 us -> 3.69 us
    all_to_all x2 -> x0, blocking collectives: 120 us -> none  [the longest x1 66.2 us: local(): lax.all_to_all(send_rows.reshape(experts, CAP, width), ('ep', 'mb'), spli...]
    all_to_all x5, starting transfers between devices: 23.9 us -> 70.8 us  [the longest x1 44.4 us: local(): lax.all_to_all(send_rows.reshape(experts, CAP, width), ('ep', 'mb'), spli...]
    all_gather x1, waiting for transfers between devices: 0.02 us -> 38.5 us  [local(): portion = lax.all_gather(jnp.concatenate([arrived, gain_rows], 0), 'tp')]
    all_to_all x5, waiting for transfers between devices: 107 us -> 74.9 us  [the longest x1 21.2 us: local(): lax.all_to_all(send_rows.reshape(experts, CAP, width), ('ep', 'mb'), spli...]
    reduce_scatter x0 -> x1, waiting for transfers between devices: none -> 29 us  [local(): summed = lax.psum_scatter(partial_out, 'tp')]
    dot_general x7 -> x5, matrix products: 14.3 us -> 1.93 us  [the longest x1 0.99 us: local(): jnp.dot(dispatch, hidden, preferred_element_type=f32).astype(bf16)]
    reshape x2 -> x0, local copies, waits for them, and re-layouts: 5.91 us -> none  [in_blocks(): return jnp.moveaxis(x.reshape(*before, peers, -1, *after), dim, 0)]
    reduce_sum x6 -> x3, other arithmetic: 4.02 us -> 0.29 us  [the longest x1 0.18 us: cached_attention(): mass = jnp.sum(prob, -1)]
  transfers between devices with their start and end apart: 6 -> 7, of which waited for: 5 -> 7; matrix products, arithmetic and copies ran while one was open for 3% -> 2% of each run, Pallas kernels for 0% -> 0%
where the time goes in v1:
time: 246 us; the launch traced here: 245 us
  waiting for transfers between devices  142 us (58%)
  starting transfers between devices  70.9 us (29%)
  between operations  14.3 us (6%)
  other arithmetic  6.01 us (2%)
  local copies, waits for them, and re-layouts  5.82 us (2%)
  Pallas kernels  3.69 us (2%)
    all_to_all x1, starting transfers between devices, local(): lax.all_to_all(send_rows.reshape(experts, CAP, width), ('ep', 'mb'), spli...  44.4 us
    all_gather x1, waiting for transfers between devices, local(): portion = lax.all_gather(jnp.concatenate([arrived, gain_rows], 0), 'tp')  38.5 us
    reduce_scatter x1, waiting for transfers between devices, local(): summed = lax.psum_scatter(partial_out, 'tp')  29 us
    all_to_all x1, waiting for transfers between devices, local(): lax.all_to_all(send_rows.reshape(experts, CAP, width), ('ep', 'mb'), spli...  21.2 us
    all_to_all x1, waiting for transfers between devices, local(): lax.all_to_all(summed.reshape(experts, CAP, width), ('ep', 'mb'), split_a...  20.4 us
    all_to_all x1, starting transfers between devices, local(): lax.all_to_all(summed.reshape(experts, CAP, width), ('ep', 'mb'), split_a...  13.9 us
    all_to_all x1, waiting for transfers between devices, cached_attention(): lax.all_to_all(both.reshape(peers, own, span + heads, keys), 'tp', split_...  12.5 us
    all_to_all x1, waiting for transfers between devices, local(): lax.all_to_all(jnp.broadcast_to(small, (peers, *small.shape)), 'tp', spli...  11.5 us
  transfers between devices with their start and end apart: 7, of which 7 were waited for; matrix products, arithmetic and copies ran while one was open for 2% of the time, Pallas kernels for 0%

profile of v1, /device:TPU:80, one launch (start us, length us, event | category | flops | bytes accessed | tf_op | source)
XLA Modules:
  0.0 245.3 jit_solution(10159323954351524624)
XLA Ops:
  7.2 0.9 add_select_fusion
  8.1 0.1 copy.51
  8.1 0.1 fusion.10
  8.3 1.0 convolution_convert_fusion
  9.3 0.8 copy.53
  10.1 44.4 %all-to-all-start = ((bf16[32,8,448]{2,1,0:T(8,128)(2,1)}), bf16[32,8,448]{2,1,0:T(8,128)(2,1)S(1)}, u32[]{:S(2)}, u32[]{:S(2)}) async-start(bf16[32,8,448]{2,1,0:T(8,128)(2,1)} %bitcast), calls=%async_computation | async-start | bytes 524288 | tf_op jit(solution)/shard_map/all_to_all | solution.py:157
  54.6 0.1 all-gather.3.cloned.1.call-start
  54.6 0.7 reduce-precision_convert_fusion.1
  55.4 21.2 %all-to-all-done = bf16[32,8,448]{2,1,0:T(8,128)(2,1)S(1)} async-done(((bf16[32,8,448]{2,1,0:T(8,128)(2,1)}), bf16[32,8,448]{2,1,0:T(8,128)(2,1)S(1)}, u32[]{:S(2)}, u32[]{:S(2)}) %all-to-all-start) | async-done | bytes 229408 | tf_op jit(solution)/shard_map/all_to_all | solution.py:157
  76.5 0.7 pad_maximum_fusion.1
  77.4 38.5 %all-gather.3.cloned.1.call-done = bf16[2112,448]{1,0:T(8,128)(2,1)} async-done(((bf16[264,448]{1,0:T(8,128)(2,1)}), bf16[2112,448]{1,0:T(8,128)(2,1)}) %all-gather.3.cloned.1.call-update) | async-done | bytes 1892368 | tf_op jit(solution)/shard_map/all_gather | solution.py:165
  115.9 1.6 copy-done.1
  117.5 1.2 copy-done.4
  118.7 3.7 %expert.1 = bf16[8,256,448]{2,1,0:T(8,128)(2,1)} custom-call(bf16[8,264,448]{2,1,0:T(8,128)(2,1)S(1)} %bitcast.48, bf16[3584,128]{1,0:T(8,128)(2,1)S(1)} %bitcast.49, bf16[3584,128]{1,0:T(8,128)(2,1)S(1)} %bitcast.50, bf16[128,3584]{1,0:T(8,128)(2,1)S(1)} %bitcast.51), custom_call_target="tpu_custom_call" | custom-call | tf_op jit(solution)/shard_map/expert/pallas_call | solution.py:78
  122.5 0.9 copy-done.5
  123.4 0.8 pad_maximum_fusion
  124.2 4.3 %all-to-all-start.2 = ((bf16[8,2,24,576]{3,2,1,0:T(8,128)(2,1)}), bf16[8,2,24,576]{3,2,1,0:T(8,128)(2,1)S(1)}, u32[]{:S(2)}, u32[]{:S(2)}) async-start(bf16[8,2,24,576]{3,2,1,0:T(8,128)(2,1)} %bitcast.8), calls=%async_computation.3 | async-start | bytes 983040 | tf_op jit(solution)/shard_map/all_to_all | solution.py:95
  128.6 0.1 copy.52
  128.7 0.1 dynamic_slice.3
  128.7 0.1 select_reduce_fusion
  128.9 0.1 iota_compare_fusion.3
  129.0 12.5 %all-to-all-done.2 = bf16[8,2,24,576]{3,2,1,0:T(8,128)(2,1)S(1)} async-done(((bf16[8,2,24,576]{3,2,1,0:T(8,128)(2,1)}), bf16[8,2,24,576]{3,2,1,0:T(8,128)(2,1)S(1)}, u32[]{:S(2)}, u32[]{:S(2)}) %all-to-all-start.2) | async-done | bytes 442400 | tf_op jit(solution)/shard_map/all_to_all | solution.py:95
  141.6 29.0 %reduce-scatter.2.cloned.1.call-done = bf16[1,256,448]{2,1,0:T(8,128)(2,1)} async-done(((bf16[8,256,448]{2,1,0:T(8,128)(2,1)}), bf16[1,256,448]{2,1,0:T(8,128)(2,1)}) %reduce-scatter.2.cloned.1.call-update) | async-done | bytes 229392 | tf_op jit(solution)/shard_map/reduce_scatter | solution.py:167
  170.6 13.9 %all-to-all-start.1 = ((bf16[32,8,448]{2,1,0:T(8,128)(2,1)}), bf16[32,8,448]{2,1,0:T(8,128)(2,1)S(1)}, u32[]{:S(2)}, u32[]{:S(2)}) async-start(bf16[32,8,448]{2,1,0:T(8,128)(2,1)} %bitcast.57), calls=%async_computation.2 | async-start | bytes 524288 | tf_op jit(solution)/shard_map/all_to_all | solution.py:168
  184.4 0.3 fusion.48
  184.8 0.2 fusion.11
  185.0 0.1 copy.57
  185.1 0.2 fusion
  185.4 0.7 copy_bitcast_fusion
  186.0 20.4 %all-to-all-done.1 = bf16[32,8,448]{2,1,0:T(8,128)(2,1)S(1)} async-done(((bf16[32,8,448]{2,1,0:T(8,128)(2,1)}), bf16[32,8,448]{2,1,0:T(8,128)(2,1)S(1)}, u32[]{:S(2)}, u32[]{:S(2)}) %all-to-all-start.1) | async-done | bytes 229408 | tf_op jit(solution)/shard_map/all_to_all | solution.py:168
  206.4 4.5 %all-to-all-start.3 = ((bf16[8,2,8,640]{3,2,1,0:T(8,128)(2,1)}), bf16[8,2,8,640]{3,2,1,0:T(8,128)(2,1)S(1)}, u32[]{:S(2)}, u32[]{:S(2)}) async-start(bf16[8,2,8,640]{3,2,1,0:T(8,128)(2,1)} %copy_bitcast_fusion), calls=%async_computation.4 | async-start | bytes 327680 | tf_op jit(solution)/shard_map/all_to_all | solution.py:119
  210.9 0.3 fusion.16
  211.2 0.2 fusion.21
  211.4 0.1 broadcast_in_dim.66
  211.5 0.1 pad_maximum_fusion.2
  211.5 9.2 %all-to-all-done.3 = bf16[8,2,8,640]{3,2,1,0:T(8,128)(2,1)S(1)} async-done(((bf16[8,2,8,640]{3,2,1,0:T(8,128)(2,1)}), bf16[8,2,8,640]{3,2,1,0:T(8,128)(2,1)S(1)}, u32[]{:S(2)}, u32[]{:S(2)}) %all-to-all-start.3) | async-done | bytes 163872 | tf_op jit(solution)/shard_map/all_to_all | solution.py:119
  220.8 0.7 broadcast_in_dim.67
  221.5 3.6 %all-to-all-start.4 = ((f32[8,16,640]{2,1,0:T(8,128)}), f32[8,16,640]{2,1,0:T(8,128)S(1)}, u32[]{:S(2)}, u32[]{:S(2)}) async-start(f32[8,16,640]{2,1,0:T(8,128)} %broadcast_in_dim.67), calls=%async_computation.5 | async-start | bytes 655360 | tf_op jit(solution)/shard_map/all_to_all | solution.py:189
  225.2 0.1 convert_reduce_fusion
  225.3 11.5 %all-to-all-done.4 = f32[8,16,640]{2,1,0:T(8,128)S(1)} async-done(((f32[8,16,640]{2,1,0:T(8,128)}), f32[8,16,640]{2,1,0:T(8,128)S(1)}, u32[]{:S(2)}, u32[]{:S(2)}) %all-to-all-start.4) | async-done | bytes 327712 | tf_op jit(solution)/shard_map/all_to_all | solution.py:189
  236.8 0.2 fusion.41
  237.0 0.1 slice_multiply_fusion
  237.1 0.1 multiply_reduce_fusion
  237.2 0.1 fusion.47
  237.3 0.1 fusion.32
  237.4 0.1 maximum_bitcast_fusion
  237.5 0.2 fusion.13
  237.7 0.8 add_convert_fusion
  (43 shorter events, 0.5 us)
Async XLA Ops:
  7.2 204.0 %copy-start = (bf16[448,576]{1,0:T(8,128)(2,1)S(1)}, bf16[448,576]{1,0:T(8,128)(2,1)}, u32[]{:S(2)}) copy-start(bf16[448,576]{1,0:T(8,128)(2,1)} %param.23) | copy-start | bytes 1548292
  7.2 108.7 %copy-start.2 = (bf16[1,3584,128]{2,1,0:T(8,128)(2,1)S(1)}, bf16[1,3584,128]{2,1,0:T(8,128)(2,1)}, u32[]{:S(2)}) copy-start(bf16[1,3584,128]{2,1,0:T(8,128)(2,1)} %param.19) | copy-start | bytes 2752516
  7.2 108.7 %copy-start.3 = (bf16[1,3584,128]{2,1,0:T(8,128)(2,1)S(1)}, bf16[1,3584,128]{2,1,0:T(8,128)(2,1)}, u32[]{:S(2)}) copy-start(bf16[1,3584,128]{2,1,0:T(8,128)(2,1)} %param.20) | copy-start | bytes 2752516
  10.1 66.5 %all-to-all-start = ((bf16[32,8,448]{2,1,0:T(8,128)(2,1)}), bf16[32,8,448]{2,1,0:T(8,128)(2,1)S(1)}, u32[]{:S(2)}, u32[]{:S(2)}) async-start(bf16[32,8,448]{2,1,0:T(8,128)(2,1)} %bitcast), calls=%async_computation | async-start | bytes 524288 | tf_op jit(solution)/shard_map/all_to_all | solution.py:157
  54.6 61.4 %all-gather.3.cloned.1.call-start = ((), (), s32[]{:S(2)}) async-start(), calls=%async_computation.7 | async-start | bytes 2433024 | tf_op jit(solution)/shard_map/all_gather | solution.py:165
  77.3 93.2 %reduce-scatter.2.cloned.1.call-start = ((), (), s32[]{:S(2)}) async-start(), calls=%async_computation.6 | async-start | bytes 2359296 | tf_op jit(solution)/shard_map/reduce_scatter | solution.py:167
  115.9 1.6 copy-start.1
  117.5 1.2 copy-start.4
  122.4 1.0 copy-start.5
  122.4 1.0 copy-start.6
  122.4 6.2 %copy-start.10 = (f32[16,8]{0,1:T(8,128)S(1)}, f32[16,8]{0,1:T(8,128)}, u32[]{:S(2)}) copy-start(f32[16,8]{0,1:T(8,128)} %param.18) | copy-start | bytes 1540
  122.4 6.2 %copy-start.9 = (s32[16,8]{0,1:T(8,128)S(1)}, s32[16,8]{0,1:T(8,128)}, u32[]{:S(2)}) copy-start(s32[16,8]{0,1:T(8,128)} %param.17) | copy-start | bytes 1540
  122.4 6.3 %copy-start.13 = (s32[16]{0:T(128)S(1)}, s32[16]{0:T(128)}, u32[]{:S(2)}) copy-start(s32[16]{0:T(128)} %param.27) | copy-start | bytes 196
  124.2 17.3 %all-to-all-start.2 = ((bf16[8,2,24,576]{3,2,1,0:T(8,128)(2,1)}), bf16[8,2,24,576]{3,2,1,0:T(8,128)(2,1)S(1)}, u32[]{:S(2)}, u32[]{:S(2)}) async-start(bf16[8,2,24,576]{3,2,1,0:T(8,128)(2,1)} %bitcast.8), calls=%async_computation.3 | async-start | bytes 983040 | tf_op jit(solution)/shard_map/all_to_all | solution.py:95
  129.0 82.0 %copy-start.8 = (bf16[16,448]{1,0:T(8,128)(2,1)S(1)}, bf16[16,448]{1,0:T(8,128)(2,1)}, u32[]{:S(2)}) copy-start(bf16[16,448]{1,0:T(8,128)(2,1)} %param.14) | copy-start | bytes 43012
  141.5 69.7 %copy-start.11 = (f32[448]{0:T(512)S(1)}, f32[448]{0:T(512)}, u32[]{:S(2)}) copy-start(f32[448]{0:T(512)} %param.22) | copy-start | bytes 5380
  170.6 35.9 %all-to-all-start.1 = ((bf16[32,8,448]{2,1,0:T(8,128)(2,1)}), bf16[32,8,448]{2,1,0:T(8,128)(2,1)S(1)}, u32[]{:S(2)}, u32[]{:S(2)}) async-start(bf16[32,8,448]{2,1,0:T(8,128)(2,1)} %bitcast.57), calls=%async_computation.2 | async-start | bytes 524288 | tf_op jit(solution)/shard_map/all_to_all | solution.py:168
  185.1 52.1 %copy-start.12 = (f32[512]{0:T(512)S(1)}, f32[512]{0:T(512)}, u32[]{:S(2)}) copy-start(f32[512]{0:T(512)} %param.24) | copy-start | bytes 6148
  206.4 14.3 %all-to-all-start.3 = ((bf16[8,2,8,640]{3,2,1,0:T(8,128)(2,1)}), bf16[8,2,8,640]{3,2,1,0:T(8,128)(2,1)S(1)}, u32[]{:S(2)}, u32[]{:S(2)}) async-start(bf16[8,2,8,640]{3,2,1,0:T(8,128)(2,1)} %copy_bitcast_fusion), calls=%async_computation.4 | async-start | bytes 327680 | tf_op jit(solution)/shard_map/all_to_all | solution.py:119
  211.2 27.3 %copy-start.7 = (bf16[16,448]{1,0:T(8,128)(2,1)}, bf16[16,448]{1,0:T(8,128)(2,1)S(1)}, u32[]{:S(2)}) copy-start(bf16[16,448]{1,0:T(8,128)(2,1)S(1)} %get-tuple-element.17) | copy-start | bytes 43012
  221.5 15.3 %all-to-all-start.4 = ((f32[8,16,640]{2,1,0:T(8,128)}), f32[8,16,640]{2,1,0:T(8,128)S(1)}, u32[]{:S(2)}, u32[]{:S(2)}) async-start(f32[8,16,640]{2,1,0:T(8,128)} %broadcast_in_dim.67), calls=%async_computation.5 | async-start | bytes 655360 | tf_op jit(solution)/shard_map/all_to_all | solution.py:189
Sparse Core Ops, SparseCore 0:
  77.5 38.3 all-gather.2
  122.6 47.9 reduce-scatter.1

commit v2 on v1

v2 whole, which is shorter than its diff:
```python
import jax
import jax.numpy as jnp
from jax import lax
from jax.experimental import pallas as pl
from jax.experimental.pallas import tpu as pltpu
from jax.sharding import PartitionSpec as P


D = 3584
LAT = 512
CAP = 8
EXTRA = 8

epsilon = 1e-06
route_scale = 2.5
score_scale = 192.0 ** (-0.5)
f32 = jnp.float32
bf16 = jnp.bfloat16
VMEM = pl.BlockSpec(memory_space=pltpu.VMEM)
SMEM = pl.BlockSpec(memory_space=pltpu.SMEM)
PARAMS = pltpu.CompilerParams(vmem_limit_bytes=40 * 1024 * 1024)


def shape(dims, dtype):
    return jax.ShapeDtypeStruct(dims, dtype)


def exchange(x, axis):
    return lax.all_to_all(x, axis, split_axis=0, concat_axis=0, tiled=True)


def route_kernel(ids_ref, slots_ref, aff_ref, hid_ref, send_ref, comb_ref):
    experts = send_ref.shape[0]
    tokens, top = ids_ref.shape
    rows = experts * CAP
    slots = slots_ref[...]
    kept = slots < CAP
    affinity = aff_ref[...]
    weight = route_scale * affinity / jnp.sum(affinity, -1, keepdims=True)
    target = jnp.where(kept, ids_ref[...] * CAP + slots, -1)
    lane = lax.broadcasted_iota(jnp.int32, (tokens, rows), 1)
    pick = jnp.zeros((tokens, rows), f32)
    comb = jnp.zeros((tokens, rows), f32)
    for k in range(top):
        match = target[:, k : k + 1] == lane
        pick = jnp.where(match, 1.0, pick)
        comb = jnp.where(match, weight[:, k : k + 1], comb)
    comb_ref[...] = comb
    sent = lax.dot_general(
        pick.astype(bf16), hid_ref[...], (((0,), (0,)), ((), ())), preferred_element_type=f32
    )
    send_ref[...] = sent.reshape(send_ref.shape).astype(bf16)


def route(expert_ids, slots, affinity, hidden, experts):
    tokens, width = hidden.shape
    return pl.pallas_call(
        route_kernel,
        out_shape=(shape((experts, CAP, width), bf16), shape((tokens, experts * CAP), f32)),
        in_specs=[VMEM] * 4,
        out_specs=(VMEM, VMEM),
        compiler_params=PARAMS,
        name="route",
    )(expert_ids, slots, affinity, hidden)


def units_kernel(x_ref, wg_ref, wu_ref, o_ref, g_ref, u_ref):
    peers, padded, cols = x_ref.shape
    rows = padded - EXTRA
    square = jnp.zeros((rows, 1), f32)
    for j in range(peers):
        x = x_ref[j, :rows, :].astype(f32)
        square = square + jnp.sum(x * x, -1, keepdims=True)
    scale = lax.rsqrt(square / D + epsilon)
    for j in range(peers):
        x = x_ref[j, :rows, :].astype(f32)
        gain = jnp.sum(x_ref[j, rows:, :].astype(f32), 0, keepdims=True)
        normed = (x * scale * gain).astype(bf16)
        part = pl.ds(j * cols, cols)
        gate = jnp.dot(normed, wg_ref[part, :], preferred_element_type=f32)
        up = jnp.dot(normed, wu_ref[part, :], preferred_element_type=f32)
        if j == 0:
            g_ref[...] = gate
            u_ref[...] = up
        else:
            g_ref[...] += gate
            u_ref[...] += up
    gate = g_ref[...]
    units = (gate / (1.0 + jnp.exp(-gate)) * u_ref[...]).astype(bf16)
    for j in range(peers):
        o_ref[j] = units


def expert_units(x, w_gate, w_up):
    peers, padded, _ = x.shape
    rows, hid = padded - EXTRA, w_gate.shape[1]
    return pl.pallas_call(
        units_kernel,
        out_shape=shape((peers, rows, hid), bf16),
        in_specs=[VMEM] * 3,
        out_specs=VMEM,
        scratch_shapes=[pltpu.VMEM((rows, hid), f32), pltpu.VMEM((rows, hid), f32)],
        compiler_params=PARAMS,
        name="units",
    )(x, w_gate, w_up)


def pack_kernel(me_ref, wd_ref, cache_ref, q_ref, *refs):
    outs, tiles_ref = refs[:-1], refs[-1]
    peers = len(outs)
    hid, width = tiles_ref.shape[1:]
    span, heads, keys = cache_ref.shape[1], q_ref.shape[1], cache_ref.shape[2]
    own = cache_ref.shape[0] // peers
    for j in range(peers):
        tiles_ref[j] = wd_ref[:, j * width : (j + 1) * width]
    for k in range(peers):
        to = lax.rem(me_ref[0] + k, peers)
        outs[k][:hid, :width] = tiles_ref[to]
        outs[k][:hid, width:] = jnp.zeros((hid, keys - width), bf16)
        for i in range(own):
            row = hid + i * (span + heads)
            outs[k][row : row + span, :] = cache_ref[to * own + i]
            outs[k][row + span : row + span + heads, :] = q_ref[to * own + i]


def pack(me, w_down, cache, queries, peers):
    hid, width = w_down.shape[0], w_down.shape[1] // peers
    seqs, span, keys = cache.shape
    rows = hid + seqs // peers * (span + queries.shape[1])
    return pl.pallas_call(
        pack_kernel,
        out_shape=tuple(shape((rows, keys), bf16) for _ in range(peers)),
        in_specs=[SMEM] + [VMEM] * 3,
        out_specs=tuple(VMEM for _ in range(peers)),
        scratch_shapes=[pltpu.VMEM((peers, hid, width), bf16)],
        compiler_params=PARAMS,
        name="pack",
    )(me, w_down, cache, queries)


def spread_kernel(x_ref, gain_ref, o_ref):
    rows = o_ref.shape[1] - EXTRA
    gain = gain_ref[...]
    first = gain.astype(bf16).astype(f32)
    second = (gain - first).astype(bf16).astype(f32)
    third = gain - first - second
    row = lax.broadcasted_iota(jnp.int32, (EXTRA, gain.shape[1]), 0)
    tail = jnp.where(
        row == 0, first, jnp.where(row == 1, second, jnp.where(row == 2, third, 0.0))
    ).astype(bf16)
    x = x_ref[...].reshape(rows, gain.shape[1])
    for j in range(o_ref.shape[0]):
        o_ref[j, :rows, :] = x
        o_ref[j, rows:, :] = tail


def spread_rows(arrived, gain, peers):
    experts, cap, width = arrived.shape
    return pl.pallas_call(
        spread_kernel,
        out_shape=shape((peers, experts * cap + EXTRA, width), bf16),
        in_specs=[VMEM] * 2,
        out_specs=VMEM,
        compiler_params=PARAMS,
        name="rows",
    )(arrived, gain)


def down_kernel(me_ref, u_ref, *refs):
    blocks, o_ref = refs[:-1], refs[-1]
    peers, _, hid = u_ref.shape
    width = o_ref.shape[-1]
    acc = jnp.zeros((u_ref.shape[1], width), f32)
    for k in range(peers):
        group = lax.rem(me_ref[0] + (peers - k), peers)
        acc = acc + jnp.dot(
            u_ref[group], blocks[k][:hid, :width], preferred_element_type=f32
        )
    o_ref[...] = acc.reshape(o_ref.shape).astype(bf16)


def expert_down(me, units, blocks, experts, width):
    return pl.pallas_call(
        down_kernel,
        out_shape=shape((experts, CAP, width), bf16),
        in_specs=[SMEM] + [VMEM] * (1 + len(blocks)),
        out_specs=VMEM,
        compiler_params=PARAMS,
        name="down",
    )(me, units, *blocks)


def attend_kernel(me_ref, len_ref, *refs):
    peers = (len(refs) - 2) // 2
    blocks, outs, c_ref, q_ref = refs[:peers], refs[peers:-2], refs[-2], refs[-1]
    own, heads, _ = outs[0].shape
    span = c_ref.shape[1] // peers
    first = blocks[0].shape[0] - own * (span + heads)
    me = me_ref[0]
    for i in range(own):
        for k in range(peers):
            row = first + i * (span + heads)
            c_ref[i, k * span : (k + 1) * span, :] = blocks[k][row : row + span, :]
            q_ref[i, k * heads : (k + 1) * heads, :] = blocks[k][
                row + span : row + span + heads, :
            ]
    lane = lax.broadcasted_iota(jnp.int32, (peers * heads, peers * span), 1)
    block = lax.rem(me + (peers - lane // span), peers)
    position = block * span + lane % span
    for i in range(own):
        live = position < len_ref[me * own + i]
        keys = c_ref[i]
        scores = (
            lax.dot_general(
                q_ref[i], keys, (((1,), (1,)), ((), ())), preferred_element_type=f32
            )
            * score_scale
        )
        scores = jnp.where(live, scores, -1e30)
        peak = jnp.max(scores, -1, keepdims=True)
        prob = jnp.where(live, jnp.exp(scores - peak), 0.0)
        mass = jnp.sum(prob, -1, keepdims=True)
        out = jnp.dot(prob.astype(bf16), keys[:, :LAT], preferred_element_type=f32)
        out = (out / mass).astype(bf16)
        total = peak + jnp.log(mass)
        high = total.astype(bf16).astype(f32)
        middle = (total - high).astype(bf16).astype(f32)
        low = total - high - middle
        tail_lane = lax.broadcasted_iota(jnp.int32, (peers * heads, 128), 1)
        tail = jnp.where(
            tail_lane == 0,
            high,
            jnp.where(tail_lane == 1, middle, jnp.where(tail_lane == 2, low, 0.0)),
        ).astype(bf16)
        for k in range(peers):
            outs[k][i, :, :LAT] = out[k * heads : (k + 1) * heads]
            outs[k][i, :, LAT:] = tail[k * heads : (k + 1) * heads]


def attend(me, lengths, blocks, own, span, heads):
    peers, keys = len(blocks), blocks[0].shape[1]
    return pl.pallas_call(
        attend_kernel,
        out_shape=tuple(shape((own, heads, LAT + 128), bf16) for _ in range(peers)),
        in_specs=[SMEM, SMEM] + [VMEM] * peers,
        out_specs=tuple(VMEM for _ in range(peers)),
        scratch_shapes=[
            pltpu.VMEM((own, peers * span, keys), bf16),
            pltpu.VMEM((own, peers * heads, keys), bf16),
        ],
        compiler_params=PARAMS,
        name="attend",
    )(me, lengths, *blocks)


def close_kernel(ret_ref, comb_ref, hid_ref, gain_ref, wdkv_ref, next_ref, small_ref):
    rows = comb_ref.shape[1]
    keys = wdkv_ref.shape[1]
    returned = ret_ref[...].reshape(rows, ret_ref.shape[-1])
    comb = comb_ref[...]
    high = comb.astype(bf16)
    low = (comb - high.astype(f32)).astype(bf16)
    moe = jnp.dot(high, returned, preferred_element_type=f32) + jnp.dot(
        low, returned, preferred_element_type=f32
    )
    result = (hid_ref[...].astype(f32) + moe).astype(bf16)
    next_ref[...] = result
    wide = result.astype(f32)
    square = jnp.sum(wide * wide, -1, keepdims=True)
    first = square.astype(bf16).astype(f32)
    second = (square - first).astype(bf16).astype(f32)
    third = square - first - second
    lane = lax.broadcasted_iota(jnp.int32, (wide.shape[0], small_ref.shape[2] - keys), 1)
    tail = jnp.where(
        lane == 0, first, jnp.where(lane == 1, second, jnp.where(lane == 2, third, 0.0))
    ).astype(bf16)
    down = jnp.dot(
        (wide * gain_ref[...]).astype(bf16), wdkv_ref[...], preferred_element_type=f32
    ).astype(bf16)
    for j in range(small_ref.shape[0]):
        small_ref[j, :, :keys] = down
        small_ref[j, :, keys:] = tail


def close(returned, combine, hidden, gain, w_dkv, peers):
    tokens, width = hidden.shape
    return pl.pallas_call(
        close_kernel,
        out_shape=(
            shape((tokens, width), bf16),
            shape((peers, tokens, w_dkv.shape[1] + 64), bf16),
        ),
        in_specs=[VMEM] * 5,
        out_specs=(VMEM, VMEM),
        compiler_params=PARAMS,
        name="close",
    )(returned, combine, hidden, gain, w_dkv)


def merge_kernel(me_ref, all_ref, gain_ref, cos_ref, sin_ref, q_ref, *refs):
    backs, o_ref, back_ref = refs[:-2], refs[-2], refs[-1]
    peers = len(backs)
    own_seqs = backs[0].shape[0]
    for k in range(peers):
        source = lax.rem(me_ref[0] + k, peers)
        back_ref[pl.ds(source * own_seqs, own_seqs)] = backs[k][...]
    keys = q_ref.shape[-1]
    total = all_ref[0].astype(f32)
    for j in range(1, all_ref.shape[0]):
        total = total + all_ref[j].astype(f32)
    square = jnp.sum(total[:, keys:], -1, keepdims=True)
    down = total[:, :keys] * lax.rsqrt(square / D + epsilon)
    latent = down[:, :LAT]
    latent = (
        latent
        * lax.rsqrt(jnp.mean(latent * latent, -1, keepdims=True) + epsilon)
        * gain_ref[...]
    )
    rope = down[:, LAT:]
    half = rope.shape[-1] // 2
    turned = jnp.concatenate([rope[:, half:], rope[:, :half]], 1)
    rope = rope * cos_ref[...] + turned * sin_ref[...]
    latent = latent.astype(bf16).astype(f32)[:, None, :]
    rope = rope.astype(bf16).astype(f32)[:, None, :]
    own = (
        jnp.sum(q_ref[:, :, :LAT].astype(f32) * latent, -1, keepdims=True)
        + jnp.sum(q_ref[:, :, LAT:].astype(f32) * rope, -1, keepdims=True)
    ) * score_scale
    cached = jnp.sum(back_ref[:, :, LAT:].astype(f32), -1, keepdims=True)
    peak = jnp.maximum(own, cached)
    own_prob = jnp.exp(own - peak)
    cached_prob = jnp.exp(cached - peak)
    total_prob = own_prob + cached_prob
    o_ref[...] = (
        back_ref[:, :, :LAT].astype(f32) * (cached_prob / total_prob)
        + latent * (own_prob / total_prob)
    ).astype(bf16)


def merge(me, everything, gain, cos, sin, queries, backs):
    seqs, heads, _ = queries.shape
    return pl.pallas_call(
        merge_kernel,
        out_shape=shape((seqs, heads, LAT), bf16),
        in_specs=[SMEM] + [VMEM] * (5 + len(backs)),
        out_specs=VMEM,
        scratch_shapes=[pltpu.VMEM((seqs, heads, LAT + 128), bf16)],
        compiler_params=PARAMS,
        name="merge",
    )(me, everything, gain, cos, sin, queries, *backs)


def mark_kernel(x_ref, o_ref):
    o_ref[...] = x_ref[...]


def mark(x):
    return pl.pallas_call(
        mark_kernel, out_shape=shape(x.shape, x.dtype), in_specs=[VMEM], out_specs=VMEM
    )(x)


def rope_tables(lengths, half):
    inv_freq = 10000.0 ** (-jnp.arange(half, dtype=f32) / half)
    angles = lengths.astype(f32)[:, None] * inv_freq[None, :]
    cos, sin = jnp.cos(angles), jnp.sin(angles)
    return jnp.concatenate([cos, cos], 1), jnp.concatenate([-sin, sin], 1)


def local(
    hidden,
    moe_gain,
    expert_ids,
    slots,
    affinity,
    w_gate,
    w_up,
    w_down,
    attn_gain,
    w_dkv,
    kv_gain,
    queries,
    cache,
    lengths,
):
    seqs, width = hidden.shape
    peers = lax.axis_size("tp")
    experts = lax.axis_size("ep") * lax.axis_size("mb")
    me = lax.axis_index("tp").astype(jnp.int32).reshape(1)

    def moved(x, k):
        return lax.ppermute(x, "tp", [(i, (i + k) % peers) for i in range(peers)])

    send_rows, combine = route(expert_ids, slots, affinity, hidden, experts)
    arrived = exchange(send_rows, ("ep", "mb"))
    blocks = list(pack(me, w_down[0], cache, queries, peers))
    for k in range(1, peers):
        blocks[k] = moved(blocks[k], k)
    rows = spread_rows(arrived, mark(moe_gain[None]), peers)
    portion = exchange(rows, "tp")
    backs = list(attend(me, lengths, blocks, seqs // peers, cache.shape[1], queries.shape[1]))
    for k in range(1, peers):
        backs[k] = moved(backs[k], peers - k)
    units = expert_units(portion, w_gate[0], w_up[0])
    all_units = exchange(units, "tp")
    output = expert_down(me, all_units, blocks, experts, width)
    returned = exchange(output, ("ep", "mb"))
    attn_gain = mark(attn_gain[None])
    next_hidden, small = close(returned, combine, hidden, attn_gain, w_dkv, peers)
    everything = exchange(small, "tp")
    cos, sin = rope_tables(lengths, (queries.shape[-1] - LAT) // 2)
    latent_out = merge(me, everything, kv_gain[None], cos, sin, queries, backs)
    return (next_hidden, latent_out)


def solution(mesh):
    return jax.shard_map(
        local,
        mesh=mesh,
        in_specs=(
            P(("grp", "ep", "mb"), "tp"),
            P("tp"),
            P(("grp", "ep", "mb"), None),
            P(("grp", "ep", "mb"), None),
            P(("grp", "ep", "mb"), None),
            P(("ep", "mb"), None, "tp"),
            P(("ep", "mb"), None, "tp"),
            P(("ep", "mb"), "tp", None),
            P("tp"),
            P("tp", None),
            P(),
            P(("grp", "ep", "mb"), "tp", None),
            P(("grp", "ep", "mb"), "tp", None),
            P(("grp", "ep", "mb")),
        ),
        out_specs=(P(("grp", "ep", "mb"), "tp"), P(("grp", "ep", "mb"), "tp", None)),
        check_vma=False,
    )
```

time: 246 us -> 257 us (1.045)
  waiting for transfers between devices: 142 us -> 61.5 us
  blocking collectives: 0 us -> 59.9 us
  starting transfers between devices: 70.9 us -> 118 us
  between operations: 14.3 us -> 0.9 us
  Pallas kernels: 3.69 us -> 11.4 us
  other arithmetic: 6.01 us -> 0.21 us
    ppermute x0 -> x14, starting transfers between devices: none -> 60.6 us  [moved(): return lax.ppermute(x, 'tp', [(i, (i + k) % peers) for i in range(peers)])]
    all_to_all x0 -> x1, blocking collectives: none -> 59.9 us  [exchange(): return lax.all_to_all(x, axis, split_axis=0, concat_axis=0, tiled=True)]
    all_to_all x5 -> x4, waiting for transfers between devices: 74.9 us -> 33.6 us  [exchange(): return lax.all_to_all(x, axis, split_axis=0, concat_axis=0, tiled=True)]
    all_gather x1 -> x0, waiting for transfers between devices: 38.5 us -> none  [local(): portion = lax.all_gather(jnp.concatenate([arrived, gain_rows], 0), 'tp')]
    reduce_scatter x1 -> x0, waiting for transfers between devices: 29 us -> none  [local(): summed = lax.psum_scatter(partial_out, 'tp')]
    ppermute x0 -> x14, waiting for transfers between devices: none -> 27.8 us  [moved(): return lax.ppermute(x, 'tp', [(i, (i + k) % peers) for i in range(peers)])]
    all_to_all x5 -> x4, starting transfers between devices: 70.8 us -> 57 us  [exchange(): return lax.all_to_all(x, axis, split_axis=0, concat_axis=0, tiled=True)]
    pallas_call x1 -> x10, Pallas kernels: 3.69 us -> 11.4 us  [the longest x1 2.55 us: expert_units(): pl.pallas_call(units_kernel, out_shape=shape((peers, rows, hid), bf16), i...]
  transfers between devices with their start and end apart: 7 -> 18, of which waited for: 7 -> 8; matrix products, arithmetic and copies ran while one was open for 2% -> 0% of each run, Pallas kernels for 0% -> 2%
where the time goes in v2:
time: 257 us; the launch traced here: 256 us
  starting transfers between devices  118 us (46%)
  waiting for transfers between devices  61.5 us (24%)
  blocking collectives  59.9 us (23%)
  Pallas kernels  11.4 us (4%)
  local copies, waits for them, and re-layouts  4.4 us (2%)
    ppermute x14, starting transfers between devices, moved(): return lax.ppermute(x, 'tp', [(i, (i + k) % peers) for i in range(peers)])  60.6 us
    all_to_all x1, blocking collectives, exchange(): return lax.all_to_all(x, axis, split_axis=0, concat_axis=0, tiled=True)  59.9 us
    all_to_all x4, starting transfers between devices, exchange(): return lax.all_to_all(x, axis, split_axis=0, concat_axis=0, tiled=True)  57 us
    all_to_all x4, waiting for transfers between devices, exchange(): return lax.all_to_all(x, axis, split_axis=0, concat_axis=0, tiled=True)  33.6 us
    ppermute x14, waiting for transfers between devices, moved(): return lax.ppermute(x, 'tp', [(i, (i + k) % peers) for i in range(peers)])  27.8 us
  transfers between devices with their start and end apart: 18, of which 8 were waited for; matrix products, arithmetic and copies ran while one was open for 0% of the time, Pallas kernels for 2%

profile of v2, /device:TPU:80, one launch (start us, length us, event | category | flops | bytes accessed | tf_op | source)
XLA Modules:
  0.0 255.8 jit_solution(12221281623031062829)
XLA Ops:
  0.6 0.8 copy.16.ids_ref
  1.4 0.8 copy.17.slots_ref
  2.1 0.8 copy.18.aff_ref
  2.9 0.7 copy-done.6
  3.6 1.0 route.1
  4.7 44.4 %all-to-all-start = ((bf16[32,8,448]{2,1,0:T(8,128)(2,1)}), bf16[32,8,448]{2,1,0:T(8,128)(2,1)S(1)}, u32[]{:S(2)}, u32[]{:S(2)}) async-start(bf16[32,8,448]{2,1,0:T(8,128)(2,1)} %get-tuple-element.22), calls=%async_computation | async-start | bytes 524288 | tf_op jit(solution)/shard_map/all_to_all | solution.py:29
  49.1 1.3 shard_map.149.gain_ref
  50.4 20.7 %all-to-all-done.x_ref = bf16[32,8,448]{2,1,0:T(8,128)(2,1)S(1)} async-done(((bf16[32,8,448]{2,1,0:T(8,128)(2,1)}), bf16[32,8,448]{2,1,0:T(8,128)(2,1)S(1)}, u32[]{:S(2)}, u32[]{:S(2)}) %all-to-all-start) | async-done | bytes 229408 | tf_op jit(solution)/shard_map/all_to_all | solution.py:29
  71.1 0.7 copy-done.9
  71.8 0.1 rows.1
  71.9 0.0 copy-start.1
  72.0 0.0 copy-start.2
  72.0 59.9 %all_to_all.25.x_ref = bf16[8,264,448]{2,1,0:T(8,128)(2,1)S(1)} all-to-all(bf16[8,264,448]{2,1,0:T(8,128)(2,1)S(1)} %rows.1), channel_id=1, replica_groups=mesh['grp'=2,'ep'=16,'tp'=8,'mb'=2] {'tp'}, dimensions={0} | all-to-all | bytes 3784704 | tf_op jit(solution)/shard_map/all_to_all | solution.py:29
  131.9 0.0 copy-start.5
  131.9 2.5 units.1
  134.5 3.7 %all-to-all-start.2 = ((bf16[8,256,128]{2,1,0:T(8,128)(2,1)}), bf16[8,256,128]{2,1,0:T(8,128)(2,1)S(1)}, u32[]{:S(2)}, u32[]{:S(2)}) async-start(bf16[8,256,128]{2,1,0:T(8,128)(2,1)} %units.1), calls=%async_computation.2 | async-start | bytes 1048576 | tf_op jit(solution)/shard_map/all_to_all | solution.py:29
  138.2 0.3 pack.1
  138.6 3.7 %collective-permute-start = (bf16[176,576]{1,0:T(8,128)(2,1)S(1)}, bf16[176,576]{1,0:T(8,128)(2,1)S(1)}, u32[]{:S(2)}, u32[]{:S(2)}) collective-permute-start(bf16[176,576]{1,0:T(8,128)(2,1)S(1)} %get-tuple-element.24), channel_id=1, source_target_pairs={{0,2},{2,4},{4,6},{6,8},{8,10},{10,12},{12,14},{14,0},{1,3},{3,5},... | collective-permute-start | bytes 608264 | tf_op jit(solution)/shard_map/ppermute | solution.py:392
  142.2 4.3 %collective-permute-start.1 = (bf16[176,576]{1,0:T(8,128)(2,1)S(1)}, bf16[176,576]{1,0:T(8,128)(2,1)S(1)}, u32[]{:S(2)}, u32[]{:S(2)}) collective-permute-start(bf16[176,576]{1,0:T(8,128)(2,1)S(1)} %get-tuple-element.25), channel_id=1, source_target_pairs={{0,4},{2,6},{4,8},{6,10},{8,12},{10,14},{12,0},{14,2},{1,5},{3,7},... | collective-permute-start | bytes 608264 | tf_op jit(solution)/shard_map/ppermute | solution.py:392
  146.6 4.7 %collective-permute-start.2 = (bf16[176,576]{1,0:T(8,128)(2,1)S(1)}, bf16[176,576]{1,0:T(8,128)(2,1)S(1)}, u32[]{:S(2)}, u32[]{:S(2)}) collective-permute-start(bf16[176,576]{1,0:T(8,128)(2,1)S(1)} %get-tuple-element.26), channel_id=1, source_target_pairs={{0,6},{2,8},{4,10},{6,12},{8,14},{10,0},{12,2},{14,4},{1,7},{3,9},... | collective-permute-start | bytes 608264 | tf_op jit(solution)/shard_map/ppermute | solution.py:392
  151.2 4.2 %collective-permute-start.3 = (bf16[176,576]{1,0:T(8,128)(2,1)S(1)}, bf16[176,576]{1,0:T(8,128)(2,1)S(1)}, u32[]{:S(2)}, u32[]{:S(2)}) collective-permute-start(bf16[176,576]{1,0:T(8,128)(2,1)S(1)} %get-tuple-element.27), channel_id=1, source_target_pairs={{0,8},{2,10},{4,12},{6,14},{8,0},{10,2},{12,4},{14,6},{1,9},{3,11}... | collective-permute-start | bytes 608264 | tf_op jit(solution)/shard_map/ppermute | solution.py:392
  155.5 4.7 %collective-permute-start.4 = (bf16[176,576]{1,0:T(8,128)(2,1)S(1)}, bf16[176,576]{1,0:T(8,128)(2,1)S(1)}, u32[]{:S(2)}, u32[]{:S(2)}) collective-permute-start(bf16[176,576]{1,0:T(8,128)(2,1)S(1)} %get-tuple-element.28), channel_id=1, source_target_pairs={{0,10},{2,12},{4,14},{6,0},{8,2},{10,4},{12,6},{14,8},{1,11},{3,13... | collective-permute-start | bytes 608264 | tf_op jit(solution)/shard_map/ppermute | solution.py:392
  160.2 5.5 %collective-permute-start.5 = (bf16[176,576]{1,0:T(8,128)(2,1)S(1)}, bf16[176,576]{1,0:T(8,128)(2,1)S(1)}, u32[]{:S(2)}, u32[]{:S(2)}) collective-permute-start(bf16[176,576]{1,0:T(8,128)(2,1)S(1)} %get-tuple-element.29), channel_id=1, source_target_pairs={{0,12},{2,14},{4,0},{6,2},{8,4},{10,6},{12,8},{14,10},{1,13},{3,15... | collective-permute-start | bytes 608264 | tf_op jit(solution)/shard_map/ppermute | solution.py:392
  165.7 4.2 %collective-permute-done.1.refs_2_ = bf16[176,576]{1,0:T(8,128)(2,1)S(1)} collective-permute-done((bf16[176,576]{1,0:T(8,128)(2,1)S(1)}, bf16[176,576]{1,0:T(8,128)(2,1)S(1)}, u32[]{:S(2)}, u32[]{:S(2)}) %collective-permute-start.1) | collective-permute-done | bytes 202784 | tf_op jit(solution)/shard_map/ppermute | solution.py:392
  169.9 5.2 %collective-permute-start.6 = (bf16[176,576]{1,0:T(8,128)(2,1)S(1)}, bf16[176,576]{1,0:T(8,128)(2,1)S(1)}, u32[]{:S(2)}, u32[]{:S(2)}) collective-permute-start(bf16[176,576]{1,0:T(8,128)(2,1)S(1)} %get-tuple-element.30), channel_id=1, source_target_pairs={{0,14},{2,0},{4,2},{6,4},{8,6},{10,8},{12,10},{14,12},{1,15},{3,1}... | collective-permute-start | bytes 608264 | tf_op jit(solution)/shard_map/ppermute | solution.py:392
  175.1 6.3 %collective-permute-done.2.refs_3_ = bf16[176,576]{1,0:T(8,128)(2,1)S(1)} collective-permute-done((bf16[176,576]{1,0:T(8,128)(2,1)S(1)}, bf16[176,576]{1,0:T(8,128)(2,1)S(1)}, u32[]{:S(2)}, u32[]{:S(2)}) %collective-permute-start.2) | collective-permute-done | bytes 202784 | tf_op jit(solution)/shard_map/ppermute | solution.py:392
  181.4 8.8 %collective-permute-done.3.refs_4_ = bf16[176,576]{1,0:T(8,128)(2,1)S(1)} collective-permute-done((bf16[176,576]{1,0:T(8,128)(2,1)S(1)}, bf16[176,576]{1,0:T(8,128)(2,1)S(1)}, u32[]{:S(2)}, u32[]{:S(2)}) %collective-permute-start.3) | collective-permute-done | bytes 202784 | tf_op jit(solution)/shard_map/ppermute | solution.py:392
  190.2 4.2 %collective-permute-done.6.refs_7_ = bf16[176,576]{1,0:T(8,128)(2,1)S(1)} collective-permute-done((bf16[176,576]{1,0:T(8,128)(2,1)S(1)}, bf16[176,576]{1,0:T(8,128)(2,1)S(1)}, u32[]{:S(2)}, u32[]{:S(2)}) %collective-permute-start.6) | collective-permute-done | bytes 202784 | tf_op jit(solution)/shard_map/ppermute | solution.py:392
  194.4 1.4 down.1
  195.8 4.9 %all-to-all-start.3 = ((bf16[32,8,448]{2,1,0:T(8,128)(2,1)}), bf16[32,8,448]{2,1,0:T(8,128)(2,1)S(1)}, u32[]{:S(2)}, u32[]{:S(2)}) async-start(bf16[32,8,448]{2,1,0:T(8,128)(2,1)} %down.1), calls=%async_computation.3 | async-start | bytes 524288 | tf_op jit(solution)/shard_map/all_to_all | solution.py:29
  200.7 1.3 shard_map.150.gain_ref
  202.0 1.2 attend.1
  203.3 4.6 %collective-permute-start.7 = (bf16[2,8,640]{2,1,0:T(8,128)(2,1)S(1)}, bf16[2,8,640]{2,1,0:T(8,128)(2,1)S(1)}, u32[]{:S(2)}, u32[]{:S(2)}) collective-permute-start(bf16[2,8,640]{2,1,0:T(8,128)(2,1)S(1)} %get-tuple-element.35), channel_id=1, source_target_pairs={{0,14},{2,0},{4,2},{6,4},{8,6},{10,8},{12,10},{14,12},{1,15},{3,1}... | collective-permute-start | bytes 61448 | tf_op jit(solution)/shard_map/ppermute | solution.py:392
  207.8 2.0 collective-permute-start.8
  209.8 12.9 %all-to-all-done.3.ret_ref = bf16[32,8,448]{2,1,0:T(8,128)(2,1)S(1)} async-done(((bf16[32,8,448]{2,1,0:T(8,128)(2,1)}), bf16[32,8,448]{2,1,0:T(8,128)(2,1)S(1)}, u32[]{:S(2)}, u32[]{:S(2)}) %all-to-all-start.3) | async-done | bytes 229408 | tf_op jit(solution)/shard_map/all_to_all | solution.py:29
  222.7 0.7 copy-done.8
  223.4 1.0 close.1
  224.4 3.9 %all-to-all-start.4 = ((bf16[8,16,640]{2,1,0:T(8,128)(2,1)}), bf16[8,16,640]{2,1,0:T(8,128)(2,1)S(1)}, u32[]{:S(2)}, u32[]{:S(2)}) async-start(bf16[8,16,640]{2,1,0:T(8,128)(2,1)} %get-tuple-element.33), calls=%async_computation.4 | async-start | bytes 327680 | tf_op jit(solution)/shard_map/all_to_all | solution.py:29
  228.3 0.1 fusion
  228.4 7.0 %collective-permute-start.9 = (bf16[2,8,640]{2,1,0:T(8,128)(2,1)S(1)}, bf16[2,8,640]{2,1,0:T(8,128)(2,1)S(1)}, u32[]{:S(2)}, u32[]{:S(2)}) collective-permute-start(bf16[2,8,640]{2,1,0:T(8,128)(2,1)S(1)} %get-tuple-element.37), channel_id=1, source_target_pairs={{0,10},{2,12},{4,14},{6,0},{8,2},{10,4},{12,6},{14,8},{1,11},{3,13... | collective-permute-start | bytes 61448 | tf_op jit(solution)/shard_map/ppermute | solution.py:392
  235.4 3.4 %collective-permute-start.10 = (bf16[2,8,640]{2,1,0:T(8,128)(2,1)S(1)}, bf16[2,8,640]{2,1,0:T(8,128)(2,1)S(1)}, u32[]{:S(2)}, u32[]{:S(2)}) collective-permute-start(bf16[2,8,640]{2,1,0:T(8,128)(2,1)S(1)} %get-tuple-element.38), channel_id=1, source_target_pairs={{0,8},{2,10},{4,12},{6,14},{8,0},{10,2},{12,4},{14,6},{1,9},{3,11}... | collective-permute-start | bytes 61448 | tf_op jit(solution)/shard_map/ppermute | solution.py:392
  238.8 5.2 %collective-permute-start.11 = (bf16[2,8,640]{2,1,0:T(8,128)(2,1)S(1)}, bf16[2,8,640]{2,1,0:T(8,128)(2,1)S(1)}, u32[]{:S(2)}, u32[]{:S(2)}) collective-permute-start(bf16[2,8,640]{2,1,0:T(8,128)(2,1)S(1)} %get-tuple-element.39), channel_id=1, source_target_pairs={{0,6},{2,8},{4,10},{6,12},{8,14},{10,0},{12,2},{14,4},{1,7},{3,9},... | collective-permute-start | bytes 61448 | tf_op jit(solution)/shard_map/ppermute | solution.py:392
  244.0 3.7 %collective-permute-start.12 = (bf16[2,8,640]{2,1,0:T(8,128)(2,1)S(1)}, bf16[2,8,640]{2,1,0:T(8,128)(2,1)S(1)}, u32[]{:S(2)}, u32[]{:S(2)}) collective-permute-start(bf16[2,8,640]{2,1,0:T(8,128)(2,1)S(1)} %get-tuple-element.40), channel_id=1, source_target_pairs={{0,4},{2,6},{4,8},{6,10},{8,12},{10,14},{12,0},{14,2},{1,5},{3,7},... | collective-permute-start | bytes 61448 | tf_op jit(solution)/shard_map/ppermute | solution.py:392
  247.8 2.5 collective-permute-start.13
  250.3 0.1 pad_maximum_fusion
  250.4 1.9 collective-permute-done.12.refs_6_
  252.3 2.4 collective-permute-done.13.refs_7_
  254.7 1.1 merge.1
  (30 shorter events, 0.1 us)
Async XLA Ops:
  2.9 0.7 copy-start.6
  4.7 66.4 %all-to-all-start = ((bf16[32,8,448]{2,1,0:T(8,128)(2,1)}), bf16[32,8,448]{2,1,0:T(8,128)(2,1)S(1)}, u32[]{:S(2)}, u32[]{:S(2)}) async-start(bf16[32,8,448]{2,1,0:T(8,128)(2,1)} %get-tuple-element.22), calls=%async_computation | async-start | bytes 524288 | tf_op jit(solution)/shard_map/all_to_all | solution.py:29
  71.1 0.7 copy-start.9
  71.9 60.0 %copy-start.1 = (bf16[1,3584,128]{2,1,0:T(8,128)(2,1)S(1)}, bf16[1,3584,128]{2,1,0:T(8,128)(2,1)}, u32[]{:S(2)}) copy-start(bf16[1,3584,128]{2,1,0:T(8,128)(2,1)} %param.19) | copy-start | bytes 2752516
  72.0 60.0 %copy-start.2 = (bf16[1,3584,128]{2,1,0:T(8,128)(2,1)S(1)}, bf16[1,3584,128]{2,1,0:T(8,128)(2,1)}, u32[]{:S(2)}) copy-start(bf16[1,3584,128]{2,1,0:T(8,128)(2,1)} %param.20) | copy-start | bytes 2752516
  131.9 6.3 %copy-start = (bf16[1,128,3584]{2,1,0:T(8,128)(2,1)S(1)}, bf16[1,128,3584]{2,1,0:T(8,128)(2,1)}, u32[]{:S(2)}) copy-start(bf16[1,128,3584]{2,1,0:T(8,128)(2,1)} %param.21) | copy-start | bytes 2752516
  131.9 6.3 %copy-start.3 = (bf16[16,8,576]{2,1,0:T(8,128)(2,1)S(1)}, bf16[16,8,576]{2,1,0:T(8,128)(2,1)}, u32[]{:S(2)}) copy-start(bf16[16,8,576]{2,1,0:T(8,128)(2,1)} %q_ref.3) | copy-start | bytes 442372
  131.9 6.3 %copy-start.5 = (bf16[16,16,576]{2,1,0:T(8,128)(2,1)S(1)}, bf16[16,16,576]{2,1,0:T(8,128)(2,1)}, u32[]{:S(2)}) copy-start(bf16[16,16,576]{2,1,0:T(8,128)(2,1)} %cache_ref.1) | copy-start | bytes 884740
  134.5 59.9 %all-to-all-start.2 = ((bf16[8,256,128]{2,1,0:T(8,128)(2,1)}), bf16[8,256,128]{2,1,0:T(8,128)(2,1)S(1)}, u32[]{:S(2)}, u32[]{:S(2)}) async-start(bf16[8,256,128]{2,1,0:T(8,128)(2,1)} %units.1), calls=%async_computation.2 | async-start | bytes 1048576 | tf_op jit(solution)/shard_map/all_to_all | solution.py:29
  138.2 63.8 %copy-start.11 = (s32[16]{0:T(128)S(1)}, s32[16]{0:T(128)}, u32[]{:S(2)}) copy-start(s32[16]{0:T(128)} %len_ref.1) | copy-start | bytes 196
  138.6 21.6 %collective-permute-start = (bf16[176,576]{1,0:T(8,128)(2,1)S(1)}, bf16[176,576]{1,0:T(8,128)(2,1)S(1)}, u32[]{:S(2)}, u32[]{:S(2)}) collective-permute-start(bf16[176,576]{1,0:T(8,128)(2,1)S(1)} %get-tuple-element.24), channel_id=1, source_target_pairs={{0,2},{2,4},{4,6},{6,8},{8,10},{10,12},{12,14},{14,0},{1,3},{3,5},... | collective-permute-start | bytes 608264 | tf_op jit(solution)/shard_map/ppermute | solution.py:392
  142.2 27.6 %collective-permute-start.1 = (bf16[176,576]{1,0:T(8,128)(2,1)S(1)}, bf16[176,576]{1,0:T(8,128)(2,1)S(1)}, u32[]{:S(2)}, u32[]{:S(2)}) collective-permute-start(bf16[176,576]{1,0:T(8,128)(2,1)S(1)} %get-tuple-element.25), channel_id=1, source_target_pairs={{0,4},{2,6},{4,8},{6,10},{8,12},{10,14},{12,0},{14,2},{1,5},{3,7},... | collective-permute-start | bytes 608264 | tf_op jit(solution)/shard_map/ppermute | solution.py:392
  146.6 34.8 %collective-permute-start.2 = (bf16[176,576]{1,0:T(8,128)(2,1)S(1)}, bf16[176,576]{1,0:T(8,128)(2,1)S(1)}, u32[]{:S(2)}, u32[]{:S(2)}) collective-permute-start(bf16[176,576]{1,0:T(8,128)(2,1)S(1)} %get-tuple-element.26), channel_id=1, source_target_pairs={{0,6},{2,8},{4,10},{6,12},{8,14},{10,0},{12,2},{14,4},{1,7},{3,9},... | collective-permute-start | bytes 608264 | tf_op jit(solution)/shard_map/ppermute | solution.py:392
  151.2 39.0 %collective-permute-start.3 = (bf16[176,576]{1,0:T(8,128)(2,1)S(1)}, bf16[176,576]{1,0:T(8,128)(2,1)S(1)}, u32[]{:S(2)}, u32[]{:S(2)}) collective-permute-start(bf16[176,576]{1,0:T(8,128)(2,1)S(1)} %get-tuple-element.27), channel_id=1, source_target_pairs={{0,8},{2,10},{4,12},{6,14},{8,0},{10,2},{12,4},{14,6},{1,9},{3,11}... | collective-permute-start | bytes 608264 | tf_op jit(solution)/shard_map/ppermute | solution.py:392
  155.5 34.8 %collective-permute-start.4 = (bf16[176,576]{1,0:T(8,128)(2,1)S(1)}, bf16[176,576]{1,0:T(8,128)(2,1)S(1)}, u32[]{:S(2)}, u32[]{:S(2)}) collective-permute-start(bf16[176,576]{1,0:T(8,128)(2,1)S(1)} %get-tuple-element.28), channel_id=1, source_target_pairs={{0,10},{2,12},{4,14},{6,0},{8,2},{10,4},{12,6},{14,8},{1,11},{3,13... | collective-permute-start | bytes 608264 | tf_op jit(solution)/shard_map/ppermute | solution.py:392
  160.2 30.0 %collective-permute-start.5 = (bf16[176,576]{1,0:T(8,128)(2,1)S(1)}, bf16[176,576]{1,0:T(8,128)(2,1)S(1)}, u32[]{:S(2)}, u32[]{:S(2)}) collective-permute-start(bf16[176,576]{1,0:T(8,128)(2,1)S(1)} %get-tuple-element.29), channel_id=1, source_target_pairs={{0,12},{2,14},{4,0},{6,2},{8,4},{10,6},{12,8},{14,10},{1,13},{3,15... | collective-permute-start | bytes 608264 | tf_op jit(solution)/shard_map/ppermute | solution.py:392
  169.9 24.6 %collective-permute-start.6 = (bf16[176,576]{1,0:T(8,128)(2,1)S(1)}, bf16[176,576]{1,0:T(8,128)(2,1)S(1)}, u32[]{:S(2)}, u32[]{:S(2)}) collective-permute-start(bf16[176,576]{1,0:T(8,128)(2,1)S(1)} %get-tuple-element.30), channel_id=1, source_target_pairs={{0,14},{2,0},{4,2},{6,4},{8,6},{10,8},{12,10},{14,12},{1,15},{3,1}... | collective-permute-start | bytes 608264 | tf_op jit(solution)/shard_map/ppermute | solution.py:392
  194.4 28.3 %copy-start.4 = (bf16[448,576]{1,0:T(8,128)(2,1)S(1)}, bf16[448,576]{1,0:T(8,128)(2,1)}, u32[]{:S(2)}) copy-start(bf16[448,576]{1,0:T(8,128)(2,1)} %wdkv_ref.1) | copy-start | bytes 1548292
  194.4 28.3 %copy-start.7 = (bf16[16,448]{1,0:T(8,128)(2,1)S(1)}, bf16[16,448]{1,0:T(8,128)(2,1)}, u32[]{:S(2)}) copy-start(bf16[16,448]{1,0:T(8,128)(2,1)} %hid_ref.3) | copy-start | bytes 43012
  195.8 58.9 %copy-start.10 = (f32[512]{0:T(512)S(1)}, f32[512]{0:T(512)}, u32[]{:S(2)}) copy-start(f32[512]{0:T(512)} %param.24) | copy-start | bytes 6148
  195.8 26.9 %all-to-all-start.3 = ((bf16[32,8,448]{2,1,0:T(8,128)(2,1)}), bf16[32,8,448]{2,1,0:T(8,128)(2,1)S(1)}, u32[]{:S(2)}, u32[]{:S(2)}) async-start(bf16[32,8,448]{2,1,0:T(8,128)(2,1)} %down.1), calls=%async_computation.3 | async-start | bytes 524288 | tf_op jit(solution)/shard_map/all_to_all | solution.py:29
  203.3 40.8 %collective-permute-start.7 = (bf16[2,8,640]{2,1,0:T(8,128)(2,1)S(1)}, bf16[2,8,640]{2,1,0:T(8,128)(2,1)S(1)}, u32[]{:S(2)}, u32[]{:S(2)}) collective-permute-start(bf16[2,8,640]{2,1,0:T(8,128)(2,1)S(1)} %get-tuple-element.35), channel_id=1, source_target_pairs={{0,14},{2,0},{4,2},{6,4},{8,6},{10,8},{12,10},{14,12},{1,15},{3,1}... | collective-permute-start | bytes 61448 | tf_op jit(solution)/shard_map/ppermute | solution.py:392
  207.8 39.9 %collective-permute-start.8 = (bf16[2,8,640]{2,1,0:T(8,128)(2,1)S(1)}, bf16[2,8,640]{2,1,0:T(8,128)(2,1)S(1)}, u32[]{:S(2)}, u32[]{:S(2)}) collective-permute-start(bf16[2,8,640]{2,1,0:T(8,128)(2,1)S(1)} %get-tuple-element.36), channel_id=1, source_target_pairs={{0,12},{2,14},{4,0},{6,2},{8,4},{10,6},{12,8},{14,10},{1,13},{3,15... | collective-permute-start | bytes 61448 | tf_op jit(solution)/shard_map/ppermute | solution.py:392
  222.7 0.7 copy-start.8
  224.4 30.3 %all-to-all-start.4 = ((bf16[8,16,640]{2,1,0:T(8,128)(2,1)}), bf16[8,16,640]{2,1,0:T(8,128)(2,1)S(1)}, u32[]{:S(2)}, u32[]{:S(2)}) async-start(bf16[8,16,640]{2,1,0:T(8,128)(2,1)} %get-tuple-element.33), calls=%async_computation.4 | async-start | bytes 327680 | tf_op jit(solution)/shard_map/all_to_all | solution.py:29
  228.4 21.9 %collective-permute-start.9 = (bf16[2,8,640]{2,1,0:T(8,128)(2,1)S(1)}, bf16[2,8,640]{2,1,0:T(8,128)(2,1)S(1)}, u32[]{:S(2)}, u32[]{:S(2)}) collective-permute-start(bf16[2,8,640]{2,1,0:T(8,128)(2,1)S(1)} %get-tuple-element.37), channel_id=1, source_target_pairs={{0,10},{2,12},{4,14},{6,0},{8,2},{10,4},{12,6},{14,8},{1,11},{3,13... | collective-permute-start | bytes 61448 | tf_op jit(solution)/shard_map/ppermute | solution.py:392
  235.4 15.0 %collective-permute-start.10 = (bf16[2,8,640]{2,1,0:T(8,128)(2,1)S(1)}, bf16[2,8,640]{2,1,0:T(8,128)(2,1)S(1)}, u32[]{:S(2)}, u32[]{:S(2)}) collective-permute-start(bf16[2,8,640]{2,1,0:T(8,128)(2,1)S(1)} %get-tuple-element.38), channel_id=1, source_target_pairs={{0,8},{2,10},{4,12},{6,14},{8,0},{10,2},{12,4},{14,6},{1,9},{3,11}... | collective-permute-start | bytes 61448 | tf_op jit(solution)/shard_map/ppermute | solution.py:392
  238.8 11.5 %collective-permute-start.11 = (bf16[2,8,640]{2,1,0:T(8,128)(2,1)S(1)}, bf16[2,8,640]{2,1,0:T(8,128)(2,1)S(1)}, u32[]{:S(2)}, u32[]{:S(2)}) collective-permute-start(bf16[2,8,640]{2,1,0:T(8,128)(2,1)S(1)} %get-tuple-element.39), channel_id=1, source_target_pairs={{0,6},{2,8},{4,10},{6,12},{8,14},{10,0},{12,2},{14,4},{1,7},{3,9},... | collective-permute-start | bytes 61448 | tf_op jit(solution)/shard_map/ppermute | solution.py:392
  244.0 8.2 %collective-permute-start.12 = (bf16[2,8,640]{2,1,0:T(8,128)(2,1)S(1)}, bf16[2,8,640]{2,1,0:T(8,128)(2,1)S(1)}, u32[]{:S(2)}, u32[]{:S(2)}) collective-permute-start(bf16[2,8,640]{2,1,0:T(8,128)(2,1)S(1)} %get-tuple-element.40), channel_id=1, source_target_pairs={{0,4},{2,6},{4,8},{6,10},{8,12},{10,14},{12,0},{14,2},{1,5},{3,7},... | collective-permute-start | bytes 61448 | tf_op jit(solution)/shard_map/ppermute | solution.py:392
  247.8 6.9 %collective-permute-start.13 = (bf16[2,8,640]{2,1,0:T(8,128)(2,1)S(1)}, bf16[2,8,640]{2,1,0:T(8,128)(2,1)S(1)}, u32[]{:S(2)}, u32[]{:S(2)}) collective-permute-start(bf16[2,8,640]{2,1,0:T(8,128)(2,1)S(1)} %get-tuple-element.41), channel_id=1, source_target_pairs={{0,2},{2,4},{4,6},{6,8},{8,10},{10,12},{12,14},{14,0},{1,3},{3,5},... | collective-permute-start | bytes 61448 | tf_op jit(solution)/shard_map/ppermute | solution.py:392

commit v3 on v2

v3 whole, which is shorter than its diff:
```python
import jax
import jax.numpy as jnp
from jax import lax
from jax.experimental import pallas as pl
from jax.experimental.pallas import tpu as pltpu
from jax.sharding import PartitionSpec as P


D = 3584
LAT = 512
CAP = 8
MOVES = (4, 3, 5, 2, 6, 1, 7)

epsilon = 1e-06
route_scale = 2.5
score_scale = 192.0 ** (-0.5)
f32 = jnp.float32
bf16 = jnp.bfloat16
VMEM = pl.BlockSpec(memory_space=pltpu.VMEM)
SMEM = pl.BlockSpec(memory_space=pltpu.SMEM)
PARAMS = pltpu.CompilerParams(vmem_limit_bytes=40 * 1024 * 1024)


def shape(dims, dtype):
    return jax.ShapeDtypeStruct(dims, dtype)


def exchange(x, axis):
    return lax.all_to_all(x, axis, split_axis=0, concat_axis=0, tiled=True)


def route_kernel(ids_ref, slots_ref, aff_ref, hid_ref, send_ref, comb_ref):
    experts = send_ref.shape[0]
    top, tokens = ids_ref.shape
    rows = experts * CAP
    slots = slots_ref[...]
    affinity = aff_ref[...]
    weight = route_scale * affinity / jnp.sum(affinity, 0, keepdims=True)
    target = jnp.where(slots < CAP, ids_ref[...] * CAP + slots, -1)
    row = lax.broadcasted_iota(jnp.int32, (rows, tokens), 0)
    pick = jnp.zeros((rows, tokens), f32)
    comb = jnp.zeros((rows, tokens), f32)
    for k in range(top):
        match = target[k : k + 1, :] == row
        pick = jnp.where(match, 1.0, pick)
        comb = jnp.where(match, weight[k : k + 1, :], comb)
    comb_ref[...] = comb
    sent = jnp.dot(pick.astype(bf16), hid_ref[...], preferred_element_type=f32)
    send_ref[...] = sent.reshape(send_ref.shape).astype(bf16)


def route(expert_ids, slots, affinity, hidden, experts):
    tokens, width = hidden.shape
    return pl.pallas_call(
        route_kernel,
        out_shape=(shape((experts, CAP, width), bf16), shape((experts * CAP, tokens), f32)),
        in_specs=[VMEM] * 4,
        out_specs=(VMEM, VMEM),
        compiler_params=PARAMS,
        name="route",
    )(expert_ids.T, slots.T, affinity.T, hidden)


def gain_of(block, at, width):
    rows = block[at : at + 16, :].astype(f32)
    tiles = (width + 127) // 128
    total = rows[:tiles] + rows[tiles : 2 * tiles] + rows[2 * tiles : 3 * tiles]
    return [total[q : q + 1, : min(128, width - 128 * q)] for q in range(tiles)]


def units_kernel(me_ref, x_ref, wg_ref, wu_ref, att_ref, *refs):
    peers = x_ref.shape[0]
    blocks, (o_ref, n_ref, g_ref, u_ref) = refs[:peers], refs[peers:]
    half, double = x_ref.shape[1:]
    rows, cols = 2 * half, double // 2
    square = jnp.zeros((rows, 1), f32)
    for j in range(peers):
        n_ref[:half, :] = x_ref[j, :, :cols]
        n_ref[half:, :] = x_ref[j, :, cols:]
        x = n_ref[...].astype(f32)
        square = square + jnp.sum(x * x, -1, keepdims=True)
    scale = lax.rsqrt(square / D + epsilon)
    for k in range(peers):
        j = lax.rem(me_ref[0] + (peers - k), peers)
        gain = jnp.concatenate(gain_of(blocks[k], blocks[k].shape[0] - 16, cols), 1)
        n_ref[:half, :] = x_ref[j, :, :cols]
        n_ref[half:, :] = x_ref[j, :, cols:]
        normed = (n_ref[...].astype(f32) * scale * gain).astype(bf16)
        part = pl.ds(pl.multiple_of(j * cols, 64), cols)
        gate = jnp.dot(normed, wg_ref[part, :], preferred_element_type=f32)
        up = jnp.dot(normed, wu_ref[part, :], preferred_element_type=f32)
        if k == 0:
            g_ref[...] = gate
            u_ref[...] = up
        else:
            g_ref[...] += gate
            u_ref[...] += up
        o_ref[j, rows:, :] = att_ref[k]
    gate = g_ref[...]
    units = (gate / (1.0 + jnp.exp(-gate)) * u_ref[...]).astype(bf16)
    for j in range(peers):
        o_ref[j, :rows, :] = units


def expert_units(me, x, w_gate, w_up, attended, blocks):
    peers, half, double = x.shape
    rows, cols, hid = 2 * half, double // 2, w_gate.shape[1]
    return pl.pallas_call(
        units_kernel,
        out_shape=shape((peers, rows + attended.shape[1], hid), bf16),
        in_specs=[SMEM] + [VMEM] * (4 + peers),
        out_specs=VMEM,
        scratch_shapes=[
            pltpu.VMEM((rows, cols), bf16),
            pltpu.VMEM((rows, hid), f32),
            pltpu.VMEM((rows, hid), f32),
        ],
        compiler_params=PARAMS,
        name="units",
    )(me, x, w_gate, w_up, attended, *blocks)


def pack_kernel(me_ref, wd_ref, cache_ref, q_ref, gain_ref, *refs):
    outs, tiles_ref, keys_ref = refs[:-2], refs[-2], refs[-1]
    peers = len(outs)
    half, double = tiles_ref.shape[1:]
    width = double // 2
    span, heads, keys = cache_ref.shape[1], q_ref.shape[1], cache_ref.shape[2]
    own = cache_ref.shape[0] // peers
    for j in range(peers):
        tiles_ref[j, :, :width] = wd_ref[:half, j * width : (j + 1) * width]
        tiles_ref[j, :, width:] = wd_ref[half:, j * width : (j + 1) * width]
    gain = gain_ref[...]
    first = gain.astype(bf16).astype(f32)
    second = (gain - first).astype(bf16).astype(f32)
    row = lax.broadcasted_iota(jnp.int32, (16, 128), 0)
    packed = jnp.zeros((16, 128), f32)
    tiles = (width + 127) // 128
    for p, value in enumerate((first, second, gain - first - second)):
        for q in range(tiles):
            piece = value[:, 128 * q : min(128 * (q + 1), width)]
            if piece.shape[1] < 128:
                piece = jnp.concatenate([piece, jnp.zeros((1, 128 - piece.shape[1]), f32)], 1)
            packed = jnp.where(row == p * tiles + q, piece, packed)
    packed = packed.astype(bf16)
    for k in range(peers):
        to = lax.rem(me_ref[0] + k, peers)
        at = 0
        for t in range(double // 128):
            outs[k][at : at + half, :] = tiles_ref[to, :, 128 * t : 128 * (t + 1)]
            at += half
        for i in range(own):
            keys_ref[:span, i * keys : (i + 1) * keys] = cache_ref[to * own + i]
            keys_ref[span:, i * keys : (i + 1) * keys] = q_ref[to * own + i]
        for t in range(own * keys // 128):
            outs[k][at : at + span + heads, :] = keys_ref[:, 128 * t : 128 * (t + 1)]
            at += span + heads
        outs[k][at : at + 16, :] = packed


def pack(me, w_down, cache, queries, gain, peers):
    hid, width = w_down.shape[0], w_down.shape[1] // peers
    seqs, span, keys = cache.shape
    own, heads = seqs // peers, queries.shape[1]
    rows = hid * width // 128 + own * (span + heads) * keys // 128 + 16
    return pl.pallas_call(
        pack_kernel,
        out_shape=tuple(shape((rows, 128), bf16) for _ in range(peers)),
        in_specs=[SMEM] + [VMEM] * 4,
        out_specs=tuple(VMEM for _ in range(peers)),
        scratch_shapes=[
            pltpu.VMEM((peers, hid // 2, 2 * width), bf16),
            pltpu.VMEM((span + heads, own * keys), bf16),
        ],
        compiler_params=PARAMS,
        name="pack",
    )(me, w_down, cache, queries, gain)


def spread_kernel(x_ref, o_ref):
    half, double = o_ref.shape[1:]
    width = double // 2
    x = x_ref[...].reshape(2 * half, width)
    for j in range(o_ref.shape[0]):
        o_ref[j, :, :width] = x[:half]
        o_ref[j, :, width:] = x[half:]


def spread_rows(arrived, peers):
    experts, cap, width = arrived.shape
    return pl.pallas_call(
        spread_kernel,
        out_shape=shape((peers, experts * cap // 2, 2 * width), bf16),
        in_specs=[VMEM],
        out_specs=VMEM,
        compiler_params=PARAMS,
        name="rows",
    )(arrived)


def down_kernel(me_ref, u_ref, *refs):
    blocks, o_ref, w_ref = refs[:-2], refs[-2], refs[-1]
    peers, _, hid = u_ref.shape
    experts, cap, width = o_ref.shape
    rows, half = experts * cap, hid // 2
    acc = jnp.zeros((rows, width), f32)
    for k in range(peers):
        group = lax.rem(me_ref[0] + (peers - k), peers)
        for t in range(2 * width // 128):
            w_ref[:, 128 * t : 128 * (t + 1)] = blocks[k][half * t : half * (t + 1), :]
        units = u_ref[group, :rows, :]
        acc = acc + jnp.dot(units[:, :half], w_ref[:, :width], preferred_element_type=f32)
        acc = acc + jnp.dot(units[:, half:], w_ref[:, width:], preferred_element_type=f32)
    o_ref[...] = acc.reshape(o_ref.shape).astype(bf16)


def expert_down(me, units, blocks, experts, width):
    hid = units.shape[2]
    return pl.pallas_call(
        down_kernel,
        out_shape=shape((experts, CAP, width), bf16),
        in_specs=[SMEM] + [VMEM] * (1 + len(blocks)),
        out_specs=VMEM,
        scratch_shapes=[pltpu.VMEM((hid // 2, 2 * width), bf16)],
        compiler_params=PARAMS,
        name="down",
    )(me, units, *blocks)


def attend_kernel(me_ref, len_ref, *refs):
    peers = len(refs) - 4
    blocks, (o_ref, m_ref, c_ref, q_ref) = refs[:peers], refs[peers:]
    own, positions, keys = c_ref.shape
    span, heads = positions // peers, q_ref.shape[1] // peers
    me = me_ref[0]
    first = blocks[0].shape[0] - 16 - own * keys // 128 * (span + heads)
    for k in range(peers):
        for t in range(own * keys // 128):
            at = first + t * (span + heads)
            m_ref[:, 128 * t : 128 * (t + 1)] = blocks[k][at : at + span + heads, :]
        for i in range(own):
            c_ref[i, k * span : (k + 1) * span, :] = m_ref[:span, i * keys : (i + 1) * keys]
            q_ref[i, k * heads : (k + 1) * heads, :] = m_ref[span:, i * keys : (i + 1) * keys]
    lane = lax.broadcasted_iota(jnp.int32, (peers * heads, positions), 1)
    block = lax.rem(me + (peers - lane // span), peers)
    position = block * span + lane % span
    for i in range(own):
        live = position < len_ref[me * own + i]
        known = c_ref[i]
        scores = (
            lax.dot_general(
                q_ref[i], known, (((1,), (1,)), ((), ())), preferred_element_type=f32
            )
            * score_scale
        )
        scores = jnp.where(live, scores, -1e30)
        peak = jnp.max(scores, -1, keepdims=True)
        prob = jnp.where(live, jnp.exp(scores - peak), 0.0)
        mass = jnp.sum(prob, -1, keepdims=True)
        out = jnp.dot(prob.astype(bf16), known[:, :LAT], preferred_element_type=f32)
        out = (out / mass).astype(bf16)
        total = peak + jnp.log(mass)
        high = total.astype(bf16).astype(f32)
        middle = (total - high).astype(bf16).astype(f32)
        low = total - high - middle
        tail_lane = lax.broadcasted_iota(jnp.int32, (peers * heads, 128), 1)
        tail = jnp.where(
            tail_lane == 0,
            high,
            jnp.where(tail_lane == 1, middle, jnp.where(tail_lane == 2, low, 0.0)),
        ).astype(bf16)
        for k in range(peers):
            for t in range(LAT // 128 + 1):
                at = (t * own + i) * heads
                piece = tail if t == LAT // 128 else out[:, 128 * t : 128 * (t + 1)]
                o_ref[k, at : at + heads, :] = piece[k * heads : (k + 1) * heads]


def attend(me, lengths, blocks, own, span, heads, keys):
    peers = len(blocks)
    return pl.pallas_call(
        attend_kernel,
        out_shape=shape((peers, own * heads * (LAT // 128 + 1), 128), bf16),
        in_specs=[SMEM, SMEM] + [VMEM] * peers,
        out_specs=VMEM,
        scratch_shapes=[
            pltpu.VMEM((span + heads, own * keys), bf16),
            pltpu.VMEM((own, peers * span, keys), bf16),
            pltpu.VMEM((own, peers * heads, keys), bf16),
        ],
        compiler_params=PARAMS,
        name="attend",
    )(me, lengths, *blocks)


def close_kernel(ret_ref, comb_ref, hid_ref, gain_ref, wdkv_ref, next_ref, small_ref):
    rows = comb_ref.shape[0]
    keys = wdkv_ref.shape[1]
    returned = ret_ref[...].reshape(rows, ret_ref.shape[-1])
    comb = comb_ref[...]
    high = comb.astype(bf16)
    low = (comb - high.astype(f32)).astype(bf16)
    first_dim = (((0,), (0,)), ((), ()))
    moe = lax.dot_general(
        high, returned, first_dim, preferred_element_type=f32
    ) + lax.dot_general(low, returned, first_dim, preferred_element_type=f32)
    result = (hid_ref[...].astype(f32) + moe).astype(bf16)
    next_ref[...] = result
    wide = result.astype(f32)
    square = jnp.sum(wide * wide, -1, keepdims=True)
    first = square.astype(bf16).astype(f32)
    second = (square - first).astype(bf16).astype(f32)
    third = square - first - second
    lane = lax.broadcasted_iota(jnp.int32, (wide.shape[0], small_ref.shape[2] - keys), 1)
    tail = jnp.where(
        lane == 0, first, jnp.where(lane == 1, second, jnp.where(lane == 2, third, 0.0))
    ).astype(bf16)
    down = jnp.dot(
        (wide * gain_ref[...]).astype(bf16), wdkv_ref[...], preferred_element_type=f32
    ).astype(bf16)
    for j in range(small_ref.shape[0]):
        small_ref[j, :, :keys] = down
        small_ref[j, :, keys:] = tail


def close(returned, combine, hidden, gain, w_dkv, peers):
    tokens, width = hidden.shape
    return pl.pallas_call(
        close_kernel,
        out_shape=(
            shape((tokens, width), bf16),
            shape((peers, tokens, w_dkv.shape[1] + 64), bf16),
        ),
        in_specs=[VMEM] * 5,
        out_specs=(VMEM, VMEM),
        compiler_params=PARAMS,
        name="close",
    )(returned, combine, hidden, gain, w_dkv)


def merge_kernel(all_ref, gain_ref, cos_ref, sin_ref, q_ref, units_ref, o_ref, back_ref):
    peers = all_ref.shape[0]
    seqs, heads, lanes = back_ref.shape
    own = seqs // peers
    first = units_ref.shape[1] - own * heads * (lanes // 128)
    for j in range(peers):
        for i in range(own):
            for t in range(lanes // 128):
                at = first + (t * own + i) * heads
                back_ref[j * own + i, :, 128 * t : 128 * (t + 1)] = units_ref[
                    j, at : at + heads, :
                ]
    keys = q_ref.shape[-1]
    total = all_ref[0].astype(f32)
    for j in range(1, all_ref.shape[0]):
        total = total + all_ref[j].astype(f32)
    square = jnp.sum(total[:, keys:], -1, keepdims=True)
    down = total[:, :keys] * lax.rsqrt(square / D + epsilon)
    latent = down[:, :LAT]
    latent = (
        latent
        * lax.rsqrt(jnp.mean(latent * latent, -1, keepdims=True) + epsilon)
        * gain_ref[...]
    )
    rope = down[:, LAT:]
    half = rope.shape[-1] // 2
    turned = jnp.concatenate([rope[:, half:], rope[:, :half]], 1)
    rope = rope * cos_ref[...] + turned * sin_ref[...]
    latent = latent.astype(bf16).astype(f32)[:, None, :]
    rope = rope.astype(bf16).astype(f32)[:, None, :]
    own = (
        jnp.sum(q_ref[:, :, :LAT].astype(f32) * latent, -1, keepdims=True)
        + jnp.sum(q_ref[:, :, LAT:].astype(f32) * rope, -1, keepdims=True)
    ) * score_scale
    cached = jnp.sum(back_ref[:, :, LAT:].astype(f32), -1, keepdims=True)
    peak = jnp.maximum(own, cached)
    own_prob = jnp.exp(own - peak)
    cached_prob = jnp.exp(cached - peak)
    total_prob = own_prob + cached_prob
    o_ref[...] = (
        back_ref[:, :, :LAT].astype(f32) * (cached_prob / total_prob)
        + latent * (own_prob / total_prob)
    ).astype(bf16)


def merge(everything, gain, cos, sin, queries, units):
    seqs, heads, _ = queries.shape
    return pl.pallas_call(
        merge_kernel,
        out_shape=shape((seqs, heads, LAT), bf16),
        in_specs=[VMEM] * 6,
        out_specs=VMEM,
        scratch_shapes=[pltpu.VMEM((seqs, heads, LAT + 128), bf16)],
        compiler_params=PARAMS,
        name="merge",
    )(everything, gain, cos, sin, queries, units)


def mark_kernel(x_ref, o_ref):
    o_ref[...] = x_ref[...]


def mark(x):
    return pl.pallas_call(
        mark_kernel, out_shape=shape(x.shape, x.dtype), in_specs=[VMEM], out_specs=VMEM
    )(x)


def rope_tables(lengths, half):
    inv_freq = 10000.0 ** (-jnp.arange(half, dtype=f32) / half)
    angles = lengths.astype(f32)[:, None] * inv_freq[None, :]
    cos, sin = jnp.cos(angles), jnp.sin(angles)
    return jnp.concatenate([cos, cos], 1), jnp.concatenate([-sin, sin], 1)


def local(
    hidden,
    moe_gain,
    expert_ids,
    slots,
    affinity,
    w_gate,
    w_up,
    w_down,
    attn_gain,
    w_dkv,
    kv_gain,
    queries,
    cache,
    lengths,
):
    seqs, width = hidden.shape
    peers = lax.axis_size("tp")
    experts = lax.axis_size("ep") * lax.axis_size("mb")
    me = lax.axis_index("tp").astype(jnp.int32).reshape(1)

    def moved(x, k):
        return lax.ppermute(x, "tp", [(i, (i + k) % peers) for i in range(peers)])

    send_rows, combine = route(expert_ids, slots, affinity, hidden, experts)
    arrived = exchange(send_rows, ("ep", "mb"))
    blocks = list(pack(me, w_down[0], cache, queries, moe_gain[None], peers))
    for k in MOVES:
        blocks[k] = moved(blocks[k], k)
    attn_gain = mark(attn_gain[None])
    rows = spread_rows(arrived, peers)
    portion = exchange(rows, "tp")
    span, heads, keys = cache.shape[1], queries.shape[1], queries.shape[2]
    attended = attend(me, lengths, blocks, seqs // peers, span, heads, keys)
    units = expert_units(me, portion, w_gate[0], w_up[0], attended, blocks)
    all_units = exchange(units, "tp")
    output = expert_down(me, all_units, blocks, experts, width)
    returned = exchange(output, ("ep", "mb"))
    next_hidden, small = close(returned, combine, hidden, attn_gain, w_dkv, peers)
    everything = exchange(small, "tp")
    cos, sin = rope_tables(lengths, (keys - LAT) // 2)
    latent_out = merge(everything, kv_gain[None], cos, sin, queries, all_units)
    return (next_hidden, latent_out)


def solution(mesh):
    return jax.shard_map(
        local,
        mesh=mesh,
        in_specs=(
            P(("grp", "ep", "mb"), "tp"),
            P("tp"),
            P(("grp", "ep", "mb"), None),
            P(("grp", "ep", "mb"), None),
            P(("grp", "ep", "mb"), None),
            P(("ep", "mb"), None, "tp"),
            P(("ep", "mb"), None, "tp"),
            P(("ep", "mb"), "tp", None),
            P("tp"),
            P("tp", None),
            P(),
            P(("grp", "ep", "mb"), "tp", None),
            P(("grp", "ep", "mb"), "tp", None),
            P(("grp", "ep", "mb")),
        ),
        out_specs=(P(("grp", "ep", "mb"), "tp"), P(("grp", "ep", "mb"), "tp", None)),
        check_vma=False,
    )
```

time: 257 us -> 230 us (0.89)
  starting transfers between devices: 118 us -> 45.7 us
  blocking collectives: 59.9 us -> 88.9 us
  waiting for transfers between devices: 61.5 us -> 73.8 us
  local copies, waits for them, and re-layouts: 4.4 us -> 9.63 us
    all_to_all x4 -> x3, starting transfers between devices: 57 us -> 15.8 us  [exchange(): return lax.all_to_all(x, axis, split_axis=0, concat_axis=0, tiled=True)]
    ppermute x14 -> x7, starting transfers between devices: 60.6 us -> 29.9 us  [moved(): return lax.ppermute(x, 'tp', [(i, (i + k) % peers) for i in range(peers)])]
    all_to_all x1 -> x2, blocking collectives: 59.9 us -> 88.9 us  [exchange(): return lax.all_to_all(x, axis, split_axis=0, concat_axis=0, tiled=True)]
    ppermute x14 -> x7, waiting for transfers between devices: 27.8 us -> 44.1 us  [moved(): return lax.ppermute(x, 'tp', [(i, (i + k) % peers) for i in range(peers)])]
    unnamed x27 -> x36, local copies, waits for them, and re-layouts: 4.4 us -> 9.63 us
    all_to_all x4 -> x3, waiting for transfers between devices: 33.6 us -> 29.6 us  [exchange(): return lax.all_to_all(x, axis, split_axis=0, concat_axis=0, tiled=True)]
  transfers between devices with their start and end apart: 18 -> 10, of which waited for: 8 -> 6; matrix products, arithmetic and copies ran while one was open for 0% -> 0% of each run, Pallas kernels for 2% -> 1%
where the time goes in v3:
time: 230 us; the launch traced here: 229 us
  blocking collectives  88.9 us (39%)
  waiting for transfers between devices  73.8 us (32%)
  starting transfers between devices  45.7 us (20%)
  Pallas kernels  10.1 us (4%)
  local copies, waits for them, and re-layouts  9.63 us (4%)
    all_to_all x2, blocking collectives, exchange(): return lax.all_to_all(x, axis, split_axis=0, concat_axis=0, tiled=True)  88.9 us
    ppermute x7, waiting for transfers between devices, moved(): return lax.ppermute(x, 'tp', [(i, (i + k) % peers) for i in range(peers)])  44.1 us
    ppermute x7, starting transfers between devices, moved(): return lax.ppermute(x, 'tp', [(i, (i + k) % peers) for i in range(peers)])  29.9 us
    all_to_all x3, waiting for transfers between devices, exchange(): return lax.all_to_all(x, axis, split_axis=0, concat_axis=0, tiled=True)  29.6 us
    all_to_all x3, starting transfers between devices, exchange(): return lax.all_to_all(x, axis, split_axis=0, concat_axis=0, tiled=True)  15.8 us
    unnamed x36, local copies, waits for them, and re-layouts  9.63 us
  transfers between devices with their start and end apart: 10, of which 6 were waited for; matrix products, arithmetic and copies ran while one was open for 0% of the time, Pallas kernels for 1%

profile of v3, /device:TPU:80, one launch (start us, length us, event | category | flops | bytes accessed | tf_op | source)
XLA Modules:
  0.0 229.2 jit_solution(17054063946951186687)
XLA Ops:
  0.6 0.0 copy-start.9
  0.6 0.7 copy-done.9
  1.4 0.7 copy-done.12
  2.0 0.7 copy-done.13
  2.7 0.7 copy-done.14
  3.4 0.2 route.1
  3.7 66.2 %all_to_all.25.x_ref = bf16[32,8,448]{2,1,0:T(8,128)(2,1)S(1)} all-to-all(bf16[32,8,448]{2,1,0:T(8,128)(2,1)S(1)} %get-tuple-element.14), channel_id=1, replica_groups=mesh['grp'=2,'ep'=16,'tp'=8,'mb'=2] {'ep','mb'}, dimensions={0} | all-to-all | bytes 458752 | tf_op jit(solution)/shard_map/all_to_all | solution.py:29
  69.9 0.2 rows.1
  70.1 1.2 copy-done
  71.4 7.5 %all-to-all-start.1 = ((bf16[8,128,896]{2,1,0:T(8,128)(2,1)}), bf16[8,128,896]{2,1,0:T(8,128)(2,1)S(1)}, u32[]{:S(2)}, u32[]{:S(2)}) async-start(bf16[8,128,896]{2,1,0:T(8,128)(2,1)} %copy-done), calls=%async_computation.1 | async-start | bytes 3670016 | tf_op jit(solution)/shard_map/all_to_all | solution.py:29
  78.9 0.0 copy-start.8
  78.9 1.0 copy-done.8
  79.8 0.5 pack.1
  80.3 3.9 %collective-permute-start = (bf16[680,128]{1,0:T(8,128)(2,1)S(1)}, bf16[680,128]{1,0:T(8,128)(2,1)S(1)}, u32[]{:S(2)}, u32[]{:S(2)}) collective-permute-start(bf16[680,128]{1,0:T(8,128)(2,1)S(1)} %get-tuple-element.16), channel_id=1, source_target_pairs={{0,2},{2,4},{4,6},{6,8},{8,10},{10,12},{12,14},{14,0},{1,3},{3,5},... | collective-permute-start | bytes 522248 | tf_op jit(solution)/shard_map/ppermute | solution.py:438
  84.3 4.3 %collective-permute-start.1 = (bf16[680,128]{1,0:T(8,128)(2,1)S(1)}, bf16[680,128]{1,0:T(8,128)(2,1)S(1)}, u32[]{:S(2)}, u32[]{:S(2)}) collective-permute-start(bf16[680,128]{1,0:T(8,128)(2,1)S(1)} %get-tuple-element.17), channel_id=1, source_target_pairs={{0,4},{2,6},{4,8},{6,10},{8,12},{10,14},{12,0},{14,2},{1,5},{3,7},... | collective-permute-start | bytes 522248 | tf_op jit(solution)/shard_map/ppermute | solution.py:438
  88.6 4.6 %collective-permute-start.2 = (bf16[680,128]{1,0:T(8,128)(2,1)S(1)}, bf16[680,128]{1,0:T(8,128)(2,1)S(1)}, u32[]{:S(2)}, u32[]{:S(2)}) collective-permute-start(bf16[680,128]{1,0:T(8,128)(2,1)S(1)} %get-tuple-element.18), channel_id=1, source_target_pairs={{0,6},{2,8},{4,10},{6,12},{8,14},{10,0},{12,2},{14,4},{1,7},{3,9},... | collective-permute-start | bytes 522248 | tf_op jit(solution)/shard_map/ppermute | solution.py:438
  93.2 4.3 %collective-permute-start.3 = (bf16[680,128]{1,0:T(8,128)(2,1)S(1)}, bf16[680,128]{1,0:T(8,128)(2,1)S(1)}, u32[]{:S(2)}, u32[]{:S(2)}) collective-permute-start(bf16[680,128]{1,0:T(8,128)(2,1)S(1)} %get-tuple-element.19), channel_id=1, source_target_pairs={{0,8},{2,10},{4,12},{6,14},{8,0},{10,2},{12,4},{14,6},{1,9},{3,11}... | collective-permute-start | bytes 522248 | tf_op jit(solution)/shard_map/ppermute | solution.py:438
  97.5 4.6 %collective-permute-start.4 = (bf16[680,128]{1,0:T(8,128)(2,1)S(1)}, bf16[680,128]{1,0:T(8,128)(2,1)S(1)}, u32[]{:S(2)}, u32[]{:S(2)}) collective-permute-start(bf16[680,128]{1,0:T(8,128)(2,1)S(1)} %get-tuple-element.20), channel_id=1, source_target_pairs={{0,10},{2,12},{4,14},{6,0},{8,2},{10,4},{12,6},{14,8},{1,11},{3,13... | collective-permute-start | bytes 522248 | tf_op jit(solution)/shard_map/ppermute | solution.py:438
  102.1 25.0 %collective-permute-done.refs_1_ = bf16[680,128]{1,0:T(8,128)(2,1)S(1)} collective-permute-done((bf16[680,128]{1,0:T(8,128)(2,1)S(1)}, bf16[680,128]{1,0:T(8,128)(2,1)S(1)}, u32[]{:S(2)}, u32[]{:S(2)}) %collective-permute-start) | collective-permute-done | bytes 174112 | tf_op jit(solution)/shard_map/ppermute | solution.py:438
  127.1 3.8 %collective-permute-start.5 = (bf16[680,128]{1,0:T(8,128)(2,1)S(1)}, bf16[680,128]{1,0:T(8,128)(2,1)S(1)}, u32[]{:S(2)}, u32[]{:S(2)}) collective-permute-start(bf16[680,128]{1,0:T(8,128)(2,1)S(1)} %get-tuple-element.21), channel_id=1, source_target_pairs={{0,12},{2,14},{4,0},{6,2},{8,4},{10,6},{12,8},{14,10},{1,13},{3,15... | collective-permute-start | bytes 522248 | tf_op jit(solution)/shard_map/ppermute | solution.py:438
  130.9 4.1 %collective-permute-done.1.refs_2_ = bf16[680,128]{1,0:T(8,128)(2,1)S(1)} collective-permute-done((bf16[680,128]{1,0:T(8,128)(2,1)S(1)}, bf16[680,128]{1,0:T(8,128)(2,1)S(1)}, u32[]{:S(2)}, u32[]{:S(2)}) %collective-permute-start.1) | collective-permute-done | bytes 174112 | tf_op jit(solution)/shard_map/ppermute | solution.py:438
  135.1 4.3 %collective-permute-start.6 = (bf16[680,128]{1,0:T(8,128)(2,1)S(1)}, bf16[680,128]{1,0:T(8,128)(2,1)S(1)}, u32[]{:S(2)}, u32[]{:S(2)}) collective-permute-start(bf16[680,128]{1,0:T(8,128)(2,1)S(1)} %get-tuple-element.22), channel_id=1, source_target_pairs={{0,14},{2,0},{4,2},{6,4},{8,6},{10,8},{12,10},{14,12},{1,15},{3,1}... | collective-permute-start | bytes 522248 | tf_op jit(solution)/shard_map/ppermute | solution.py:438
  139.4 6.1 %collective-permute-done.2.refs_3_ = bf16[680,128]{1,0:T(8,128)(2,1)S(1)} collective-permute-done((bf16[680,128]{1,0:T(8,128)(2,1)S(1)}, bf16[680,128]{1,0:T(8,128)(2,1)S(1)}, u32[]{:S(2)}, u32[]{:S(2)}) %collective-permute-start.2) | collective-permute-done | bytes 174112 | tf_op jit(solution)/shard_map/ppermute | solution.py:438
  145.5 8.9 %collective-permute-done.3.refs_4_ = bf16[680,128]{1,0:T(8,128)(2,1)S(1)} collective-permute-done((bf16[680,128]{1,0:T(8,128)(2,1)S(1)}, bf16[680,128]{1,0:T(8,128)(2,1)S(1)}, u32[]{:S(2)}, u32[]{:S(2)}) %collective-permute-start.3) | collective-permute-done | bytes 174112 | tf_op jit(solution)/shard_map/ppermute | solution.py:438
  154.4 0.0 collective-permute-done.4.refs_5_
  154.4 0.0 collective-permute-done.5.refs_6_
  154.4 0.0 collective-permute-done.6.refs_7_
  154.4 1.3 attend.1.att_ref
  155.8 0.7 copy-done.5
  156.4 0.0 all-to-all-done.1.x_ref
  156.4 1.2 copy-done.2
  157.6 1.2 copy-done.3
  158.8 0.9 copy-done.6
  159.7 2.3 units.1
  162.0 0.0 copy-start.7
  162.0 0.0 copy-start.10
  162.0 22.7 %all_to_all.26.u_ref.units_ref = bf16[8,336,128]{2,1,0:T(8,128)(2,1)S(1)} all-to-all(bf16[8,336,128]{2,1,0:T(8,128)(2,1)S(1)} %units.1), channel_id=1, replica_groups=mesh['grp'=2,'ep'=16,'tp'=8,'mb'=2] {'tp'}, dimensions={0} | all-to-all | bytes 1376256 | tf_op jit(solution)/shard_map/all_to_all | solution.py:29
  184.7 2.1 down.1
  186.8 4.8 %all-to-all-start.3 = ((bf16[32,8,448]{2,1,0:T(8,128)(2,1)}), bf16[32,8,448]{2,1,0:T(8,128)(2,1)S(1)}, u32[]{:S(2)}, u32[]{:S(2)}) async-start(bf16[32,8,448]{2,1,0:T(8,128)(2,1)} %down.1), calls=%async_computation.3 | async-start | bytes 524288 | tf_op jit(solution)/shard_map/all_to_all | solution.py:29
  191.6 1.3 shard_map.149.gain_ref
  192.9 20.7 %all-to-all-done.3.ret_ref = bf16[32,8,448]{2,1,0:T(8,128)(2,1)S(1)} async-done(((bf16[32,8,448]{2,1,0:T(8,128)(2,1)}), bf16[32,8,448]{2,1,0:T(8,128)(2,1)S(1)}, u32[]{:S(2)}, u32[]{:S(2)}) %all-to-all-start.3) | async-done | bytes 229408 | tf_op jit(solution)/shard_map/all_to_all | solution.py:29
  213.6 0.7 copy-done.11
  214.2 1.0 close.1
  215.3 3.6 %all-to-all-start.4 = ((bf16[8,16,640]{2,1,0:T(8,128)(2,1)}), bf16[8,16,640]{2,1,0:T(8,128)(2,1)S(1)}, u32[]{:S(2)}, u32[]{:S(2)}) async-start(bf16[8,16,640]{2,1,0:T(8,128)(2,1)} %get-tuple-element.25), calls=%async_computation.4 | async-start | bytes 327680 | tf_op jit(solution)/shard_map/all_to_all | solution.py:29
  218.9 0.1 fusion
  219.0 0.1 pad_maximum_fusion
  219.1 9.0 %all-to-all-done.4.all_ref = bf16[8,16,640]{2,1,0:T(8,128)(2,1)S(1)} async-done(((bf16[8,16,640]{2,1,0:T(8,128)(2,1)}), bf16[8,16,640]{2,1,0:T(8,128)(2,1)S(1)}, u32[]{:S(2)}, u32[]{:S(2)}) %all-to-all-start.4) | async-done | bytes 163872 | tf_op jit(solution)/shard_map/all_to_all | solution.py:29
  228.1 1.1 merge.1
  (23 shorter events, 0.1 us)
Async XLA Ops:
  0.6 0.7 copy-start.9
  1.4 0.7 copy-start.12
  2.0 0.7 copy-start.13
  2.7 0.7 copy-start.14
  70.1 1.3 copy-start
  71.4 7.5 %copy-start.1 = (bf16[1,128,3584]{2,1,0:T(8,128)(2,1)S(1)}, bf16[1,128,3584]{2,1,0:T(8,128)(2,1)}, u32[]{:S(2)}) copy-start(bf16[1,128,3584]{2,1,0:T(8,128)(2,1)} %param.21) | copy-start | bytes 2752516
  71.4 7.5 %copy-start.4 = (bf16[16,8,576]{2,1,0:T(8,128)(2,1)S(1)}, bf16[16,8,576]{2,1,0:T(8,128)(2,1)}, u32[]{:S(2)}) copy-start(bf16[16,8,576]{2,1,0:T(8,128)(2,1)} %q_ref.3) | copy-start | bytes 442372
  71.4 7.5 %copy-start.15 = (f32[448]{0:T(512)S(1)}, f32[448]{0:T(512)}, u32[]{:S(2)}) copy-start(f32[448]{0:T(512)} %param.15) | copy-start | bytes 5380
  71.4 83.0 %copy-start.17 = (s32[16]{0:T(128)S(1)}, s32[16]{0:T(128)}, u32[]{:S(2)}) copy-start(s32[16]{0:T(128)} %len_ref.1) | copy-start | bytes 196
  71.4 85.0 %all-to-all-start.1 = ((bf16[8,128,896]{2,1,0:T(8,128)(2,1)}), bf16[8,128,896]{2,1,0:T(8,128)(2,1)S(1)}, u32[]{:S(2)}, u32[]{:S(2)}) async-start(bf16[8,128,896]{2,1,0:T(8,128)(2,1)} %copy-done), calls=%async_computation.1 | async-start | bytes 3670016 | tf_op jit(solution)/shard_map/all_to_all | solution.py:29
  78.9 1.0 copy-start.8
  80.3 46.8 %collective-permute-start = (bf16[680,128]{1,0:T(8,128)(2,1)S(1)}, bf16[680,128]{1,0:T(8,128)(2,1)S(1)}, u32[]{:S(2)}, u32[]{:S(2)}) collective-permute-start(bf16[680,128]{1,0:T(8,128)(2,1)S(1)} %get-tuple-element.16), channel_id=1, source_target_pairs={{0,2},{2,4},{4,6},{6,8},{8,10},{10,12},{12,14},{14,0},{1,3},{3,5},... | collective-permute-start | bytes 522248 | tf_op jit(solution)/shard_map/ppermute | solution.py:438
  84.3 50.8 %collective-permute-start.1 = (bf16[680,128]{1,0:T(8,128)(2,1)S(1)}, bf16[680,128]{1,0:T(8,128)(2,1)S(1)}, u32[]{:S(2)}, u32[]{:S(2)}) collective-permute-start(bf16[680,128]{1,0:T(8,128)(2,1)S(1)} %get-tuple-element.17), channel_id=1, source_target_pairs={{0,4},{2,6},{4,8},{6,10},{8,12},{10,14},{12,0},{14,2},{1,5},{3,7},... | collective-permute-start | bytes 522248 | tf_op jit(solution)/shard_map/ppermute | solution.py:438
  88.6 56.9 %collective-permute-start.2 = (bf16[680,128]{1,0:T(8,128)(2,1)S(1)}, bf16[680,128]{1,0:T(8,128)(2,1)S(1)}, u32[]{:S(2)}, u32[]{:S(2)}) collective-permute-start(bf16[680,128]{1,0:T(8,128)(2,1)S(1)} %get-tuple-element.18), channel_id=1, source_target_pairs={{0,6},{2,8},{4,10},{6,12},{8,14},{10,0},{12,2},{14,4},{1,7},{3,9},... | collective-permute-start | bytes 522248 | tf_op jit(solution)/shard_map/ppermute | solution.py:438
  93.2 61.2 %collective-permute-start.3 = (bf16[680,128]{1,0:T(8,128)(2,1)S(1)}, bf16[680,128]{1,0:T(8,128)(2,1)S(1)}, u32[]{:S(2)}, u32[]{:S(2)}) collective-permute-start(bf16[680,128]{1,0:T(8,128)(2,1)S(1)} %get-tuple-element.19), channel_id=1, source_target_pairs={{0,8},{2,10},{4,12},{6,14},{8,0},{10,2},{12,4},{14,6},{1,9},{3,11}... | collective-permute-start | bytes 522248 | tf_op jit(solution)/shard_map/ppermute | solution.py:438
  97.5 56.9 %collective-permute-start.4 = (bf16[680,128]{1,0:T(8,128)(2,1)S(1)}, bf16[680,128]{1,0:T(8,128)(2,1)S(1)}, u32[]{:S(2)}, u32[]{:S(2)}) collective-permute-start(bf16[680,128]{1,0:T(8,128)(2,1)S(1)} %get-tuple-element.20), channel_id=1, source_target_pairs={{0,10},{2,12},{4,14},{6,0},{8,2},{10,4},{12,6},{14,8},{1,11},{3,13... | collective-permute-start | bytes 522248 | tf_op jit(solution)/shard_map/ppermute | solution.py:438
  127.1 27.3 %collective-permute-start.5 = (bf16[680,128]{1,0:T(8,128)(2,1)S(1)}, bf16[680,128]{1,0:T(8,128)(2,1)S(1)}, u32[]{:S(2)}, u32[]{:S(2)}) collective-permute-start(bf16[680,128]{1,0:T(8,128)(2,1)S(1)} %get-tuple-element.21), channel_id=1, source_target_pairs={{0,12},{2,14},{4,0},{6,2},{8,4},{10,6},{12,8},{14,10},{1,13},{3,15... | collective-permute-start | bytes 522248 | tf_op jit(solution)/shard_map/ppermute | solution.py:438
  135.1 19.3 %collective-permute-start.6 = (bf16[680,128]{1,0:T(8,128)(2,1)S(1)}, bf16[680,128]{1,0:T(8,128)(2,1)S(1)}, u32[]{:S(2)}, u32[]{:S(2)}) collective-permute-start(bf16[680,128]{1,0:T(8,128)(2,1)S(1)} %get-tuple-element.22), channel_id=1, source_target_pairs={{0,14},{2,0},{4,2},{6,4},{8,6},{10,8},{12,10},{14,12},{1,15},{3,1}... | collective-permute-start | bytes 522248 | tf_op jit(solution)/shard_map/ppermute | solution.py:438
  155.8 0.7 copy-start.5
  156.4 1.2 copy-start.2
  157.6 1.2 copy-start.3
  158.8 0.9 copy-start.6
  162.0 51.6 %copy-start.7 = (bf16[448,576]{1,0:T(8,128)(2,1)S(1)}, bf16[448,576]{1,0:T(8,128)(2,1)}, u32[]{:S(2)}) copy-start(bf16[448,576]{1,0:T(8,128)(2,1)} %wdkv_ref.1) | copy-start | bytes 1548292
  162.0 51.5 %copy-start.10 = (bf16[16,448]{1,0:T(8,128)(2,1)S(1)}, bf16[16,448]{1,0:T(8,128)(2,1)}, u32[]{:S(2)}) copy-start(bf16[16,448]{1,0:T(8,128)(2,1)} %hid_ref.3) | copy-start | bytes 43012
  184.7 43.3 %copy-start.16 = (f32[512]{0:T(512)S(1)}, f32[512]{0:T(512)}, u32[]{:S(2)}) copy-start(f32[512]{0:T(512)} %param.24) | copy-start | bytes 6148
  186.8 26.7 %all-to-all-start.3 = ((bf16[32,8,448]{2,1,0:T(8,128)(2,1)}), bf16[32,8,448]{2,1,0:T(8,128)(2,1)S(1)}, u32[]{:S(2)}, u32[]{:S(2)}) async-start(bf16[32,8,448]{2,1,0:T(8,128)(2,1)} %down.1), calls=%async_computation.3 | async-start | bytes 524288 | tf_op jit(solution)/shard_map/all_to_all | solution.py:29
  213.6 0.7 copy-start.11
  215.3 12.8 %all-to-all-start.4 = ((bf16[8,16,640]{2,1,0:T(8,128)(2,1)}), bf16[8,16,640]{2,1,0:T(8,128)(2,1)S(1)}, u32[]{:S(2)}, u32[]{:S(2)}) async-start(bf16[8,16,640]{2,1,0:T(8,128)(2,1)} %get-tuple-element.25), calls=%async_computation.4 | async-start | bytes 327680 | tf_op jit(solution)/shard_map/all_to_all | solution.py:29

commit v4 on v3

--- a/solution.py
+++ b/solution.py
@@ -18,6 +18,7 @@
 bf16 = jnp.bfloat16
 VMEM = pl.BlockSpec(memory_space=pltpu.VMEM)
 SMEM = pl.BlockSpec(memory_space=pltpu.SMEM)
+HBM = pl.BlockSpec(memory_space=pltpu.HBM)
 PARAMS = pltpu.CompilerParams(vmem_limit_bytes=40 * 1024 * 1024)
 
 
@@ -29,7 +30,33 @@
     return lax.all_to_all(x, axis, split_axis=0, concat_axis=0, tiled=True)
 
 
-def route_kernel(ids_ref, slots_ref, aff_ref, hid_ref, send_ref, comb_ref):
+def ahead(me_ref, k, peers):
+    return lax.rem(me_ref[0] + me_ref[1] * k + peers, peers)
+
+
+def behind(me_ref, k, peers):
+    return lax.rem(me_ref[0] - me_ref[1] * k + peers, peers)
+
+
+def in_hbm(x):
+    return pltpu.with_memory_space_constraint(x, pltpu.HBM)
+
+
+def fetch(sources, targets, sems):
+    copies = [
+        pltpu.make_async_copy(source, target, sems.at[i])
+        for i, (source, target) in enumerate(zip(sources, targets))
+    ]
+    for copy in copies:
+        copy.start()
+    return copies
+
+
+def route_kernel(ids_hbm, slots_hbm, aff_hbm, hid_hbm, send_ref, comb_ref, *refs):
+    ids_ref, slots_ref, aff_ref, hid_ref, sems = refs
+    copies = fetch((ids_hbm, slots_hbm, aff_hbm, hid_hbm), refs[:4], sems)
+    for copy in copies:
+        copy.wait()
     experts = send_ref.shape[0]
     top, tokens = ids_ref.shape
     rows = experts * CAP
@@ -51,14 +78,17 @@
 
 def route(expert_ids, slots, affinity, hidden, experts):
     tokens, width = hidden.shape
+    inputs = (expert_ids.T, slots.T, affinity.T, hidden)
     return pl.pallas_call(
         route_kernel,
         out_shape=(shape((experts, CAP, width), bf16), shape((experts * CAP, tokens), f32)),
-        in_specs=[VMEM] * 4,
+        in_specs=[HBM] * 4,
         out_specs=(VMEM, VMEM),
+        scratch_shapes=[pltpu.VMEM(x.shape, x.dtype) for x in inputs]
+        + [pltpu.SemaphoreType.DMA((4,))],
         compiler_params=PARAMS,
         name="route",
-    )(expert_ids.T, slots.T, affinity.T, hidden)
+    )(*[in_hbm(x) for x in inputs])
 
 
 def gain_of(block, at, width):
@@ -68,24 +98,30 @@
     return [total[q : q + 1, : min(128, width - 128 * q)] for q in range(tiles)]
 
 
-def units_kernel(me_ref, x_ref, wg_ref, wu_ref, att_ref, *refs):
-    peers = x_ref.shape[0]
-    blocks, (o_ref, n_ref, g_ref, u_ref) = refs[:peers], refs[peers:]
-    half, double = x_ref.shape[1:]
-    rows, cols = 2 * half, double // 2
+def units_kernel(me_ref, wg_hbm, wu_hbm, att_ref, *refs):
+    peers = att_ref.shape[0]
+    blocks, parts = refs[:peers], refs[peers : 2 * peers + 1]
+    o_ref, wg_ref, wu_ref, n_ref, g_ref, u_ref, sems = refs[2 * peers + 1 :]
+    copies = fetch((wg_hbm, wu_hbm), (wg_ref, wu_ref), sems)
+    half, double = parts[0].shape
+    rows, cols, middle = 2 * half, double // 2, peers // 2
     square = jnp.zeros((rows, 1), f32)
-    for j in range(peers):
-        n_ref[:half, :] = x_ref[j, :, :cols]
-        n_ref[half:, :] = x_ref[j, :, cols:]
-        x = n_ref[...].astype(f32)
+    for k in range(peers):
+        at = 0
+        for part in parts[k : k + 1] if k < middle else parts[k : k + 2] if k == middle else parts[k + 1 : k + 2]:
+            end = at + part.shape[0]
+            n_ref[k, at:end, :] = part[:, :cols]
+            n_ref[k, half + at : half + end, :] = part[:, cols:]
+            at = end
+        x = n_ref[k].astype(f32)
         square = square + jnp.sum(x * x, -1, keepdims=True)
     scale = lax.rsqrt(square / D + epsilon)
+    copies[0].wait()
+    copies[1].wait()
     for k in range(peers):
-        j = lax.rem(me_ref[0] + (peers - k), peers)
+        j = behind(me_ref, k, peers)
         gain = jnp.concatenate(gain_of(blocks[k], blocks[k].shape[0] - 16, cols), 1)
-        n_ref[:half, :] = x_ref[j, :, :cols]
-        n_ref[half:, :] = x_ref[j, :, cols:]
-        normed = (n_ref[...].astype(f32) * scale * gain).astype(bf16)
+        normed = (n_ref[k].astype(f32) * scale * gain).astype(bf16)
         part = pl.ds(pl.multiple_of(j * cols, 64), cols)
         gate = jnp.dot(normed, wg_ref[part, :], preferred_element_type=f32)
         up = jnp.dot(normed, wu_ref[part, :], preferred_element_type=f32)
@@ -102,31 +138,37 @@
         o_ref[j, :rows, :] = units
 
 
-def expert_units(me, x, w_gate, w_up, attended, blocks):
-    peers, half, double = x.shape
+def expert_units(me, parts, w_gate, w_up, attended, blocks):
+    peers = len(blocks)
+    half, double = parts[0].shape
     rows, cols, hid = 2 * half, double // 2, w_gate.shape[1]
     return pl.pallas_call(
         units_kernel,
         out_shape=shape((peers, rows + attended.shape[1], hid), bf16),
-        in_specs=[SMEM] + [VMEM] * (4 + peers),
+        in_specs=[SMEM, HBM, HBM] + [VMEM] * (2 * peers + 2),
         out_specs=VMEM,
         scratch_shapes=[
-            pltpu.VMEM((rows, cols), bf16),
+            pltpu.VMEM(w_gate.shape, bf16),
+            pltpu.VMEM(w_up.shape, bf16),
+            pltpu.VMEM((peers, rows, cols), bf16),
             pltpu.VMEM((rows, hid), f32),
             pltpu.VMEM((rows, hid), f32),
+            pltpu.SemaphoreType.DMA((2,)),
         ],
         compiler_params=PARAMS,
         name="units",
-    )(me, x, w_gate, w_up, attended, *blocks)
-
-
-def pack_kernel(me_ref, wd_ref, cache_ref, q_ref, gain_ref, *refs):
-    outs, tiles_ref, keys_ref = refs[:-2], refs[-2], refs[-1]
+    )(me, in_hbm(w_gate), in_hbm(w_up), attended, *blocks, *parts)
+
+
+def pack_kernel(me_ref, wd_hbm, cache_hbm, q_hbm, gain_ref, *refs):
+    outs, (wd_ref, cache_ref, q_ref, tiles_ref, keys_ref, sems) = refs[:-6], refs[-6:]
+    copies = fetch((wd_hbm, cache_hbm, q_hbm), (wd_ref, cache_ref, q_ref), sems)
     peers = len(outs)
     half, double = tiles_ref.shape[1:]
     width = double // 2
     span, heads, keys = cache_ref.shape[1], q_ref.shape[1], cache_ref.shape[2]
     own = cache_ref.shape[0] // peers
+    copies[0].wait()
     for j in range(peers):
         tiles_ref[j, :, :width] = wd_ref[:half, j * width : (j + 1) * width]
         tiles_ref[j, :, width:] = wd_ref[half:, j * width : (j + 1) * width]
@@ -143,8 +185,10 @@
                 piece = jnp.concatenate([piece, jnp.zeros((1, 128 - piece.shape[1]), f32)], 1)
             packed = jnp.where(row == p * tiles + q, piece, packed)
     packed = packed.astype(bf16)
+    copies[1].wait()
+    copies[2].wait()
     for k in range(peers):
-        to = lax.rem(me_ref[0] + k, peers)
+        to = ahead(me_ref, k, peers)
         at = 0
         for t in range(double // 128):
             outs[k][at : at + half, :] = tiles_ref[to, :, 128 * t : 128 * (t + 1)]
@@ -166,36 +210,50 @@
     return pl.pallas_call(
         pack_kernel,
         out_shape=tuple(shape((rows, 128), bf16) for _ in range(peers)),
-        in_specs=[SMEM] + [VMEM] * 4,
+        in_specs=[SMEM] + [HBM] * 3 + [VMEM],
         out_specs=tuple(VMEM for _ in range(peers)),
         scratch_shapes=[
+            pltpu.VMEM(w_down.shape, bf16),
+            pltpu.VMEM(cache.shape, bf16),
+            pltpu.VMEM(queries.shape, bf16),
             pltpu.VMEM((peers, hid // 2, 2 * width), bf16),
             pltpu.VMEM((span + heads, own * keys), bf16),
+            pltpu.SemaphoreType.DMA((3,)),
         ],
         compiler_params=PARAMS,
         name="pack",
-    )(me, w_down, cache, queries, gain)
-
-
-def spread_kernel(x_ref, o_ref):
-    half, double = o_ref.shape[1:]
+    )(me, in_hbm(w_down), in_hbm(cache), in_hbm(queries), gain)
+
+
+def rows_kernel(x_ref, o_ref):
+    half, double = o_ref.shape
     width = double // 2
     x = x_ref[...].reshape(2 * half, width)
-    for j in range(o_ref.shape[0]):
-        o_ref[j, :, :width] = x[:half]
-        o_ref[j, :, width:] = x[half:]
-
-
-def spread_rows(arrived, peers):
+    o_ref[:, :width] = x[:half]
+    o_ref[:, width:] = x[half:]
+
+
+def packed_rows(arrived):
     experts, cap, width = arrived.shape
     return pl.pallas_call(
-        spread_kernel,
-        out_shape=shape((peers, experts * cap // 2, 2 * width), bf16),
+        rows_kernel,
+        out_shape=shape((experts * cap // 2, 2 * width), bf16),
         in_specs=[VMEM],
         out_specs=VMEM,
         compiler_params=PARAMS,
         name="rows",
     )(arrived)
+
+
+def ring(x, moved, peers):
+    steps, half = peers // 2, x.shape[0] // 2
+    there, back = [x], [x]
+    for _ in range(1, steps):
+        there.append(moved(there[-1], 1))
+        back.append(moved(back[-1], peers - 1))
+    upper = moved(there[-1][:half], 1)
+    lower = moved(back[-1][half:], peers - 1)
+    return there + [upper, lower] + back[:0:-1]
 
 
 def down_kernel(me_ref, u_ref, *refs):
@@ -205,7 +263,7 @@
     rows, half = experts * cap, hid // 2
     acc = jnp.zeros((rows, width), f32)
     for k in range(peers):
-        group = lax.rem(me_ref[0] + (peers - k), peers)
+        group = behind(me_ref, k, peers)
         for t in range(2 * width // 128):
             w_ref[:, 128 * t : 128 * (t + 1)] = blocks[k][half * t : half * (t + 1), :]
         units = u_ref[group, :rows, :]
@@ -242,7 +300,7 @@
             c_ref[i, k * span : (k + 1) * span, :] = m_ref[:span, i * keys : (i + 1) * keys]
             q_ref[i, k * heads : (k + 1) * heads, :] = m_ref[span:, i * keys : (i + 1) * keys]
     lane = lax.broadcasted_iota(jnp.int32, (peers * heads, positions), 1)
-    block = lax.rem(me + (peers - lane // span), peers)
+    block = behind(me_ref, lane // span, peers)
     position = block * span + lane % span
     for i in range(own):
         live = position < len_ref[me * own + i]
@@ -396,16 +454,6 @@
     )(everything, gain, cos, sin, queries, units)
 
 
-def mark_kernel(x_ref, o_ref):
-    o_ref[...] = x_ref[...]
-
-
-def mark(x):
-    return pl.pallas_call(
-        mark_kernel, out_shape=shape(x.shape, x.dtype), in_specs=[VMEM], out_specs=VMEM
-    )(x)
-
-
 def rope_tables(lengths, half):
     inv_freq = 10000.0 ** (-jnp.arange(half, dtype=f32) / half)
     angles = lengths.astype(f32)[:, None] * inv_freq[None, :]
@@ -432,26 +480,31 @@
     seqs, width = hidden.shape
     peers = lax.axis_size("tp")
     experts = lax.axis_size("ep") * lax.axis_size("mb")
-    me = lax.axis_index("tp").astype(jnp.int32).reshape(1)
+    cores = lax.axis_size("mb")
+    sense = 1 - 2 * (lax.axis_index("mb") % 2)
+    me = jnp.stack([lax.axis_index("tp"), sense]).astype(jnp.int32)
 
     def moved(x, k):
-        return lax.ppermute(x, "tp", [(i, (i + k) % peers) for i in range(peers)])
+        pairs = [
+            (i * cores + c, (i + (k if c % 2 == 0 else peers - k)) % peers * cores + c)
+            for i in range(peers)
+            for c in range(cores)
+        ]
+        return lax.ppermute(x, ("tp", "mb"), pairs)
 
     send_rows, combine = route(expert_ids, slots, affinity, hidden, experts)
     arrived = exchange(send_rows, ("ep", "mb"))
     blocks = list(pack(me, w_down[0], cache, queries, moe_gain[None], peers))
     for k in MOVES:
         blocks[k] = moved(blocks[k], k)
-    attn_gain = mark(attn_gain[None])
-    rows = spread_rows(arrived, peers)
-    portion = exchange(rows, "tp")
+    parts = ring(packed_rows(arrived), moved, peers)
     span, heads, keys = cache.shape[1], queries.shape[1], queries.shape[2]
     attended = attend(me, lengths, blocks, seqs // peers, span, heads, keys)
-    units = expert_units(me, portion, w_gate[0], w_up[0], attended, blocks)
+    units = expert_units(me, parts, w_gate[0], w_up[0], attended, blocks)
     all_units = exchange(units, "tp")
     output = expert_down(me, all_units, blocks, experts, width)
     returned = exchange(output, ("ep", "mb"))
-    next_hidden, small = close(returned, combine, hidden, attn_gain, w_dkv, peers)
+    next_hidden, small = close(returned, combine, hidden, attn_gain[None], w_dkv, peers)
     everything = exchange(small, "tp")
     cos, sin = rope_tables(lengths, (keys - LAT) // 2)
     latent_out = merge(everything, kv_gain[None], cos, sin, queries, all_units)

time: 230 us -> 213 us (0.926)
  waiting for transfers between devices: 73.8 us -> 35.1 us
  starting transfers between devices: 45.7 us -> 73 us
  local copies, waits for them, and re-layouts: 9.63 us -> 1.41 us
  Pallas kernels: 10.1 us -> 13.8 us
    ppermute x7 -> x15, waiting for transfers between devices: 44.1 us -> 4.21 us  [moved(): return lax.ppermute(x, ('tp', 'mb'), pairs)]
    ppermute x7 -> x15, starting transfers between devices: 29.9 us -> 64.3 us  [moved(): return lax.ppermute(x, ('tp', 'mb'), pairs)]
    unnamed x36 -> x14, local copies, waits for them, and re-layouts: 9.63 us -> 1.38 us
    all_to_all x3 -> x2, starting transfers between devices: 15.8 us -> 8.63 us  [exchange(): return lax.all_to_all(x, axis, split_axis=0, concat_axis=0, tiled=True)]
    all_to_all x3 -> x2, waiting for transfers between devices: 29.6 us -> 30.9 us  [exchange(): return lax.all_to_all(x, axis, split_axis=0, concat_axis=0, tiled=True)]
  transfers between devices with their start and end apart: 10 -> 17, of which waited for: 6 -> 4; matrix products, arithmetic and copies ran while one was open for 0% -> 0% of each run, Pallas kernels for 1% -> 2%
where the time goes in v4:
time: 213 us; the launch traced here: 212 us
  blocking collectives  87.2 us (41%)
  starting transfers between devices  73 us (34%)
  waiting for transfers between devices  35.1 us (16%)
  Pallas kernels  13.8 us (6%)
    all_to_all x2, blocking collectives, exchange(): return lax.all_to_all(x, axis, split_axis=0, concat_axis=0, tiled=True)  87.2 us
    ppermute x15, starting transfers between devices, moved(): return lax.ppermute(x, ('tp', 'mb'), pairs)  64.3 us
    all_to_all x2, waiting for transfers between devices, exchange(): return lax.all_to_all(x, axis, split_axis=0, concat_axis=0, tiled=True)  30.9 us
    all_to_all x2, starting transfers between devices, exchange(): return lax.all_to_all(x, axis, split_axis=0, concat_axis=0, tiled=True)  8.63 us
  transfers between devices with their start and end apart: 17, of which 4 were waited for; matrix products, arithmetic and copies ran while one was open for 0% of the time, Pallas kernels for 2%

profile of v4, /device:TPU:80, one launch (start us, length us, event | category | flops | bytes accessed | tf_op | source)
XLA Modules:
  0.0 211.7 jit_solution(3982190822936282392)
XLA Ops:
  0.6 1.1 route.1
  1.7 66.2 %all_to_all.20.x_ref = bf16[32,8,448]{2,1,0:T(8,128)(2,1)S(1)} all-to-all(bf16[32,8,448]{2,1,0:T(8,128)(2,1)S(1)} %get-tuple-element.22), channel_id=1, replica_groups=mesh['grp'=2,'ep'=16,'tp'=8,'mb'=2] {'ep','mb'}, dimensions={0} | all-to-all | bytes 458752 | tf_op jit(solution)/shard_map/all_to_all | solution.py:30
  67.9 0.1 rows.1.refs_8_
  68.0 3.6 %collective-permute-start.7 = (bf16[128,896]{1,0:T(8,128)(2,1)S(1)}, bf16[128,896]{1,0:T(8,128)(2,1)S(1)}, u32[]{:S(2)}, u32[]{:S(2)}) collective-permute-start(bf16[128,896]{1,0:T(8,128)(2,1)S(1)} %rows.1.refs_8_), channel_id=1, source_target_pairs={{0,2},{1,15},{2,4},{3,1},{4,6},{5,3},{6,8},{7,5},{8,10},{9,7},{10,... | collective-permute-start | bytes 688136 | tf_op jit(solution)/shard_map/ppermute | solution.py:493
  71.6 4.1 %collective-permute-start.11 = (bf16[128,896]{1,0:T(8,128)(2,1)S(1)}, bf16[128,896]{1,0:T(8,128)(2,1)S(1)}, u32[]{:S(2)}, u32[]{:S(2)}) collective-permute-start(bf16[128,896]{1,0:T(8,128)(2,1)S(1)} %rows.1.refs_8_), channel_id=1, source_target_pairs={{0,14},{1,3},{2,0},{3,5},{4,2},{5,7},{6,4},{7,9},{8,6},{9,11},{10,... | collective-permute-start | bytes 688136 | tf_op jit(solution)/shard_map/ppermute | solution.py:493
  75.8 2.0 collective-permute-done.7.refs_9_
  77.8 2.3 %collective-permute-start.8 = (bf16[128,896]{1,0:T(8,128)(2,1)S(1)}, bf16[128,896]{1,0:T(8,128)(2,1)S(1)}, u32[]{:S(2)}, u32[]{:S(2)}) collective-permute-start(bf16[128,896]{1,0:T(8,128)(2,1)S(1)} %collective-permute-done.7.refs_9_), channel_id=1, source_target_pairs={{0,2},{1,15},{2,4},{3,1},{4,6},{5,3},{6,8},{7,5},{8,10},{9,7},{10,... | collective-permute-start | bytes 688136 | tf_op jit(solution)/shard_map/ppermute | solution.py:493
  80.1 0.0 collective-permute-done.11.refs_16_
  80.1 4.8 %collective-permute-start.12 = (bf16[128,896]{1,0:T(8,128)(2,1)S(1)}, bf16[128,896]{1,0:T(8,128)(2,1)S(1)}, u32[]{:S(2)}, u32[]{:S(2)}) collective-permute-start(bf16[128,896]{1,0:T(8,128)(2,1)S(1)} %collective-permute-done.11.refs_16_), channel_id=1, source_target_pairs={{0,14},{1,3},{2,0},{3,5},{4,2},{5,7},{6,4},{7,9},{8,6},{9,11},{10,... | collective-permute-start | bytes 688136 | tf_op jit(solution)/shard_map/ppermute | solution.py:493
  84.9 0.1 pad_add_fusion.me_ref
  85.0 0.7 copy-done.3
  85.7 2.3 %pack.1 = (bf16[680,128]{1,0:T(8,128)(2,1)S(1)}, bf16[680,128]{1,0:T(8,128)(2,1)S(1)}, bf16[680,128]{1,0:T(8,128)(2,1)S(1)}, bf16[680,128]{1,0:T(8,128)(2,1)S(1)...) custom-call(s32[2]{0:T(128)S(1)} %pad_add_fusion.me_ref, ...), custom_call_target="tpu_custom_call" | custom-call | tf_op jit(solution)/shard_map/pack/pallas_call | solution.py:210
  88.0 2.0 collective-permute-start
  90.0 0.0 collective-permute-done.8.refs_10_
  90.0 3.6 %collective-permute-start.9 = (bf16[128,896]{1,0:T(8,128)(2,1)S(1)}, bf16[128,896]{1,0:T(8,128)(2,1)S(1)}, u32[]{:S(2)}, u32[]{:S(2)}) collective-permute-start(bf16[128,896]{1,0:T(8,128)(2,1)S(1)} %collective-permute-done.8.refs_10_), channel_id=1, source_target_pairs={{0,2},{1,15},{2,4},{3,1},{4,6},{5,3},{6,8},{7,5},{8,10},{9,7},{10,... | collective-permute-start | bytes 688136 | tf_op jit(solution)/shard_map/ppermute | solution.py:493
  93.6 0.0 collective-permute-done.12.refs_15_
  93.6 3.5 %collective-permute-start.13 = (bf16[128,896]{1,0:T(8,128)(2,1)S(1)}, bf16[128,896]{1,0:T(8,128)(2,1)S(1)}, u32[]{:S(2)}, u32[]{:S(2)}) collective-permute-start(bf16[128,896]{1,0:T(8,128)(2,1)S(1)} %collective-permute-done.12.refs_15_), channel_id=1, source_target_pairs={{0,14},{1,3},{2,0},{3,5},{4,2},{5,7},{6,4},{7,9},{8,6},{9,11},{10,... | collective-permute-start | bytes 688136 | tf_op jit(solution)/shard_map/ppermute | solution.py:493
  97.1 6.7 %collective-permute-start.1 = (bf16[680,128]{1,0:T(8,128)(2,1)S(1)}, bf16[680,128]{1,0:T(8,128)(2,1)S(1)}, u32[]{:S(2)}, u32[]{:S(2)}) collective-permute-start(bf16[680,128]{1,0:T(8,128)(2,1)S(1)} %get-tuple-element.16), channel_id=1, source_target_pairs={{0,4},{1,13},{2,6},{3,15},{4,8},{5,1},{6,10},{7,3},{8,12},{9,5},{1... | collective-permute-start | bytes 522248 | tf_op jit(solution)/shard_map/ppermute | solution.py:493
  103.8 3.4 %collective-permute-start.2 = (bf16[680,128]{1,0:T(8,128)(2,1)S(1)}, bf16[680,128]{1,0:T(8,128)(2,1)S(1)}, u32[]{:S(2)}, u32[]{:S(2)}) collective-permute-start(bf16[680,128]{1,0:T(8,128)(2,1)S(1)} %get-tuple-element.17), channel_id=1, source_target_pairs={{0,6},{1,11},{2,8},{3,13},{4,10},{5,15},{6,12},{7,1},{8,14},{9,3},... | collective-permute-start | bytes 522248 | tf_op jit(solution)/shard_map/ppermute | solution.py:493
  107.2 0.0 collective-permute-done.refs_1_
  107.2 3.8 %collective-permute-start.3 = (bf16[680,128]{1,0:T(8,128)(2,1)S(1)}, bf16[680,128]{1,0:T(8,128)(2,1)S(1)}, u32[]{:S(2)}, u32[]{:S(2)}) collective-permute-start(bf16[680,128]{1,0:T(8,128)(2,1)S(1)} %get-tuple-element.18), channel_id=1, source_target_pairs={{0,8},{1,9},{2,10},{3,11},{4,12},{5,13},{6,14},{7,15},{8,0},{9,1},... | collective-permute-start | bytes 522248 | tf_op jit(solution)/shard_map/ppermute | solution.py:493
  111.0 0.0 collective-permute-done.1.refs_2_
  111.0 5.8 %collective-permute-start.4 = (bf16[680,128]{1,0:T(8,128)(2,1)S(1)}, bf16[680,128]{1,0:T(8,128)(2,1)S(1)}, u32[]{:S(2)}, u32[]{:S(2)}) collective-permute-start(bf16[680,128]{1,0:T(8,128)(2,1)S(1)} %get-tuple-element.19), channel_id=1, source_target_pairs={{0,10},{1,7},{2,12},{3,9},{4,14},{5,11},{6,0},{7,13},{8,2},{9,15},... | collective-permute-start | bytes 522248 | tf_op jit(solution)/shard_map/ppermute | solution.py:493
  116.8 0.0 collective-permute-done.9.refs_11_
  116.8 11.7 %collective-permute-start.5 = (bf16[680,128]{1,0:T(8,128)(2,1)S(1)}, bf16[680,128]{1,0:T(8,128)(2,1)S(1)}, u32[]{:S(2)}, u32[]{:S(2)}) collective-permute-start(bf16[680,128]{1,0:T(8,128)(2,1)S(1)} %get-tuple-element.20), channel_id=1, source_target_pairs={{0,12},{1,5},{2,14},{3,7},{4,0},{5,9},{6,2},{7,11},{8,4},{9,13},{1... | collective-permute-start | bytes 522248 | tf_op jit(solution)/shard_map/ppermute | solution.py:493
  128.5 0.0 collective-permute-done.13.refs_14_
  128.6 2.0 collective-permute-start.6
  130.6 0.0 copy-start.6
  130.6 4.0 %collective-permute-start.10 = (bf16[64,896]{1,0:T(8,128)(2,1)S(1)}, bf16[64,896]{1,0:T(8,128)(2,1)S(1)}, u32[]{:S(2)}, u32[]{:S(2)}) collective-permute-start(bf16[64,896]{1,0:T(8,128)(2,1)S(1)} %slice.8), channel_id=1, source_target_pairs={{0,2},{1,15},{2,4},{3,1},{4,6},{5,3},{6,8},{7,5},{8,10},{9,7},{10,... | collective-permute-start | bytes 344072 | tf_op jit(solution)/shard_map/ppermute | solution.py:493
  134.5 0.0 collective-permute-done.3.refs_4_
  134.5 3.2 %collective-permute-start.14 = (bf16[64,896]{1,0:T(8,128)(2,1)S(1)}, bf16[64,896]{1,0:T(8,128)(2,1)S(1)}, u32[]{:S(2)}, u32[]{:S(2)}) collective-permute-start(bf16[64,896]{1,0:T(8,128)(2,1)S(1)} %slice.9), channel_id=1, source_target_pairs={{0,14},{1,3},{2,0},{3,5},{4,2},{5,7},{6,4},{7,9},{8,6},{9,11},{10,... | collective-permute-start | bytes 344072 | tf_op jit(solution)/shard_map/ppermute | solution.py:493
  137.7 0.0 collective-permute-done.4.refs_5_
  137.8 1.3 attend.1.att_ref
  139.1 0.0 collective-permute-done.10.refs_12_
  139.1 2.1 %collective-permute-done.14.refs_13_ = bf16[64,896]{1,0:T(8,128)(2,1)S(1)} collective-permute-done((bf16[64,896]{1,0:T(8,128)(2,1)S(1)}, bf16[64,896]{1,0:T(8,128)(2,1)S(1)}, u32[]{:S(2)}, u32[]{:S(2)}) %collective-permute-start.14) | collective-permute-done | bytes 114720 | tf_op jit(solution)/shard_map/ppermute | solution.py:493
  141.3 4.2 %units.1 = bf16[8,336,128]{2,1,0:T(8,128)(2,1)S(1)} custom-call(s32[2]{0:T(128)S(1)} %pad_add_fusion.me_ref, bf16[3584,128]{1,0:T(8,128)(2,1)} %bitcast.15, bf16[3584,128]{1,0:T(8,128)(2,1)} %bitcast.16, bf16[8,80,128]{2,1,0:T(8,128)(2,1)S(1)} %attend.1.att_ref, bf16[680,128]{1,0:T(8,128)(2,1)S(1)} %get-tuple-element.14.refs_0_, ...), custom_call_target="tpu_custom_call" | custom-call | tf_op jit(solution)/shard_map/units/pallas_call | solution.py:145
  145.5 20.9 %all_to_all.21.u_ref.units_ref = bf16[8,336,128]{2,1,0:T(8,128)(2,1)S(1)} all-to-all(bf16[8,336,128]{2,1,0:T(8,128)(2,1)S(1)} %units.1), channel_id=1, replica_groups=mesh['grp'=2,'ep'=16,'tp'=8,'mb'=2] {'tp'}, dimensions={0} | all-to-all | bytes 1376256 | tf_op jit(solution)/shard_map/all_to_all | solution.py:30
  166.4 2.6 %down.1 = bf16[32,8,448]{2,1,0:T(8,128)(2,1)} custom-call(s32[2]{0:T(128)S(1)} %pad_add_fusion.me_ref, bf16[8,336,128]{2,1,0:T(8,128)(2,1)S(1)} %all_to_all.21.u_ref.units_ref, bf16[680,128]{1,0:T(8,128)(2,1)S(1)} %get-tuple-element.14.refs_0_, bf16[680,128]{1,0:T(8,128)(2,1)S(1)} %collective-permute-done.refs_1_, ...), custom_call_target="tpu_custom_call" | custom-call | tf_op jit(solution)/shard_map/down/pallas_call | solution.py:277
  169.1 4.9 %all-to-all-start.2 = ((bf16[32,8,448]{2,1,0:T(8,128)(2,1)}), bf16[32,8,448]{2,1,0:T(8,128)(2,1)S(1)}, u32[]{:S(2)}, u32[]{:S(2)}) async-start(bf16[32,8,448]{2,1,0:T(8,128)(2,1)} %down.1), calls=%async_computation.2 | async-start | bytes 524288 | tf_op jit(solution)/shard_map/all_to_all | solution.py:30
  174.0 0.0 copy-start.4
  174.0 21.9 %all-to-all-done.2.ret_ref = bf16[32,8,448]{2,1,0:T(8,128)(2,1)S(1)} async-done(((bf16[32,8,448]{2,1,0:T(8,128)(2,1)}), bf16[32,8,448]{2,1,0:T(8,128)(2,1)S(1)}, u32[]{:S(2)}, u32[]{:S(2)}) %all-to-all-start.2) | async-done | bytes 229408 | tf_op jit(solution)/shard_map/all_to_all | solution.py:30
  195.9 1.1 close.1
  197.0 3.7 %all-to-all-start.3 = ((bf16[8,16,640]{2,1,0:T(8,128)(2,1)}), bf16[8,16,640]{2,1,0:T(8,128)(2,1)S(1)}, u32[]{:S(2)}, u32[]{:S(2)}) async-start(bf16[8,16,640]{2,1,0:T(8,128)(2,1)} %get-tuple-element.25), calls=%async_computation.3 | async-start | bytes 327680 | tf_op jit(solution)/shard_map/all_to_all | solution.py:30
  200.7 0.1 fusion
  200.9 0.1 pad_maximum_fusion
  200.9 9.0 %all-to-all-done.3.all_ref = bf16[8,16,640]{2,1,0:T(8,128)(2,1)S(1)} async-done(((bf16[8,16,640]{2,1,0:T(8,128)(2,1)}), bf16[8,16,640]{2,1,0:T(8,128)(2,1)S(1)}, u32[]{:S(2)}, u32[]{:S(2)}) %all-to-all-start.3) | async-done | bytes 163872 | tf_op jit(solution)/shard_map/all_to_all | solution.py:30
  209.9 0.7 copy-done.5
  210.6 1.1 merge.1
  (17 shorter events, 0.1 us)
Async XLA Ops:
  68.0 9.8 %collective-permute-start.7 = (bf16[128,896]{1,0:T(8,128)(2,1)S(1)}, bf16[128,896]{1,0:T(8,128)(2,1)S(1)}, u32[]{:S(2)}, u32[]{:S(2)}) collective-permute-start(bf16[128,896]{1,0:T(8,128)(2,1)S(1)} %rows.1.refs_8_), channel_id=1, source_target_pairs={{0,2},{1,15},{2,4},{3,1},{4,6},{5,3},{6,8},{7,5},{8,10},{9,7},{10,... | collective-permute-start | bytes 688136 | tf_op jit(solution)/shard_map/ppermute | solution.py:493
  71.6 8.5 %collective-permute-start.11 = (bf16[128,896]{1,0:T(8,128)(2,1)S(1)}, bf16[128,896]{1,0:T(8,128)(2,1)S(1)}, u32[]{:S(2)}, u32[]{:S(2)}) collective-permute-start(bf16[128,896]{1,0:T(8,128)(2,1)S(1)} %rows.1.refs_8_), channel_id=1, source_target_pairs={{0,14},{1,3},{2,0},{3,5},{4,2},{5,7},{6,4},{7,9},{8,6},{9,11},{10,... | collective-permute-start | bytes 688136 | tf_op jit(solution)/shard_map/ppermute | solution.py:493
  77.8 12.2 %collective-permute-start.8 = (bf16[128,896]{1,0:T(8,128)(2,1)S(1)}, bf16[128,896]{1,0:T(8,128)(2,1)S(1)}, u32[]{:S(2)}, u32[]{:S(2)}) collective-permute-start(bf16[128,896]{1,0:T(8,128)(2,1)S(1)} %collective-permute-done.7.refs_9_), channel_id=1, source_target_pairs={{0,2},{1,15},{2,4},{3,1},{4,6},{5,3},{6,8},{7,5},{8,10},{9,7},{10,... | collective-permute-start | bytes 688136 | tf_op jit(solution)/shard_map/ppermute | solution.py:493
  80.1 13.4 %collective-permute-start.12 = (bf16[128,896]{1,0:T(8,128)(2,1)S(1)}, bf16[128,896]{1,0:T(8,128)(2,1)S(1)}, u32[]{:S(2)}, u32[]{:S(2)}) collective-permute-start(bf16[128,896]{1,0:T(8,128)(2,1)S(1)} %collective-permute-done.11.refs_16_), channel_id=1, source_target_pairs={{0,14},{1,3},{2,0},{3,5},{4,2},{5,7},{6,4},{7,9},{8,6},{9,11},{10,... | collective-permute-start | bytes 688136 | tf_op jit(solution)/shard_map/ppermute | solution.py:493
  85.0 0.7 copy-start.3
  88.0 19.2 %collective-permute-start = (bf16[680,128]{1,0:T(8,128)(2,1)S(1)}, bf16[680,128]{1,0:T(8,128)(2,1)S(1)}, u32[]{:S(2)}, u32[]{:S(2)}) collective-permute-start(bf16[680,128]{1,0:T(8,128)(2,1)S(1)} %get-tuple-element.15), channel_id=1, source_target_pairs={{0,2},{1,15},{2,4},{3,1},{4,6},{5,3},{6,8},{7,5},{8,10},{9,7},{10,... | collective-permute-start | bytes 522248 | tf_op jit(solution)/shard_map/ppermute | solution.py:493
  90.0 26.9 %collective-permute-start.9 = (bf16[128,896]{1,0:T(8,128)(2,1)S(1)}, bf16[128,896]{1,0:T(8,128)(2,1)S(1)}, u32[]{:S(2)}, u32[]{:S(2)}) collective-permute-start(bf16[128,896]{1,0:T(8,128)(2,1)S(1)} %collective-permute-done.8.refs_10_), channel_id=1, source_target_pairs={{0,2},{1,15},{2,4},{3,1},{4,6},{5,3},{6,8},{7,5},{8,10},{9,7},{10,... | collective-permute-start | bytes 688136 | tf_op jit(solution)/shard_map/ppermute | solution.py:493
  93.6 35.0 %collective-permute-start.13 = (bf16[128,896]{1,0:T(8,128)(2,1)S(1)}, bf16[128,896]{1,0:T(8,128)(2,1)S(1)}, u32[]{:S(2)}, u32[]{:S(2)}) collective-permute-start(bf16[128,896]{1,0:T(8,128)(2,1)S(1)} %collective-permute-done.12.refs_15_), channel_id=1, source_target_pairs={{0,14},{1,3},{2,0},{3,5},{4,2},{5,7},{6,4},{7,9},{8,6},{9,11},{10,... | collective-permute-start | bytes 688136 | tf_op jit(solution)/shard_map/ppermute | solution.py:493
  97.1 13.9 %collective-permute-start.1 = (bf16[680,128]{1,0:T(8,128)(2,1)S(1)}, bf16[680,128]{1,0:T(8,128)(2,1)S(1)}, u32[]{:S(2)}, u32[]{:S(2)}) collective-permute-start(bf16[680,128]{1,0:T(8,128)(2,1)S(1)} %get-tuple-element.16), channel_id=1, source_target_pairs={{0,4},{1,13},{2,6},{3,15},{4,8},{5,1},{6,10},{7,3},{8,12},{9,5},{1... | collective-permute-start | bytes 522248 | tf_op jit(solution)/shard_map/ppermute | solution.py:493
  103.8 26.8 %collective-permute-start.2 = (bf16[680,128]{1,0:T(8,128)(2,1)S(1)}, bf16[680,128]{1,0:T(8,128)(2,1)S(1)}, u32[]{:S(2)}, u32[]{:S(2)}) collective-permute-start(bf16[680,128]{1,0:T(8,128)(2,1)S(1)} %get-tuple-element.17), channel_id=1, source_target_pairs={{0,6},{1,11},{2,8},{3,13},{4,10},{5,15},{6,12},{7,1},{8,14},{9,3},... | collective-permute-start | bytes 522248 | tf_op jit(solution)/shard_map/ppermute | solution.py:493
  107.2 27.3 %collective-permute-start.3 = (bf16[680,128]{1,0:T(8,128)(2,1)S(1)}, bf16[680,128]{1,0:T(8,128)(2,1)S(1)}, u32[]{:S(2)}, u32[]{:S(2)}) collective-permute-start(bf16[680,128]{1,0:T(8,128)(2,1)S(1)} %get-tuple-element.18), channel_id=1, source_target_pairs={{0,8},{1,9},{2,10},{3,11},{4,12},{5,13},{6,14},{7,15},{8,0},{9,1},... | collective-permute-start | bytes 522248 | tf_op jit(solution)/shard_map/ppermute | solution.py:493
  111.0 26.7 %collective-permute-start.4 = (bf16[680,128]{1,0:T(8,128)(2,1)S(1)}, bf16[680,128]{1,0:T(8,128)(2,1)S(1)}, u32[]{:S(2)}, u32[]{:S(2)}) collective-permute-start(bf16[680,128]{1,0:T(8,128)(2,1)S(1)} %get-tuple-element.19), channel_id=1, source_target_pairs={{0,10},{1,7},{2,12},{3,9},{4,14},{5,11},{6,0},{7,13},{8,2},{9,15},... | collective-permute-start | bytes 522248 | tf_op jit(solution)/shard_map/ppermute | solution.py:493
  116.8 20.9 %collective-permute-start.5 = (bf16[680,128]{1,0:T(8,128)(2,1)S(1)}, bf16[680,128]{1,0:T(8,128)(2,1)S(1)}, u32[]{:S(2)}, u32[]{:S(2)}) collective-permute-start(bf16[680,128]{1,0:T(8,128)(2,1)S(1)} %get-tuple-element.20), channel_id=1, source_target_pairs={{0,12},{1,5},{2,14},{3,7},{4,0},{5,9},{6,2},{7,11},{8,4},{9,13},{1... | collective-permute-start | bytes 522248 | tf_op jit(solution)/shard_map/ppermute | solution.py:493
  128.6 9.2 %collective-permute-start.6 = (bf16[680,128]{1,0:T(8,128)(2,1)S(1)}, bf16[680,128]{1,0:T(8,128)(2,1)S(1)}, u32[]{:S(2)}, u32[]{:S(2)}) collective-permute-start(bf16[680,128]{1,0:T(8,128)(2,1)S(1)} %get-tuple-element.21), channel_id=1, source_target_pairs={{0,14},{1,3},{2,0},{3,5},{4,2},{5,7},{6,4},{7,9},{8,6},{9,11},{10,... | collective-permute-start | bytes 522248 | tf_op jit(solution)/shard_map/ppermute | solution.py:493
  130.6 7.2 %copy-start.6 = (s32[16]{0:T(128)S(1)}, s32[16]{0:T(128)}, u32[]{:S(2)}) copy-start(s32[16]{0:T(128)} %len_ref.1) | copy-start | bytes 196
  130.6 8.5 %collective-permute-start.10 = (bf16[64,896]{1,0:T(8,128)(2,1)S(1)}, bf16[64,896]{1,0:T(8,128)(2,1)S(1)}, u32[]{:S(2)}, u32[]{:S(2)}) collective-permute-start(bf16[64,896]{1,0:T(8,128)(2,1)S(1)} %slice.8), channel_id=1, source_target_pairs={{0,2},{1,15},{2,4},{3,1},{4,6},{5,3},{6,8},{7,5},{8,10},{9,7},{10,... | collective-permute-start | bytes 344072 | tf_op jit(solution)/shard_map/ppermute | solution.py:493
  134.5 6.7 %collective-permute-start.14 = (bf16[64,896]{1,0:T(8,128)(2,1)S(1)}, bf16[64,896]{1,0:T(8,128)(2,1)S(1)}, u32[]{:S(2)}, u32[]{:S(2)}) collective-permute-start(bf16[64,896]{1,0:T(8,128)(2,1)S(1)} %slice.9), channel_id=1, source_target_pairs={{0,14},{1,3},{2,0},{3,5},{4,2},{5,7},{6,4},{7,9},{8,6},{9,11},{10,... | collective-permute-start | bytes 344072 | tf_op jit(solution)/shard_map/ppermute | solution.py:493
  166.4 29.5 %copy-start.1 = (bf16[448,576]{1,0:T(8,128)(2,1)S(1)}, bf16[448,576]{1,0:T(8,128)(2,1)}, u32[]{:S(2)}) copy-start(bf16[448,576]{1,0:T(8,128)(2,1)} %wdkv_ref.1) | copy-start | bytes 1548292
  169.1 26.9 %copy-start.2 = (bf16[16,448]{1,0:T(8,128)(2,1)S(1)}, bf16[16,448]{1,0:T(8,128)(2,1)}, u32[]{:S(2)}) copy-start(bf16[16,448]{1,0:T(8,128)(2,1)} %hid_ref.1) | copy-start | bytes 43012
  169.1 26.9 %all-to-all-start.2 = ((bf16[32,8,448]{2,1,0:T(8,128)(2,1)}), bf16[32,8,448]{2,1,0:T(8,128)(2,1)S(1)}, u32[]{:S(2)}, u32[]{:S(2)}) async-start(bf16[32,8,448]{2,1,0:T(8,128)(2,1)} %down.1), calls=%async_computation.2 | async-start | bytes 524288 | tf_op jit(solution)/shard_map/all_to_all | solution.py:30
  174.0 21.9 %copy-start.4 = (f32[448]{0:T(512)S(1)}, f32[448]{0:T(512)}, u32[]{:S(2)}) copy-start(f32[448]{0:T(512)} %param.22) | copy-start | bytes 5380
  197.0 12.9 %copy-start = (bf16[16,8,576]{2,1,0:T(8,128)(2,1)S(1)}, bf16[16,8,576]{2,1,0:T(8,128)(2,1)}, u32[]{:S(2)}) copy-start(bf16[16,8,576]{2,1,0:T(8,128)(2,1)} %q_ref.1) | copy-start | bytes 442372
  197.0 12.9 %all-to-all-start.3 = ((bf16[8,16,640]{2,1,0:T(8,128)(2,1)}), bf16[8,16,640]{2,1,0:T(8,128)(2,1)S(1)}, u32[]{:S(2)}, u32[]{:S(2)}) async-start(bf16[8,16,640]{2,1,0:T(8,128)(2,1)} %get-tuple-element.25), calls=%async_computation.3 | async-start | bytes 327680 | tf_op jit(solution)/shard_map/all_to_all | solution.py:30
  209.9 0.7 copy-start.5

commit v5 on v4

--- a/solution.py
+++ b/solution.py
@@ -9,7 +9,9 @@
 D = 3584
 LAT = 512
 CAP = 8
-MOVES = (4, 3, 5, 2, 6, 1, 7)
+EARLY = (4, 3, 5, 2)
+LATE = (6, 1, 7)
+GAIN_ROWS = 8
 
 epsilon = 1e-06
 route_scale = 2.5
@@ -28,14 +30,6 @@
 
 def exchange(x, axis):
     return lax.all_to_all(x, axis, split_axis=0, concat_axis=0, tiled=True)
-
-
-def ahead(me_ref, k, peers):
-    return lax.rem(me_ref[0] + me_ref[1] * k + peers, peers)
-
-
-def behind(me_ref, k, peers):
-    return lax.rem(me_ref[0] - me_ref[1] * k + peers, peers)
 
 
 def in_hbm(x):
@@ -91,27 +85,23 @@
     )(*[in_hbm(x) for x in inputs])
 
 
-def gain_of(block, at, width):
-    rows = block[at : at + 16, :].astype(f32)
-    tiles = (width + 127) // 128
-    total = rows[:tiles] + rows[tiles : 2 * tiles] + rows[2 * tiles : 3 * tiles]
-    return [total[q : q + 1, : min(128, width - 128 * q)] for q in range(tiles)]
-
-
-def units_kernel(me_ref, wg_hbm, wu_hbm, att_ref, *refs):
-    peers = att_ref.shape[0]
-    blocks, parts = refs[:peers], refs[peers : 2 * peers + 1]
-    o_ref, wg_ref, wu_ref, n_ref, g_ref, u_ref, sems = refs[2 * peers + 1 :]
+def units_kernel(me_ref, wg_hbm, wu_hbm, *refs):
+    parts = refs[:-7]
+    o_ref, wg_ref, wu_ref, n_ref, g_ref, u_ref, sems = refs[-7:]
     copies = fetch((wg_hbm, wu_hbm), (wg_ref, wu_ref), sems)
-    half, double = parts[0].shape
-    rows, cols, middle = 2 * half, double // 2, peers // 2
+    peers, rows, cols = n_ref.shape
+    half, middle = rows // 2, peers // 2
     square = jnp.zeros((rows, 1), f32)
+    gains = []
     for k in range(peers):
+        first = k if k <= middle else k + 1
         at = 0
-        for part in parts[k : k + 1] if k < middle else parts[k : k + 2] if k == middle else parts[k + 1 : k + 2]:
-            end = at + part.shape[0]
-            n_ref[k, at:end, :] = part[:, :cols]
-            n_ref[k, half + at : half + end, :] = part[:, cols:]
+        for part in parts[first : first + (2 if k == middle else 1)]:
+            end = min(at + part.shape[0], half)
+            n_ref[k, at:end, :] = part[: end - at, :cols]
+            n_ref[k, half + at : half + end, :] = part[: end - at, cols:]
+            if at + part.shape[0] > half:
+                gains.append(jnp.sum(part[end - at :, :cols].astype(f32), 0, keepdims=True))
             at = end
         x = n_ref[k].astype(f32)
         square = square + jnp.sum(x * x, -1, keepdims=True)
@@ -119,9 +109,8 @@
     copies[0].wait()
     copies[1].wait()
     for k in range(peers):
-        j = behind(me_ref, k, peers)
-        gain = jnp.concatenate(gain_of(blocks[k], blocks[k].shape[0] - 16, cols), 1)
-        normed = (n_ref[k].astype(f32) * scale * gain).astype(bf16)
+        j = lax.rem(me_ref[0] + (peers - k), peers)
+        normed = (n_ref[k].astype(f32) * scale * gains[k]).astype(bf16)
         part = pl.ds(pl.multiple_of(j * cols, 64), cols)
         gate = jnp.dot(normed, wg_ref[part, :], preferred_element_type=f32)
         up = jnp.dot(normed, wu_ref[part, :], preferred_element_type=f32)
@@ -131,21 +120,19 @@
         else:
             g_ref[...] += gate
             u_ref[...] += up
-        o_ref[j, rows:, :] = att_ref[k]
     gate = g_ref[...]
     units = (gate / (1.0 + jnp.exp(-gate)) * u_ref[...]).astype(bf16)
     for j in range(peers):
-        o_ref[j, :rows, :] = units
-
-
-def expert_units(me, parts, w_gate, w_up, attended, blocks):
-    peers = len(blocks)
-    half, double = parts[0].shape
-    rows, cols, hid = 2 * half, double // 2, w_gate.shape[1]
+        o_ref[j] = units
+
+
+def expert_units(me, parts, w_gate, w_up, peers):
+    half, cols, hid = parts[0].shape[0] - GAIN_ROWS, parts[0].shape[1] // 2, w_gate.shape[1]
+    rows = 2 * half
     return pl.pallas_call(
         units_kernel,
-        out_shape=shape((peers, rows + attended.shape[1], hid), bf16),
-        in_specs=[SMEM, HBM, HBM] + [VMEM] * (2 * peers + 2),
+        out_shape=shape((peers, rows, hid), bf16),
+        in_specs=[SMEM, HBM, HBM] + [VMEM] * len(parts),
         out_specs=VMEM,
         scratch_shapes=[
             pltpu.VMEM(w_gate.shape, bf16),
@@ -157,10 +144,10 @@
         ],
         compiler_params=PARAMS,
         name="units",
-    )(me, in_hbm(w_gate), in_hbm(w_up), attended, *blocks, *parts)
-
-
-def pack_kernel(me_ref, wd_hbm, cache_hbm, q_hbm, gain_ref, *refs):
+    )(me, in_hbm(w_gate), in_hbm(w_up), *parts)
+
+
+def pack_kernel(me_ref, wd_hbm, cache_hbm, q_hbm, *refs):
     outs, (wd_ref, cache_ref, q_ref, tiles_ref, keys_ref, sems) = refs[:-6], refs[-6:]
     copies = fetch((wd_hbm, cache_hbm, q_hbm), (wd_ref, cache_ref, q_ref), sems)
     peers = len(outs)
@@ -172,23 +159,10 @@
     for j in range(peers):
         tiles_ref[j, :, :width] = wd_ref[:half, j * width : (j + 1) * width]
         tiles_ref[j, :, width:] = wd_ref[half:, j * width : (j + 1) * width]
-    gain = gain_ref[...]
-    first = gain.astype(bf16).astype(f32)
-    second = (gain - first).astype(bf16).astype(f32)
-    row = lax.broadcasted_iota(jnp.int32, (16, 128), 0)
-    packed = jnp.zeros((16, 128), f32)
-    tiles = (width + 127) // 128
-    for p, value in enumerate((first, second, gain - first - second)):
-        for q in range(tiles):
-            piece = value[:, 128 * q : min(128 * (q + 1), width)]
-            if piece.shape[1] < 128:
-                piece = jnp.concatenate([piece, jnp.zeros((1, 128 - piece.shape[1]), f32)], 1)
-            packed = jnp.where(row == p * tiles + q, piece, packed)
-    packed = packed.astype(bf16)
     copies[1].wait()
     copies[2].wait()
     for k in range(peers):
-        to = ahead(me_ref, k, peers)
+        to = lax.rem(me_ref[0] + k, peers)
         at = 0
         for t in range(double // 128):
             outs[k][at : at + half, :] = tiles_ref[to, :, 128 * t : 128 * (t + 1)]
@@ -199,18 +173,17 @@
         for t in range(own * keys // 128):
             outs[k][at : at + span + heads, :] = keys_ref[:, 128 * t : 128 * (t + 1)]
             at += span + heads
-        outs[k][at : at + 16, :] = packed
-
-
-def pack(me, w_down, cache, queries, gain, peers):
+
+
+def pack(me, w_down, cache, queries, peers):
     hid, width = w_down.shape[0], w_down.shape[1] // peers
     seqs, span, keys = cache.shape
     own, heads = seqs // peers, queries.shape[1]
-    rows = hid * width // 128 + own * (span + heads) * keys // 128 + 16
+    rows = hid * width // 128 + own * (span + heads) * keys // 128
     return pl.pallas_call(
         pack_kernel,
         out_shape=tuple(shape((rows, 128), bf16) for _ in range(peers)),
-        in_specs=[SMEM] + [HBM] * 3 + [VMEM],
+        in_specs=[SMEM] + [HBM] * 3,
         out_specs=tuple(VMEM for _ in range(peers)),
         scratch_shapes=[
             pltpu.VMEM(w_down.shape, bf16),
@@ -222,37 +195,46 @@
         ],
         compiler_params=PARAMS,
         name="pack",
-    )(me, in_hbm(w_down), in_hbm(cache), in_hbm(queries), gain)
-
-
-def rows_kernel(x_ref, o_ref):
-    half, double = o_ref.shape
-    width = double // 2
+    )(me, in_hbm(w_down), in_hbm(cache), in_hbm(queries))
+
+
+def rows_kernel(x_ref, gain_ref, o_ref):
+    half, width = o_ref.shape[0] - GAIN_ROWS, o_ref.shape[1] // 2
     x = x_ref[...].reshape(2 * half, width)
-    o_ref[:, :width] = x[:half]
-    o_ref[:, width:] = x[half:]
-
-
-def packed_rows(arrived):
+    o_ref[:half, :width] = x[:half]
+    o_ref[:half, width:] = x[half:]
+    gain = gain_ref[...]
+    first = gain.astype(bf16).astype(f32)
+    second = (gain - first).astype(bf16).astype(f32)
+    third = gain - first - second
+    row = lax.broadcasted_iota(jnp.int32, (GAIN_ROWS, width), 0)
+    parts = jnp.where(
+        row == 0, first, jnp.where(row == 1, second, jnp.where(row == 2, third, 0.0))
+    ).astype(bf16)
+    o_ref[half:, :width] = parts
+    o_ref[half:, width:] = parts
+
+
+def packed_rows(arrived, gain):
     experts, cap, width = arrived.shape
     return pl.pallas_call(
         rows_kernel,
-        out_shape=shape((experts * cap // 2, 2 * width), bf16),
-        in_specs=[VMEM],
+        out_shape=shape((experts * cap // 2 + GAIN_ROWS, 2 * width), bf16),
+        in_specs=[VMEM] * 2,
         out_specs=VMEM,
         compiler_params=PARAMS,
         name="rows",
-    )(arrived)
+    )(arrived, gain)
 
 
 def ring(x, moved, peers):
-    steps, half = peers // 2, x.shape[0] // 2
+    steps, cut = peers // 2, (x.shape[0] // 2 + 7) // 8 * 8
     there, back = [x], [x]
     for _ in range(1, steps):
         there.append(moved(there[-1], 1))
         back.append(moved(back[-1], peers - 1))
-    upper = moved(there[-1][:half], 1)
-    lower = moved(back[-1][half:], peers - 1)
+    upper = moved(there[-1][:cut], 1)
+    lower = moved(back[-1][cut:], peers - 1)
     return there + [upper, lower] + back[:0:-1]
 
 
@@ -263,7 +245,7 @@
     rows, half = experts * cap, hid // 2
     acc = jnp.zeros((rows, width), f32)
     for k in range(peers):
-        group = behind(me_ref, k, peers)
+        group = lax.rem(me_ref[0] + (peers - k), peers)
         for t in range(2 * width // 128):
             w_ref[:, 128 * t : 128 * (t + 1)] = blocks[k][half * t : half * (t + 1), :]
         units = u_ref[group, :rows, :]
@@ -291,7 +273,7 @@
     own, positions, keys = c_ref.shape
     span, heads = positions // peers, q_ref.shape[1] // peers
     me = me_ref[0]
-    first = blocks[0].shape[0] - 16 - own * keys // 128 * (span + heads)
+    first = blocks[0].shape[0] - own * keys // 128 * (span + heads)
     for k in range(peers):
         for t in range(own * keys // 128):
             at = first + t * (span + heads)
@@ -300,7 +282,7 @@
             c_ref[i, k * span : (k + 1) * span, :] = m_ref[:span, i * keys : (i + 1) * keys]
             q_ref[i, k * heads : (k + 1) * heads, :] = m_ref[span:, i * keys : (i + 1) * keys]
     lane = lax.broadcasted_iota(jnp.int32, (peers * heads, positions), 1)
-    block = behind(me_ref, lane // span, peers)
+    block = lax.rem(me + (peers - lane // span), peers)
     position = block * span + lane % span
     for i in range(own):
         live = position < len_ref[me * own + i]
@@ -328,17 +310,15 @@
             jnp.where(tail_lane == 1, middle, jnp.where(tail_lane == 2, low, 0.0)),
         ).astype(bf16)
         for k in range(peers):
-            for t in range(LAT // 128 + 1):
-                at = (t * own + i) * heads
-                piece = tail if t == LAT // 128 else out[:, 128 * t : 128 * (t + 1)]
-                o_ref[k, at : at + heads, :] = piece[k * heads : (k + 1) * heads]
+            o_ref[k, i * heads : (i + 1) * heads, :LAT] = out[k * heads : (k + 1) * heads]
+            o_ref[k, i * heads : (i + 1) * heads, LAT:] = tail[k * heads : (k + 1) * heads]
 
 
 def attend(me, lengths, blocks, own, span, heads, keys):
     peers = len(blocks)
     return pl.pallas_call(
         attend_kernel,
-        out_shape=shape((peers, own * heads * (LAT // 128 + 1), 128), bf16),
+        out_shape=shape((peers, own * heads, LAT + 128), bf16),
         in_specs=[SMEM, SMEM] + [VMEM] * peers,
         out_specs=VMEM,
         scratch_shapes=[
@@ -351,7 +331,9 @@
     )(me, lengths, *blocks)
 
 
-def close_kernel(ret_ref, comb_ref, hid_ref, gain_ref, wdkv_ref, next_ref, small_ref):
+def close_kernel(
+    me_ref, ret_ref, comb_ref, hid_ref, gain_ref, wdkv_ref, att_ref, next_ref, small_ref
+):
     rows = comb_ref.shape[0]
     keys = wdkv_ref.shape[1]
     returned = ret_ref[...].reshape(rows, ret_ref.shape[-1])
@@ -376,42 +358,41 @@
     down = jnp.dot(
         (wide * gain_ref[...]).astype(bf16), wdkv_ref[...], preferred_element_type=f32
     ).astype(bf16)
-    for j in range(small_ref.shape[0]):
-        small_ref[j, :, :keys] = down
-        small_ref[j, :, keys:] = tail
-
-
-def close(returned, combine, hidden, gain, w_dkv, peers):
+    tokens, peers = wide.shape[0], small_ref.shape[0]
+    for j in range(peers):
+        small_ref[j, :tokens, :keys] = down
+        small_ref[j, :tokens, keys:] = tail
+        small_ref[lax.rem(me_ref[0] + (peers - j), peers), tokens:, :] = att_ref[j]
+
+
+def close(me, returned, combine, hidden, gain, w_dkv, attended):
     tokens, width = hidden.shape
+    peers, extra, lanes = attended.shape
     return pl.pallas_call(
         close_kernel,
         out_shape=(
             shape((tokens, width), bf16),
-            shape((peers, tokens, w_dkv.shape[1] + 64), bf16),
+            shape((peers, tokens + extra, lanes), bf16),
         ),
-        in_specs=[VMEM] * 5,
+        in_specs=[SMEM] + [VMEM] * 6,
         out_specs=(VMEM, VMEM),
         compiler_params=PARAMS,
         name="close",
-    )(returned, combine, hidden, gain, w_dkv)
-
-
-def merge_kernel(all_ref, gain_ref, cos_ref, sin_ref, q_ref, units_ref, o_ref, back_ref):
+    )(me, returned, combine, hidden, gain, w_dkv, attended)
+
+
+def merge_kernel(all_ref, gain_ref, cos_ref, sin_ref, q_ref, o_ref, back_ref):
     peers = all_ref.shape[0]
-    seqs, heads, lanes = back_ref.shape
+    seqs, heads, _ = back_ref.shape
     own = seqs // peers
-    first = units_ref.shape[1] - own * heads * (lanes // 128)
     for j in range(peers):
         for i in range(own):
-            for t in range(lanes // 128):
-                at = first + (t * own + i) * heads
-                back_ref[j * own + i, :, 128 * t : 128 * (t + 1)] = units_ref[
-                    j, at : at + heads, :
-                ]
+            at = seqs + i * heads
+            back_ref[j * own + i] = all_ref[j, at : at + heads, :]
     keys = q_ref.shape[-1]
-    total = all_ref[0].astype(f32)
-    for j in range(1, all_ref.shape[0]):
-        total = total + all_ref[j].astype(f32)
+    total = all_ref[0, :seqs, :].astype(f32)
+    for j in range(1, peers):
+        total = total + all_ref[j, :seqs, :].astype(f32)
     square = jnp.sum(total[:, keys:], -1, keepdims=True)
     down = total[:, :keys] * lax.rsqrt(square / D + epsilon)
     latent = down[:, :LAT]
@@ -441,17 +422,17 @@
     ).astype(bf16)
 
 
-def merge(everything, gain, cos, sin, queries, units):
+def merge(everything, gain, cos, sin, queries):
     seqs, heads, _ = queries.shape
     return pl.pallas_call(
         merge_kernel,
         out_shape=shape((seqs, heads, LAT), bf16),
-        in_specs=[VMEM] * 6,
+        in_specs=[VMEM] * 5,
         out_specs=VMEM,
         scratch_shapes=[pltpu.VMEM((seqs, heads, LAT + 128), bf16)],
         compiler_params=PARAMS,
         name="merge",
-    )(everything, gain, cos, sin, queries, units)
+    )(everything, gain, cos, sin, queries)
 
 
 def rope_tables(lengths, half):
@@ -480,34 +461,29 @@
     seqs, width = hidden.shape
     peers = lax.axis_size("tp")
     experts = lax.axis_size("ep") * lax.axis_size("mb")
-    cores = lax.axis_size("mb")
-    sense = 1 - 2 * (lax.axis_index("mb") % 2)
-    me = jnp.stack([lax.axis_index("tp"), sense]).astype(jnp.int32)
+    me = lax.axis_index("tp").astype(jnp.int32).reshape(1)
 
     def moved(x, k):
-        pairs = [
-            (i * cores + c, (i + (k if c % 2 == 0 else peers - k)) % peers * cores + c)
-            for i in range(peers)
-            for c in range(cores)
-        ]
-        return lax.ppermute(x, ("tp", "mb"), pairs)
+        return lax.ppermute(x, "tp", [(i, (i + k) % peers) for i in range(peers)])
 
     send_rows, combine = route(expert_ids, slots, affinity, hidden, experts)
     arrived = exchange(send_rows, ("ep", "mb"))
-    blocks = list(pack(me, w_down[0], cache, queries, moe_gain[None], peers))
-    for k in MOVES:
+    blocks = list(pack(me, w_down[0], cache, queries, peers))
+    for k in EARLY + LATE:
         blocks[k] = moved(blocks[k], k)
-    parts = ring(packed_rows(arrived), moved, peers)
+    parts = ring(packed_rows(arrived, moe_gain[None]), moved, peers)
     span, heads, keys = cache.shape[1], queries.shape[1], queries.shape[2]
     attended = attend(me, lengths, blocks, seqs // peers, span, heads, keys)
-    units = expert_units(me, parts, w_gate[0], w_up[0], attended, blocks)
+    units = expert_units(me, parts, w_gate[0], w_up[0], peers)
     all_units = exchange(units, "tp")
     output = expert_down(me, all_units, blocks, experts, width)
     returned = exchange(output, ("ep", "mb"))
-    next_hidden, small = close(returned, combine, hidden, attn_gain[None], w_dkv, peers)
+    next_hidden, small = close(
+        me, returned, combine, hidden, attn_gain[None], w_dkv, attended
+    )
     everything = exchange(small, "tp")
     cos, sin = rope_tables(lengths, (keys - LAT) // 2)
-    latent_out = merge(everything, kv_gain[None], cos, sin, queries, all_units)
+    latent_out = merge(everything, kv_gain[None], cos, sin, queries)
     return (next_hidden, latent_out)
 
 

time: 213 us -> 218 us (1.023)
  waiting for transfers between devices: 35.1 us -> 60.2 us
  blocking collectives: 87.2 us -> 66.2 us
  starting transfers between devices: 73 us -> 75.7 us
    ppermute x15, waiting for transfers between devices: 4.21 us -> 26.4 us  [moved(): return lax.ppermute(x, 'tp', [(i, (i + k) % peers) for i in range(peers)])]
    all_to_all x2 -> x1, blocking collectives: 87.2 us -> 66.2 us  [exchange(): return lax.all_to_all(x, axis, split_axis=0, concat_axis=0, tiled=True)]
    all_to_all x2 -> x3, starting transfers between devices: 8.63 us -> 17.4 us  [exchange(): return lax.all_to_all(x, axis, split_axis=0, concat_axis=0, tiled=True)]
    ppermute x15, starting transfers between devices: 64.3 us -> 58.3 us  [moved(): return lax.ppermute(x, 'tp', [(i, (i + k) % peers) for i in range(peers)])]
    all_to_all x2 -> x3, waiting for transfers between devices: 30.9 us -> 33.8 us  [exchange(): return lax.all_to_all(x, axis, split_axis=0, concat_axis=0, tiled=True)]
  transfers between devices with their start and end apart: 17 -> 18, of which waited for: 4 -> 11; matrix products, arithmetic and copies ran while one was open for 0% -> 0% of each run, Pallas kernels for 2% -> 1%
where the time goes in v5:
time: 218 us; the launch traced here: 217 us
  starting transfers between devices  75.7 us (35%)
  blocking collectives  66.2 us (30%)
  waiting for transfers between devices  60.2 us (28%)
  Pallas kernels  13.1 us (6%)
    all_to_all x1, blocking collectives, exchange(): return lax.all_to_all(x, axis, split_axis=0, concat_axis=0, tiled=True)  66.2 us
    ppermute x15, starting transfers between devices, moved(): return lax.ppermute(x, 'tp', [(i, (i + k) % peers) for i in range(peers)])  58.3 us
    all_to_all x3, waiting for transfers between devices, exchange(): return lax.all_to_all(x, axis, split_axis=0, concat_axis=0, tiled=True)  33.8 us
    ppermute x15, waiting for transfers between devices, moved(): return lax.ppermute(x, 'tp', [(i, (i + k) % peers) for i in range(peers)])  26.4 us
    all_to_all x3, starting transfers between devices, exchange(): return lax.all_to_all(x, axis, split_axis=0, concat_axis=0, tiled=True)  17.4 us
    pallas_call x1, Pallas kernels, expert_units(): pl.pallas_call(units_kernel, out_shape=shape((peers, rows, hid), bf16), i...  4.58 us
  transfers between devices with their start and end apart: 18, of which 11 were waited for; matrix products, arithmetic and copies ran while one was open for 0% of the time, Pallas kernels for 1%

profile of v5, /device:TPU:80, one launch (start us, length us, event | category | flops | bytes accessed | tf_op | source)
XLA Modules:
  0.0 217.1 jit_solution(13736436320778977676)
XLA Ops:
  0.6 1.1 route.1
  1.7 0.0 copy-start.3
  1.7 66.2 %all_to_all.20.x_ref = bf16[32,8,448]{2,1,0:T(8,128)(2,1)S(1)} all-to-all(bf16[32,8,448]{2,1,0:T(8,128)(2,1)S(1)} %get-tuple-element.14), channel_id=1, replica_groups=mesh['grp'=2,'ep'=16,'tp'=8,'mb'=2] {'ep','mb'}, dimensions={0} | all-to-all | bytes 458752 | tf_op jit(solution)/shard_map/all_to_all | solution.py:32
  68.0 0.1 rows.1.refs_0_
  68.1 3.6 %collective-permute-start = (bf16[136,896]{1,0:T(8,128)(2,1)S(1)}, bf16[136,896]{1,0:T(8,128)(2,1)S(1)}, u32[]{:S(2)}, u32[]{:S(2)}) collective-permute-start(bf16[136,896]{1,0:T(8,128)(2,1)S(1)} %rows.1.refs_0_), channel_id=1, source_target_pairs={{0,2},{2,4},{4,6},{6,8},{8,10},{10,12},{12,14},{14,0},{1,3},{3,5},... | collective-permute-start | bytes 731144 | tf_op jit(solution)/shard_map/ppermute | solution.py:467
  71.6 4.1 %collective-permute-start.4 = (bf16[136,896]{1,0:T(8,128)(2,1)S(1)}, bf16[136,896]{1,0:T(8,128)(2,1)S(1)}, u32[]{:S(2)}, u32[]{:S(2)}) collective-permute-start(bf16[136,896]{1,0:T(8,128)(2,1)S(1)} %rows.1.refs_0_), channel_id=1, source_target_pairs={{0,14},{2,0},{4,2},{6,4},{8,6},{10,8},{12,10},{14,12},{1,15},{3,1}... | collective-permute-start | bytes 731144 | tf_op jit(solution)/shard_map/ppermute | solution.py:467
  75.8 4.0 %collective-permute-done.refs_1_ = bf16[136,896]{1,0:T(8,128)(2,1)S(1)} collective-permute-done((bf16[136,896]{1,0:T(8,128)(2,1)S(1)}, bf16[136,896]{1,0:T(8,128)(2,1)S(1)}, u32[]{:S(2)}, u32[]{:S(2)}) %collective-permute-start) | collective-permute-done | bytes 243744 | tf_op jit(solution)/shard_map/ppermute | solution.py:467
  79.8 1.9 collective-permute-start.1
  81.8 0.0 collective-permute-done.4.refs_8_
  81.8 5.2 %collective-permute-start.5 = (bf16[136,896]{1,0:T(8,128)(2,1)S(1)}, bf16[136,896]{1,0:T(8,128)(2,1)S(1)}, u32[]{:S(2)}, u32[]{:S(2)}) collective-permute-start(bf16[136,896]{1,0:T(8,128)(2,1)S(1)} %collective-permute-done.4.refs_8_), channel_id=1, source_target_pairs={{0,14},{2,0},{4,2},{6,4},{8,6},{10,8},{12,10},{14,12},{1,15},{3,1}... | collective-permute-start | bytes 731144 | tf_op jit(solution)/shard_map/ppermute | solution.py:467
  86.9 3.2 %collective-permute-done.1.refs_2_ = bf16[136,896]{1,0:T(8,128)(2,1)S(1)} collective-permute-done((bf16[136,896]{1,0:T(8,128)(2,1)S(1)}, bf16[136,896]{1,0:T(8,128)(2,1)S(1)}, u32[]{:S(2)}, u32[]{:S(2)}) %collective-permute-start.1) | collective-permute-done | bytes 243744 | tf_op jit(solution)/shard_map/ppermute | solution.py:467
  90.1 1.9 collective-permute-start.2
  92.0 0.0 collective-permute-done.5.refs_7_
  92.1 5.2 %collective-permute-start.6 = (bf16[136,896]{1,0:T(8,128)(2,1)S(1)}, bf16[136,896]{1,0:T(8,128)(2,1)S(1)}, u32[]{:S(2)}, u32[]{:S(2)}) collective-permute-start(bf16[136,896]{1,0:T(8,128)(2,1)S(1)} %collective-permute-done.5.refs_7_), channel_id=1, source_target_pairs={{0,14},{2,0},{4,2},{6,4},{8,6},{10,8},{12,10},{14,12},{1,15},{3,1}... | collective-permute-start | bytes 731144 | tf_op jit(solution)/shard_map/ppermute | solution.py:467
  97.2 2.3 %collective-permute-done.2.refs_3_ = bf16[136,896]{1,0:T(8,128)(2,1)S(1)} collective-permute-done((bf16[136,896]{1,0:T(8,128)(2,1)S(1)}, bf16[136,896]{1,0:T(8,128)(2,1)S(1)}, u32[]{:S(2)}, u32[]{:S(2)}) %collective-permute-start.2) | collective-permute-done | bytes 243744 | tf_op jit(solution)/shard_map/ppermute | solution.py:467
  99.5 2.0 collective-permute-start.3
  101.5 0.0 collective-permute-done.6.refs_6_
  101.5 5.2 %collective-permute-start.7 = (bf16[64,896]{1,0:T(8,128)(2,1)S(1)}, bf16[64,896]{1,0:T(8,128)(2,1)S(1)}, u32[]{:S(2)}, u32[]{:S(2)}) collective-permute-start(bf16[64,896]{1,0:T(8,128)(2,1)S(1)} %slice.9), channel_id=1, source_target_pairs={{0,14},{2,0},{4,2},{6,4},{8,6},{10,8},{12,10},{14,12},{1,15},{3,1}... | collective-permute-start | bytes 344072 | tf_op jit(solution)/shard_map/ppermute | solution.py:467
  106.7 2.3 %collective-permute-done.7.refs_5_ = bf16[64,896]{1,0:T(8,128)(2,1)S(1)} collective-permute-done((bf16[64,896]{1,0:T(8,128)(2,1)S(1)}, bf16[64,896]{1,0:T(8,128)(2,1)S(1)}, u32[]{:S(2)}, u32[]{:S(2)}) %collective-permute-start.7) | collective-permute-done | bytes 114720 | tf_op jit(solution)/shard_map/ppermute | solution.py:467
  109.0 4.6 %units.1 = bf16[8,256,128]{2,1,0:T(8,128)(2,1)} custom-call(s32[1]{0:T(128)} %bitcast.me_ref, bf16[3584,128]{1,0:T(8,128)(2,1)} %bitcast.13, bf16[3584,128]{1,0:T(8,128)(2,1)} %bitcast.14, bf16[136,896]{1,0:T(8,128)(2,1)S(1)} %rows.1.refs_0_, bf16[136,896]{1,0:T(8,128)(2,1)S(1)} %collective-permute-done.refs_1_, ...), custom_call_target="tpu_custom_call" | custom-call | tf_op jit(solution)/shard_map/units/pallas_call | solution.py:132
  113.6 7.0 %all-to-all-start.1 = ((bf16[8,256,128]{2,1,0:T(8,128)(2,1)}), bf16[8,256,128]{2,1,0:T(8,128)(2,1)S(1)}, u32[]{:S(2)}, u32[]{:S(2)}) async-start(bf16[8,256,128]{2,1,0:T(8,128)(2,1)} %units.1), calls=%async_computation.1 | async-start | bytes 1048576 | tf_op jit(solution)/shard_map/all_to_all | solution.py:32
  120.6 1.7 pack.1
  122.4 4.0 %collective-permute-start.8 = (bf16[664,128]{1,0:T(8,128)(2,1)S(1)}, bf16[664,128]{1,0:T(8,128)(2,1)S(1)}, u32[]{:S(2)}, u32[]{:S(2)}) collective-permute-start(bf16[664,128]{1,0:T(8,128)(2,1)S(1)} %get-tuple-element.16), channel_id=1, source_target_pairs={{0,2},{2,4},{4,6},{6,8},{8,10},{10,12},{12,14},{14,0},{1,3},{3,5},... | collective-permute-start | bytes 509960 | tf_op jit(solution)/shard_map/ppermute | solution.py:467
  126.4 4.3 %collective-permute-start.9 = (bf16[664,128]{1,0:T(8,128)(2,1)S(1)}, bf16[664,128]{1,0:T(8,128)(2,1)S(1)}, u32[]{:S(2)}, u32[]{:S(2)}) collective-permute-start(bf16[664,128]{1,0:T(8,128)(2,1)S(1)} %get-tuple-element.17), channel_id=1, source_target_pairs={{0,4},{2,6},{4,8},{6,10},{8,12},{10,14},{12,0},{14,2},{1,5},{3,7},... | collective-permute-start | bytes 509960 | tf_op jit(solution)/shard_map/ppermute | solution.py:467
  130.7 4.6 %collective-permute-start.10 = (bf16[664,128]{1,0:T(8,128)(2,1)S(1)}, bf16[664,128]{1,0:T(8,128)(2,1)S(1)}, u32[]{:S(2)}, u32[]{:S(2)}) collective-permute-start(bf16[664,128]{1,0:T(8,128)(2,1)S(1)} %get-tuple-element.18), channel_id=1, source_target_pairs={{0,6},{2,8},{4,10},{6,12},{8,14},{10,0},{12,2},{14,4},{1,7},{3,9},... | collective-permute-start | bytes 509960 | tf_op jit(solution)/shard_map/ppermute | solution.py:467
  135.3 4.3 %collective-permute-start.11 = (bf16[664,128]{1,0:T(8,128)(2,1)S(1)}, bf16[664,128]{1,0:T(8,128)(2,1)S(1)}, u32[]{:S(2)}, u32[]{:S(2)}) collective-permute-start(bf16[664,128]{1,0:T(8,128)(2,1)S(1)} %get-tuple-element.19), channel_id=1, source_target_pairs={{0,8},{2,10},{4,12},{6,14},{8,0},{10,2},{12,4},{14,6},{1,9},{3,11}... | collective-permute-start | bytes 509960 | tf_op jit(solution)/shard_map/ppermute | solution.py:467
  139.6 4.6 %collective-permute-start.12 = (bf16[664,128]{1,0:T(8,128)(2,1)S(1)}, bf16[664,128]{1,0:T(8,128)(2,1)S(1)}, u32[]{:S(2)}, u32[]{:S(2)}) collective-permute-start(bf16[664,128]{1,0:T(8,128)(2,1)S(1)} %get-tuple-element.20), channel_id=1, source_target_pairs={{0,10},{2,12},{4,14},{6,0},{8,2},{10,4},{12,6},{14,8},{1,11},{3,13... | collective-permute-start | bytes 509960 | tf_op jit(solution)/shard_map/ppermute | solution.py:467
  144.2 5.5 %collective-permute-start.13 = (bf16[664,128]{1,0:T(8,128)(2,1)S(1)}, bf16[664,128]{1,0:T(8,128)(2,1)S(1)}, u32[]{:S(2)}, u32[]{:S(2)}) collective-permute-start(bf16[664,128]{1,0:T(8,128)(2,1)S(1)} %get-tuple-element.21), channel_id=1, source_target_pairs={{0,12},{2,14},{4,0},{6,2},{8,4},{10,6},{12,8},{14,10},{1,13},{3,15... | collective-permute-start | bytes 509960 | tf_op jit(solution)/shard_map/ppermute | solution.py:467
  149.7 2.2 %collective-permute-done.9.refs_2_ = bf16[664,128]{1,0:T(8,128)(2,1)S(1)} collective-permute-done((bf16[664,128]{1,0:T(8,128)(2,1)S(1)}, bf16[664,128]{1,0:T(8,128)(2,1)S(1)}, u32[]{:S(2)}, u32[]{:S(2)}) %collective-permute-start.9) | collective-permute-done | bytes 170016 | tf_op jit(solution)/shard_map/ppermute | solution.py:467
  152.0 1.9 collective-permute-start.14
  153.9 3.1 %collective-permute-done.10.refs_3_ = bf16[664,128]{1,0:T(8,128)(2,1)S(1)} collective-permute-done((bf16[664,128]{1,0:T(8,128)(2,1)S(1)}, bf16[664,128]{1,0:T(8,128)(2,1)S(1)}, u32[]{:S(2)}, u32[]{:S(2)}) %collective-permute-start.10) | collective-permute-done | bytes 170016 | tf_op jit(solution)/shard_map/ppermute | solution.py:467
  157.0 4.8 %collective-permute-done.11.refs_4_ = bf16[664,128]{1,0:T(8,128)(2,1)S(1)} collective-permute-done((bf16[664,128]{1,0:T(8,128)(2,1)S(1)}, bf16[664,128]{1,0:T(8,128)(2,1)S(1)}, u32[]{:S(2)}, u32[]{:S(2)}) %collective-permute-start.11) | collective-permute-done | bytes 170016 | tf_op jit(solution)/shard_map/ppermute | solution.py:467
  161.8 1.2 collective-permute-done.13.refs_6_
  162.9 3.4 %collective-permute-done.14.refs_7_ = bf16[664,128]{1,0:T(8,128)(2,1)S(1)} collective-permute-done((bf16[664,128]{1,0:T(8,128)(2,1)S(1)}, bf16[664,128]{1,0:T(8,128)(2,1)S(1)}, u32[]{:S(2)}, u32[]{:S(2)}) %collective-permute-start.14) | collective-permute-done | bytes 170016 | tf_op jit(solution)/shard_map/ppermute | solution.py:467
  166.3 2.1 down.1
  168.4 6.3 %all-to-all-start.2 = ((bf16[32,8,448]{2,1,0:T(8,128)(2,1)}), bf16[32,8,448]{2,1,0:T(8,128)(2,1)S(1)}, u32[]{:S(2)}, u32[]{:S(2)}) async-start(bf16[32,8,448]{2,1,0:T(8,128)(2,1)} %down.1), calls=%async_computation.2 | async-start | bytes 524288 | tf_op jit(solution)/shard_map/all_to_all | solution.py:32
  174.6 0.0 copy-start.1
  174.7 0.0 copy-start.2
  174.7 1.3 attend.1.att_ref
  176.0 0.0 copy-start.4
  176.0 20.6 %all-to-all-done.2.ret_ref = bf16[32,8,448]{2,1,0:T(8,128)(2,1)S(1)} async-done(((bf16[32,8,448]{2,1,0:T(8,128)(2,1)}), bf16[32,8,448]{2,1,0:T(8,128)(2,1)S(1)}, u32[]{:S(2)}, u32[]{:S(2)}) %all-to-all-start.2) | async-done | bytes 229408 | tf_op jit(solution)/shard_map/all_to_all | solution.py:32
  196.6 1.1 close.1
  197.8 4.1 %all-to-all-start.3 = ((bf16[8,32,640]{2,1,0:T(8,128)(2,1)}), bf16[8,32,640]{2,1,0:T(8,128)(2,1)S(1)}, u32[]{:S(2)}, u32[]{:S(2)}) async-start(bf16[8,32,640]{2,1,0:T(8,128)(2,1)} %get-tuple-element.25), calls=%async_computation.3 | async-start | bytes 655360 | tf_op jit(solution)/shard_map/all_to_all | solution.py:32
  201.9 0.1 fusion
  202.0 0.1 pad_maximum_fusion
  202.1 13.1 %all-to-all-done.3.all_ref = bf16[8,32,640]{2,1,0:T(8,128)(2,1)S(1)} async-done(((bf16[8,32,640]{2,1,0:T(8,128)(2,1)}), bf16[8,32,640]{2,1,0:T(8,128)(2,1)S(1)}, u32[]{:S(2)}, u32[]{:S(2)}) %all-to-all-start.3) | async-done | bytes 327712 | tf_op jit(solution)/shard_map/all_to_all | solution.py:32
  215.3 0.7 copy-done.5
  215.9 1.1 merge.1
  (17 shorter events, 0.1 us)
Async XLA Ops:
  1.7 66.3 %copy-start.3 = (f32[448]{0:T(512)S(1)}, f32[448]{0:T(512)}, u32[]{:S(2)}) copy-start(f32[448]{0:T(512)} %param.15) | copy-start | bytes 5380
  68.1 11.7 %collective-permute-start = (bf16[136,896]{1,0:T(8,128)(2,1)S(1)}, bf16[136,896]{1,0:T(8,128)(2,1)S(1)}, u32[]{:S(2)}, u32[]{:S(2)}) collective-permute-start(bf16[136,896]{1,0:T(8,128)(2,1)S(1)} %rows.1.refs_0_), channel_id=1, source_target_pairs={{0,2},{2,4},{4,6},{6,8},{8,10},{10,12},{12,14},{14,0},{1,3},{3,5},... | collective-permute-start | bytes 731144 | tf_op jit(solution)/shard_map/ppermute | solution.py:467
  71.6 10.1 %collective-permute-start.4 = (bf16[136,896]{1,0:T(8,128)(2,1)S(1)}, bf16[136,896]{1,0:T(8,128)(2,1)S(1)}, u32[]{:S(2)}, u32[]{:S(2)}) collective-permute-start(bf16[136,896]{1,0:T(8,128)(2,1)S(1)} %rows.1.refs_0_), channel_id=1, source_target_pairs={{0,14},{2,0},{4,2},{6,4},{8,6},{10,8},{12,10},{14,12},{1,15},{3,1}... | collective-permute-start | bytes 731144 | tf_op jit(solution)/shard_map/ppermute | solution.py:467
  79.8 10.3 %collective-permute-start.1 = (bf16[136,896]{1,0:T(8,128)(2,1)S(1)}, bf16[136,896]{1,0:T(8,128)(2,1)S(1)}, u32[]{:S(2)}, u32[]{:S(2)}) collective-permute-start(bf16[136,896]{1,0:T(8,128)(2,1)S(1)} %collective-permute-done.refs_1_), channel_id=1, source_target_pairs={{0,2},{2,4},{4,6},{6,8},{8,10},{10,12},{12,14},{14,0},{1,3},{3,5},... | collective-permute-start | bytes 731144 | tf_op jit(solution)/shard_map/ppermute | solution.py:467
  81.8 10.3 %collective-permute-start.5 = (bf16[136,896]{1,0:T(8,128)(2,1)S(1)}, bf16[136,896]{1,0:T(8,128)(2,1)S(1)}, u32[]{:S(2)}, u32[]{:S(2)}) collective-permute-start(bf16[136,896]{1,0:T(8,128)(2,1)S(1)} %collective-permute-done.4.refs_8_), channel_id=1, source_target_pairs={{0,14},{2,0},{4,2},{6,4},{8,6},{10,8},{12,10},{14,12},{1,15},{3,1}... | collective-permute-start | bytes 731144 | tf_op jit(solution)/shard_map/ppermute | solution.py:467
  90.1 9.4 %collective-permute-start.2 = (bf16[136,896]{1,0:T(8,128)(2,1)S(1)}, bf16[136,896]{1,0:T(8,128)(2,1)S(1)}, u32[]{:S(2)}, u32[]{:S(2)}) collective-permute-start(bf16[136,896]{1,0:T(8,128)(2,1)S(1)} %collective-permute-done.1.refs_2_), channel_id=1, source_target_pairs={{0,2},{2,4},{4,6},{6,8},{8,10},{10,12},{12,14},{14,0},{1,3},{3,5},... | collective-permute-start | bytes 731144 | tf_op jit(solution)/shard_map/ppermute | solution.py:467
  92.1 9.4 %collective-permute-start.6 = (bf16[136,896]{1,0:T(8,128)(2,1)S(1)}, bf16[136,896]{1,0:T(8,128)(2,1)S(1)}, u32[]{:S(2)}, u32[]{:S(2)}) collective-permute-start(bf16[136,896]{1,0:T(8,128)(2,1)S(1)} %collective-permute-done.5.refs_7_), channel_id=1, source_target_pairs={{0,14},{2,0},{4,2},{6,4},{8,6},{10,8},{12,10},{14,12},{1,15},{3,1}... | collective-permute-start | bytes 731144 | tf_op jit(solution)/shard_map/ppermute | solution.py:467
  99.5 9.5 %collective-permute-start.3 = (bf16[72,896]{1,0:T(8,128)(2,1)S(1)}, bf16[72,896]{1,0:T(8,128)(2,1)S(1)}, u32[]{:S(2)}, u32[]{:S(2)}) collective-permute-start(bf16[72,896]{1,0:T(8,128)(2,1)S(1)} %slice.8), channel_id=1, source_target_pairs={{0,2},{2,4},{4,6},{6,8},{8,10},{10,12},{12,14},{14,0},{1,3},{3,5},... | collective-permute-start | bytes 387080 | tf_op jit(solution)/shard_map/ppermute | solution.py:467
  101.5 7.5 %collective-permute-start.7 = (bf16[64,896]{1,0:T(8,128)(2,1)S(1)}, bf16[64,896]{1,0:T(8,128)(2,1)S(1)}, u32[]{:S(2)}, u32[]{:S(2)}) collective-permute-start(bf16[64,896]{1,0:T(8,128)(2,1)S(1)} %slice.9), channel_id=1, source_target_pairs={{0,14},{2,0},{4,2},{6,4},{8,6},{10,8},{12,10},{14,12},{1,15},{3,1}... | collective-permute-start | bytes 344072 | tf_op jit(solution)/shard_map/ppermute | solution.py:467
  113.6 52.6 %all-to-all-start.1 = ((bf16[8,256,128]{2,1,0:T(8,128)(2,1)}), bf16[8,256,128]{2,1,0:T(8,128)(2,1)S(1)}, u32[]{:S(2)}, u32[]{:S(2)}) async-start(bf16[8,256,128]{2,1,0:T(8,128)(2,1)} %units.1), calls=%async_computation.1 | async-start | bytes 1048576 | tf_op jit(solution)/shard_map/all_to_all | solution.py:32
  122.4 21.8 %collective-permute-start.8 = (bf16[664,128]{1,0:T(8,128)(2,1)S(1)}, bf16[664,128]{1,0:T(8,128)(2,1)S(1)}, u32[]{:S(2)}, u32[]{:S(2)}) collective-permute-start(bf16[664,128]{1,0:T(8,128)(2,1)S(1)} %get-tuple-element.16), channel_id=1, source_target_pairs={{0,2},{2,4},{4,6},{6,8},{8,10},{10,12},{12,14},{14,0},{1,3},{3,5},... | collective-permute-start | bytes 509960 | tf_op jit(solution)/shard_map/ppermute | solution.py:467
  126.4 25.6 %collective-permute-start.9 = (bf16[664,128]{1,0:T(8,128)(2,1)S(1)}, bf16[664,128]{1,0:T(8,128)(2,1)S(1)}, u32[]{:S(2)}, u32[]{:S(2)}) collective-permute-start(bf16[664,128]{1,0:T(8,128)(2,1)S(1)} %get-tuple-element.17), channel_id=1, source_target_pairs={{0,4},{2,6},{4,8},{6,10},{8,12},{10,14},{12,0},{14,2},{1,5},{3,7},... | collective-permute-start | bytes 509960 | tf_op jit(solution)/shard_map/ppermute | solution.py:467
  130.7 26.3 %collective-permute-start.10 = (bf16[664,128]{1,0:T(8,128)(2,1)S(1)}, bf16[664,128]{1,0:T(8,128)(2,1)S(1)}, u32[]{:S(2)}, u32[]{:S(2)}) collective-permute-start(bf16[664,128]{1,0:T(8,128)(2,1)S(1)} %get-tuple-element.18), channel_id=1, source_target_pairs={{0,6},{2,8},{4,10},{6,12},{8,14},{10,0},{12,2},{14,4},{1,7},{3,9},... | collective-permute-start | bytes 509960 | tf_op jit(solution)/shard_map/ppermute | solution.py:467
  135.3 26.5 %collective-permute-start.11 = (bf16[664,128]{1,0:T(8,128)(2,1)S(1)}, bf16[664,128]{1,0:T(8,128)(2,1)S(1)}, u32[]{:S(2)}, u32[]{:S(2)}) collective-permute-start(bf16[664,128]{1,0:T(8,128)(2,1)S(1)} %get-tuple-element.19), channel_id=1, source_target_pairs={{0,8},{2,10},{4,12},{6,14},{8,0},{10,2},{12,4},{14,6},{1,9},{3,11}... | collective-permute-start | bytes 509960 | tf_op jit(solution)/shard_map/ppermute | solution.py:467
  139.6 22.2 %collective-permute-start.12 = (bf16[664,128]{1,0:T(8,128)(2,1)S(1)}, bf16[664,128]{1,0:T(8,128)(2,1)S(1)}, u32[]{:S(2)}, u32[]{:S(2)}) collective-permute-start(bf16[664,128]{1,0:T(8,128)(2,1)S(1)} %get-tuple-element.20), channel_id=1, source_target_pairs={{0,10},{2,12},{4,14},{6,0},{8,2},{10,4},{12,6},{14,8},{1,11},{3,13... | collective-permute-start | bytes 509960 | tf_op jit(solution)/shard_map/ppermute | solution.py:467
  144.2 18.7 %collective-permute-start.13 = (bf16[664,128]{1,0:T(8,128)(2,1)S(1)}, bf16[664,128]{1,0:T(8,128)(2,1)S(1)}, u32[]{:S(2)}, u32[]{:S(2)}) collective-permute-start(bf16[664,128]{1,0:T(8,128)(2,1)S(1)} %get-tuple-element.21), channel_id=1, source_target_pairs={{0,12},{2,14},{4,0},{6,2},{8,4},{10,6},{12,8},{14,10},{1,13},{3,15... | collective-permute-start | bytes 509960 | tf_op jit(solution)/shard_map/ppermute | solution.py:467
  152.0 14.3 %collective-permute-start.14 = (bf16[664,128]{1,0:T(8,128)(2,1)S(1)}, bf16[664,128]{1,0:T(8,128)(2,1)S(1)}, u32[]{:S(2)}, u32[]{:S(2)}) collective-permute-start(bf16[664,128]{1,0:T(8,128)(2,1)S(1)} %get-tuple-element.22), channel_id=1, source_target_pairs={{0,14},{2,0},{4,2},{6,4},{8,6},{10,8},{12,10},{14,12},{1,15},{3,1}... | collective-permute-start | bytes 509960 | tf_op jit(solution)/shard_map/ppermute | solution.py:467
  168.4 6.3 %copy-start.6 = (s32[16]{0:T(128)S(1)}, s32[16]{0:T(128)}, u32[]{:S(2)}) copy-start(s32[16]{0:T(128)} %len_ref.1) | copy-start | bytes 196
  168.4 28.3 %all-to-all-start.2 = ((bf16[32,8,448]{2,1,0:T(8,128)(2,1)}), bf16[32,8,448]{2,1,0:T(8,128)(2,1)S(1)}, u32[]{:S(2)}, u32[]{:S(2)}) async-start(bf16[32,8,448]{2,1,0:T(8,128)(2,1)} %down.1), calls=%async_computation.2 | async-start | bytes 524288 | tf_op jit(solution)/shard_map/all_to_all | solution.py:32
  174.6 22.0 %copy-start.1 = (bf16[448,576]{1,0:T(8,128)(2,1)S(1)}, bf16[448,576]{1,0:T(8,128)(2,1)}, u32[]{:S(2)}) copy-start(bf16[448,576]{1,0:T(8,128)(2,1)} %wdkv_ref.1) | copy-start | bytes 1548292
  174.7 22.0 %copy-start.2 = (bf16[16,448]{1,0:T(8,128)(2,1)S(1)}, bf16[16,448]{1,0:T(8,128)(2,1)}, u32[]{:S(2)}) copy-start(bf16[16,448]{1,0:T(8,128)(2,1)} %hid_ref.1) | copy-start | bytes 43012
  176.0 20.6 %copy-start.4 = (f32[448]{0:T(512)S(1)}, f32[448]{0:T(512)}, u32[]{:S(2)}) copy-start(f32[448]{0:T(512)} %param.22) | copy-start | bytes 5380
  197.8 17.5 %copy-start = (bf16[16,8,576]{2,1,0:T(8,128)(2,1)S(1)}, bf16[16,8,576]{2,1,0:T(8,128)(2,1)}, u32[]{:S(2)}) copy-start(bf16[16,8,576]{2,1,0:T(8,128)(2,1)} %q_ref.1) | copy-start | bytes 442372
  197.8 17.5 %all-to-all-start.3 = ((bf16[8,32,640]{2,1,0:T(8,128)(2,1)}), bf16[8,32,640]{2,1,0:T(8,128)(2,1)S(1)}, u32[]{:S(2)}, u32[]{:S(2)}) async-start(bf16[8,32,640]{2,1,0:T(8,128)(2,1)} %get-tuple-element.25), calls=%async_computation.3 | async-start | bytes 655360 | tf_op jit(solution)/shard_map/all_to_all | solution.py:32
  215.3 0.7 copy-start.5

commit v6 on v4

--- a/solution.py
+++ b/solution.py
@@ -9,7 +9,8 @@
 D = 3584
 LAT = 512
 CAP = 8
-MOVES = (4, 3, 5, 2, 6, 1, 7)
+BEFORE = (4, 3, 5)
+MOVES = BEFORE + (2, 6, 1, 7)
 
 epsilon = 1e-06
 route_scale = 2.5
@@ -28,14 +29,6 @@
 
 def exchange(x, axis):
     return lax.all_to_all(x, axis, split_axis=0, concat_axis=0, tiled=True)
-
-
-def ahead(me_ref, k, peers):
-    return lax.rem(me_ref[0] + me_ref[1] * k + peers, peers)
-
-
-def behind(me_ref, k, peers):
-    return lax.rem(me_ref[0] - me_ref[1] * k + peers, peers)
 
 
 def in_hbm(x):
@@ -119,7 +112,7 @@
     copies[0].wait()
     copies[1].wait()
     for k in range(peers):
-        j = behind(me_ref, k, peers)
+        j = lax.rem(me_ref[0] + (peers - k), peers)
         gain = jnp.concatenate(gain_of(blocks[k], blocks[k].shape[0] - 16, cols), 1)
         normed = (n_ref[k].astype(f32) * scale * gain).astype(bf16)
         part = pl.ds(pl.multiple_of(j * cols, 64), cols)
@@ -160,9 +153,11 @@
     )(me, in_hbm(w_gate), in_hbm(w_up), attended, *blocks, *parts)
 
 
-def pack_kernel(me_ref, wd_hbm, cache_hbm, q_hbm, gain_ref, *refs):
-    outs, (wd_ref, cache_ref, q_ref, tiles_ref, keys_ref, sems) = refs[:-6], refs[-6:]
-    copies = fetch((wd_hbm, cache_hbm, q_hbm), (wd_ref, cache_ref, q_ref), sems)
+def pack_kernel(me_ref, wd_hbm, cache_hbm, q_hbm, gain_hbm, *refs):
+    outs, (wd_ref, cache_ref, q_ref, gain_ref, tiles_ref, keys_ref, sems) = refs[:-7], refs[-7:]
+    copies = fetch(
+        (wd_hbm, cache_hbm, q_hbm, gain_hbm), (wd_ref, cache_ref, q_ref, gain_ref), sems
+    )
     peers = len(outs)
     half, double = tiles_ref.shape[1:]
     width = double // 2
@@ -172,6 +167,7 @@
     for j in range(peers):
         tiles_ref[j, :, :width] = wd_ref[:half, j * width : (j + 1) * width]
         tiles_ref[j, :, width:] = wd_ref[half:, j * width : (j + 1) * width]
+    copies[3].wait()
     gain = gain_ref[...]
     first = gain.astype(bf16).astype(f32)
     second = (gain - first).astype(bf16).astype(f32)
@@ -188,7 +184,7 @@
     copies[1].wait()
     copies[2].wait()
     for k in range(peers):
-        to = ahead(me_ref, k, peers)
+        to = lax.rem(me_ref[0] + k, peers)
         at = 0
         for t in range(double // 128):
             outs[k][at : at + half, :] = tiles_ref[to, :, 128 * t : 128 * (t + 1)]
@@ -210,19 +206,20 @@
     return pl.pallas_call(
         pack_kernel,
         out_shape=tuple(shape((rows, 128), bf16) for _ in range(peers)),
-        in_specs=[SMEM] + [HBM] * 3 + [VMEM],
+        in_specs=[SMEM] + [HBM] * 4,
         out_specs=tuple(VMEM for _ in range(peers)),
         scratch_shapes=[
             pltpu.VMEM(w_down.shape, bf16),
             pltpu.VMEM(cache.shape, bf16),
             pltpu.VMEM(queries.shape, bf16),
+            pltpu.VMEM(gain.shape, f32),
             pltpu.VMEM((peers, hid // 2, 2 * width), bf16),
             pltpu.VMEM((span + heads, own * keys), bf16),
-            pltpu.SemaphoreType.DMA((3,)),
+            pltpu.SemaphoreType.DMA((4,)),
         ],
         compiler_params=PARAMS,
         name="pack",
-    )(me, in_hbm(w_down), in_hbm(cache), in_hbm(queries), gain)
+    )(me, in_hbm(w_down), in_hbm(cache), in_hbm(queries), in_hbm(gain))
 
 
 def rows_kernel(x_ref, o_ref):
@@ -256,33 +253,50 @@
     return there + [upper, lower] + back[:0:-1]
 
 
-def down_kernel(me_ref, u_ref, *refs):
+def columns_kernel(*refs):
     blocks, o_ref, w_ref = refs[:-2], refs[-2], refs[-1]
-    peers, _, hid = u_ref.shape
-    experts, cap, width = o_ref.shape
-    rows, half = experts * cap, hid // 2
-    acc = jnp.zeros((rows, width), f32)
-    for k in range(peers):
-        group = behind(me_ref, k, peers)
-        for t in range(2 * width // 128):
+    half, double = w_ref.shape
+    width = double // 2
+    for k in range(len(blocks)):
+        for t in range(double // 128):
             w_ref[:, 128 * t : 128 * (t + 1)] = blocks[k][half * t : half * (t + 1), :]
-        units = u_ref[group, :rows, :]
-        acc = acc + jnp.dot(units[:, :half], w_ref[:, :width], preferred_element_type=f32)
-        acc = acc + jnp.dot(units[:, half:], w_ref[:, width:], preferred_element_type=f32)
-    o_ref[...] = acc.reshape(o_ref.shape).astype(bf16)
-
-
-def expert_down(me, units, blocks, experts, width):
-    hid = units.shape[2]
-    return pl.pallas_call(
-        down_kernel,
-        out_shape=shape((experts, CAP, width), bf16),
-        in_specs=[SMEM] + [VMEM] * (1 + len(blocks)),
+        o_ref[k, :half, :] = w_ref[:, :width]
+        o_ref[k, half:, :] = w_ref[:, width:]
+
+
+def columns_of(blocks, hid, width):
+    return pl.pallas_call(
+        columns_kernel,
+        out_shape=shape((len(blocks), hid, width), bf16),
+        in_specs=[VMEM] * len(blocks),
         out_specs=VMEM,
         scratch_shapes=[pltpu.VMEM((hid // 2, 2 * width), bf16)],
         compiler_params=PARAMS,
+        name="columns",
+    )(*blocks)
+
+
+def down_kernel(me_ref, u_ref, w_ref, o_ref):
+    peers = u_ref.shape[0]
+    experts, cap, width = o_ref.shape
+    acc = jnp.zeros((experts * cap, width), f32)
+    for k in range(peers):
+        group = lax.rem(me_ref[0] + (peers - k), peers)
+        acc = acc + jnp.dot(
+            u_ref[group, : experts * cap, :], w_ref[k], preferred_element_type=f32
+        )
+    o_ref[...] = acc.reshape(o_ref.shape).astype(bf16)
+
+
+def expert_down(me, units, columns, experts):
+    return pl.pallas_call(
+        down_kernel,
+        out_shape=shape((experts, CAP, columns.shape[2]), bf16),
+        in_specs=[SMEM, VMEM, VMEM],
+        out_specs=VMEM,
+        compiler_params=PARAMS,
         name="down",
-    )(me, units, *blocks)
+    )(me, units, columns)
 
 
 def attend_kernel(me_ref, len_ref, *refs):
@@ -300,7 +314,7 @@
             c_ref[i, k * span : (k + 1) * span, :] = m_ref[:span, i * keys : (i + 1) * keys]
             q_ref[i, k * heads : (k + 1) * heads, :] = m_ref[span:, i * keys : (i + 1) * keys]
     lane = lax.broadcasted_iota(jnp.int32, (peers * heads, positions), 1)
-    block = behind(me_ref, lane // span, peers)
+    block = lax.rem(me + (peers - lane // span), peers)
     position = block * span + lane % span
     for i in range(own):
         live = position < len_ref[me * own + i]
@@ -396,7 +410,7 @@
     )(returned, combine, hidden, gain, w_dkv)
 
 
-def merge_kernel(all_ref, gain_ref, cos_ref, sin_ref, q_ref, units_ref, o_ref, back_ref):
+def merge_kernel(all_ref, table_ref, q_ref, units_ref, o_ref, back_ref):
     peers = all_ref.shape[0]
     seqs, heads, lanes = back_ref.shape
     own = seqs // peers
@@ -418,12 +432,13 @@
     latent = (
         latent
         * lax.rsqrt(jnp.mean(latent * latent, -1, keepdims=True) + epsilon)
-        * gain_ref[...]
+        * table_ref[:1, :LAT]
     )
     rope = down[:, LAT:]
     half = rope.shape[-1] // 2
     turned = jnp.concatenate([rope[:, half:], rope[:, :half]], 1)
-    rope = rope * cos_ref[...] + turned * sin_ref[...]
+    cos, sin = LAT + 2 * half, LAT + 4 * half
+    rope = rope * table_ref[:, LAT:cos] + turned * table_ref[:, cos:sin]
     latent = latent.astype(bf16).astype(f32)[:, None, :]
     rope = rope.astype(bf16).astype(f32)[:, None, :]
     own = (
@@ -441,17 +456,17 @@
     ).astype(bf16)
 
 
-def merge(everything, gain, cos, sin, queries, units):
+def merge(everything, table, queries, units):
     seqs, heads, _ = queries.shape
     return pl.pallas_call(
         merge_kernel,
         out_shape=shape((seqs, heads, LAT), bf16),
-        in_specs=[VMEM] * 6,
+        in_specs=[VMEM] * 4,
         out_specs=VMEM,
         scratch_shapes=[pltpu.VMEM((seqs, heads, LAT + 128), bf16)],
         compiler_params=PARAMS,
         name="merge",
-    )(everything, gain, cos, sin, queries, units)
+    )(everything, table, queries, units)
 
 
 def rope_tables(lengths, half):
@@ -480,17 +495,10 @@
     seqs, width = hidden.shape
     peers = lax.axis_size("tp")
     experts = lax.axis_size("ep") * lax.axis_size("mb")
-    cores = lax.axis_size("mb")
-    sense = 1 - 2 * (lax.axis_index("mb") % 2)
-    me = jnp.stack([lax.axis_index("tp"), sense]).astype(jnp.int32)
+    me = lax.axis_index("tp").astype(jnp.int32).reshape(1)
 
     def moved(x, k):
-        pairs = [
-            (i * cores + c, (i + (k if c % 2 == 0 else peers - k)) % peers * cores + c)
-            for i in range(peers)
-            for c in range(cores)
-        ]
-        return lax.ppermute(x, ("tp", "mb"), pairs)
+        return lax.ppermute(x, "tp", [(i, (i + k) % peers) for i in range(peers)])
 
     send_rows, combine = route(expert_ids, slots, affinity, hidden, experts)
     arrived = exchange(send_rows, ("ep", "mb"))
@@ -502,12 +510,14 @@
     attended = attend(me, lengths, blocks, seqs // peers, span, heads, keys)
     units = expert_units(me, parts, w_gate[0], w_up[0], attended, blocks)
     all_units = exchange(units, "tp")
-    output = expert_down(me, all_units, blocks, experts, width)
+    columns = columns_of(blocks, w_down.shape[1], width)
+    output = expert_down(me, all_units, columns, experts)
     returned = exchange(output, ("ep", "mb"))
     next_hidden, small = close(returned, combine, hidden, attn_gain[None], w_dkv, peers)
     everything = exchange(small, "tp")
-    cos, sin = rope_tables(lengths, (keys - LAT) // 2)
-    latent_out = merge(everything, kv_gain[None], cos, sin, queries, all_units)
+    gain = jnp.broadcast_to(kv_gain, (seqs, LAT))
+    table = jnp.concatenate([gain, *rope_tables(lengths, (keys - LAT) // 2)], 1)
+    latent_out = merge(everything, table, queries, all_units)
     return (next_hidden, latent_out)
 
 

time: 213 us -> 217 us (1.019)
  waiting for transfers between devices: 35.1 us -> 66.2 us
  blocking collectives: 87.2 us -> 66.2 us
  starting transfers between devices: 73 us -> 69.6 us
    all_to_all x2 -> x1, blocking collectives: 87.2 us -> 66.2 us  [exchange(): return lax.all_to_all(x, axis, split_axis=0, concat_axis=0, tiled=True)]
    all_to_all x2 -> x3, waiting for transfers between devices: 30.9 us -> 50.4 us  [exchange(): return lax.all_to_all(x, axis, split_axis=0, concat_axis=0, tiled=True)]
    ppermute x15, waiting for transfers between devices: 4.21 us -> 15.7 us  [moved(): return lax.ppermute(x, 'tp', [(i, (i + k) % peers) for i in range(peers)])]
    ppermute x15, starting transfers between devices: 64.3 us -> 57 us  [moved(): return lax.ppermute(x, 'tp', [(i, (i + k) % peers) for i in range(peers)])]
    all_to_all x2 -> x3, starting transfers between devices: 8.63 us -> 12.6 us  [exchange(): return lax.all_to_all(x, axis, split_axis=0, concat_axis=0, tiled=True)]
  transfers between devices with their start and end apart: 17 -> 18, of which waited for: 4 -> 7; matrix products, arithmetic and copies ran while one was open for 0% -> 0% of each run, Pallas kernels for 2% -> 2%
where the time goes in v6:
time: 217 us; the launch traced here: 216 us
  starting transfers between devices  69.6 us (32%)
  blocking collectives  66.2 us (31%)
  waiting for transfers between devices  66.2 us (31%)
  Pallas kernels  12.7 us (6%)
    all_to_all x1, blocking collectives, exchange(): return lax.all_to_all(x, axis, split_axis=0, concat_axis=0, tiled=True)  66.2 us
    ppermute x15, starting transfers between devices, moved(): return lax.ppermute(x, 'tp', [(i, (i + k) % peers) for i in range(peers)])  57 us
    all_to_all x3, waiting for transfers between devices, exchange(): return lax.all_to_all(x, axis, split_axis=0, concat_axis=0, tiled=True)  50.4 us
    ppermute x15, waiting for transfers between devices, moved(): return lax.ppermute(x, 'tp', [(i, (i + k) % peers) for i in range(peers)])  15.7 us
    all_to_all x3, starting transfers between devices, exchange(): return lax.all_to_all(x, axis, split_axis=0, concat_axis=0, tiled=True)  12.6 us
    pallas_call x1, Pallas kernels, expert_units(): pl.pallas_call(units_kernel, out_shape=shape((peers, rows + attended.shap...  4.53 us
  transfers between devices with their start and end apart: 18, of which 7 were waited for; matrix products, arithmetic and copies ran while one was open for 0% of the time, Pallas kernels for 2%

profile of v6, /device:TPU:80, one launch (start us, length us, event | category | flops | bytes accessed | tf_op | source)
XLA Modules:
  0.0 215.9 jit_solution(9491117513196873141)
XLA Ops:
  0.6 1.1 route.1
  1.7 66.2 %all_to_all.20.x_ref = bf16[32,8,448]{2,1,0:T(8,128)(2,1)S(1)} all-to-all(bf16[32,8,448]{2,1,0:T(8,128)(2,1)S(1)} %get-tuple-element.22), channel_id=1, replica_groups=mesh['grp'=2,'ep'=16,'tp'=8,'mb'=2] {'ep','mb'}, dimensions={0} | all-to-all | bytes 458752 | tf_op jit(solution)/shard_map/all_to_all | solution.py:31
  67.9 0.1 rows.1.refs_8_
  68.0 3.6 %collective-permute-start.7 = (bf16[128,896]{1,0:T(8,128)(2,1)S(1)}, bf16[128,896]{1,0:T(8,128)(2,1)S(1)}, u32[]{:S(2)}, u32[]{:S(2)}) collective-permute-start(bf16[128,896]{1,0:T(8,128)(2,1)S(1)} %rows.1.refs_8_), channel_id=1, source_target_pairs={{0,2},{2,4},{4,6},{6,8},{8,10},{10,12},{12,14},{14,0},{1,3},{3,5},... | collective-permute-start | bytes 688136 | tf_op jit(solution)/shard_map/ppermute | solution.py:501
  71.6 4.1 %collective-permute-start.11 = (bf16[128,896]{1,0:T(8,128)(2,1)S(1)}, bf16[128,896]{1,0:T(8,128)(2,1)S(1)}, u32[]{:S(2)}, u32[]{:S(2)}) collective-permute-start(bf16[128,896]{1,0:T(8,128)(2,1)S(1)} %rows.1.refs_8_), channel_id=1, source_target_pairs={{0,14},{2,0},{4,2},{6,4},{8,6},{10,8},{12,10},{14,12},{1,15},{3,1}... | collective-permute-start | bytes 688136 | tf_op jit(solution)/shard_map/ppermute | solution.py:501
  75.8 3.7 %collective-permute-done.7.refs_9_ = bf16[128,896]{1,0:T(8,128)(2,1)S(1)} collective-permute-done((bf16[128,896]{1,0:T(8,128)(2,1)S(1)}, bf16[128,896]{1,0:T(8,128)(2,1)S(1)}, u32[]{:S(2)}, u32[]{:S(2)}) %collective-permute-start.7) | collective-permute-done | bytes 229408 | tf_op jit(solution)/shard_map/ppermute | solution.py:501
  79.5 1.9 collective-permute-start.8
  81.4 0.0 collective-permute-done.11.refs_16_
  81.4 5.2 %collective-permute-start.12 = (bf16[128,896]{1,0:T(8,128)(2,1)S(1)}, bf16[128,896]{1,0:T(8,128)(2,1)S(1)}, u32[]{:S(2)}, u32[]{:S(2)}) collective-permute-start(bf16[128,896]{1,0:T(8,128)(2,1)S(1)} %collective-permute-done.11.refs_16_), channel_id=1, source_target_pairs={{0,14},{2,0},{4,2},{6,4},{8,6},{10,8},{12,10},{14,12},{1,15},{3,1}... | collective-permute-start | bytes 688136 | tf_op jit(solution)/shard_map/ppermute | solution.py:501
  86.6 1.8 pack.1
  88.4 2.0 collective-permute-start
  90.4 0.0 collective-permute-done.8.refs_10_
  90.4 2.3 %collective-permute-start.9 = (bf16[128,896]{1,0:T(8,128)(2,1)S(1)}, bf16[128,896]{1,0:T(8,128)(2,1)S(1)}, u32[]{:S(2)}, u32[]{:S(2)}) collective-permute-start(bf16[128,896]{1,0:T(8,128)(2,1)S(1)} %collective-permute-done.8.refs_10_), channel_id=1, source_target_pairs={{0,2},{2,4},{4,6},{6,8},{8,10},{10,12},{12,14},{14,0},{1,3},{3,5},... | collective-permute-start | bytes 688136 | tf_op jit(solution)/shard_map/ppermute | solution.py:501
  92.7 0.0 collective-permute-done.12.refs_15_
  92.7 4.8 %collective-permute-start.13 = (bf16[128,896]{1,0:T(8,128)(2,1)S(1)}, bf16[128,896]{1,0:T(8,128)(2,1)S(1)}, u32[]{:S(2)}, u32[]{:S(2)}) collective-permute-start(bf16[128,896]{1,0:T(8,128)(2,1)S(1)} %collective-permute-done.12.refs_15_), channel_id=1, source_target_pairs={{0,14},{2,0},{4,2},{6,4},{8,6},{10,8},{12,10},{14,12},{1,15},{3,1}... | collective-permute-start | bytes 688136 | tf_op jit(solution)/shard_map/ppermute | solution.py:501
  97.5 5.0 %collective-permute-start.1 = (bf16[680,128]{1,0:T(8,128)(2,1)S(1)}, bf16[680,128]{1,0:T(8,128)(2,1)S(1)}, u32[]{:S(2)}, u32[]{:S(2)}) collective-permute-start(bf16[680,128]{1,0:T(8,128)(2,1)S(1)} %get-tuple-element.16), channel_id=1, source_target_pairs={{0,4},{2,6},{4,8},{6,10},{8,12},{10,14},{12,0},{14,2},{1,5},{3,7},... | collective-permute-start | bytes 522248 | tf_op jit(solution)/shard_map/ppermute | solution.py:501
  102.5 3.4 %collective-permute-start.2 = (bf16[680,128]{1,0:T(8,128)(2,1)S(1)}, bf16[680,128]{1,0:T(8,128)(2,1)S(1)}, u32[]{:S(2)}, u32[]{:S(2)}) collective-permute-start(bf16[680,128]{1,0:T(8,128)(2,1)S(1)} %get-tuple-element.17), channel_id=1, source_target_pairs={{0,6},{2,8},{4,10},{6,12},{8,14},{10,0},{12,2},{14,4},{1,7},{3,9},... | collective-permute-start | bytes 522248 | tf_op jit(solution)/shard_map/ppermute | solution.py:501
  105.9 0.0 collective-permute-done.refs_1_
  105.9 3.7 %collective-permute-start.3 = (bf16[680,128]{1,0:T(8,128)(2,1)S(1)}, bf16[680,128]{1,0:T(8,128)(2,1)S(1)}, u32[]{:S(2)}, u32[]{:S(2)}) collective-permute-start(bf16[680,128]{1,0:T(8,128)(2,1)S(1)} %get-tuple-element.18), channel_id=1, source_target_pairs={{0,8},{2,10},{4,12},{6,14},{8,0},{10,2},{12,4},{14,6},{1,9},{3,11}... | collective-permute-start | bytes 522248 | tf_op jit(solution)/shard_map/ppermute | solution.py:501
  109.7 7.4 %collective-permute-done.1.refs_2_ = bf16[680,128]{1,0:T(8,128)(2,1)S(1)} collective-permute-done((bf16[680,128]{1,0:T(8,128)(2,1)S(1)}, bf16[680,128]{1,0:T(8,128)(2,1)S(1)}, u32[]{:S(2)}, u32[]{:S(2)}) %collective-permute-start.1) | collective-permute-done | bytes 174112 | tf_op jit(solution)/shard_map/ppermute | solution.py:501
  117.1 3.9 %collective-permute-start.4 = (bf16[680,128]{1,0:T(8,128)(2,1)S(1)}, bf16[680,128]{1,0:T(8,128)(2,1)S(1)}, u32[]{:S(2)}, u32[]{:S(2)}) collective-permute-start(bf16[680,128]{1,0:T(8,128)(2,1)S(1)} %get-tuple-element.19), channel_id=1, source_target_pairs={{0,10},{2,12},{4,14},{6,0},{8,2},{10,4},{12,6},{14,8},{1,11},{3,13... | collective-permute-start | bytes 522248 | tf_op jit(solution)/shard_map/ppermute | solution.py:501
  121.0 0.0 collective-permute-done.9.refs_11_
  121.0 8.0 %collective-permute-start.5 = (bf16[680,128]{1,0:T(8,128)(2,1)S(1)}, bf16[680,128]{1,0:T(8,128)(2,1)S(1)}, u32[]{:S(2)}, u32[]{:S(2)}) collective-permute-start(bf16[680,128]{1,0:T(8,128)(2,1)S(1)} %get-tuple-element.20), channel_id=1, source_target_pairs={{0,12},{2,14},{4,0},{6,2},{8,4},{10,6},{12,8},{14,10},{1,13},{3,15... | collective-permute-start | bytes 522248 | tf_op jit(solution)/shard_map/ppermute | solution.py:501
  129.0 0.0 collective-permute-done.13.refs_14_
  129.0 2.0 collective-permute-start.6
  131.0 0.0 copy-start.4
  131.0 0.0 collective-permute-done.2.refs_3_
  131.0 4.0 %collective-permute-start.10 = (bf16[64,896]{1,0:T(8,128)(2,1)S(1)}, bf16[64,896]{1,0:T(8,128)(2,1)S(1)}, u32[]{:S(2)}, u32[]{:S(2)}) collective-permute-start(bf16[64,896]{1,0:T(8,128)(2,1)S(1)} %slice.8), channel_id=1, source_target_pairs={{0,2},{2,4},{4,6},{6,8},{8,10},{10,12},{12,14},{14,0},{1,3},{3,5},... | collective-permute-start | bytes 344072 | tf_op jit(solution)/shard_map/ppermute | solution.py:501
  135.0 3.2 %collective-permute-start.14 = (bf16[64,896]{1,0:T(8,128)(2,1)S(1)}, bf16[64,896]{1,0:T(8,128)(2,1)S(1)}, u32[]{:S(2)}, u32[]{:S(2)}) collective-permute-start(bf16[64,896]{1,0:T(8,128)(2,1)S(1)} %slice.9), channel_id=1, source_target_pairs={{0,14},{2,0},{4,2},{6,4},{8,6},{10,8},{12,10},{14,12},{1,15},{3,1}... | collective-permute-start | bytes 344072 | tf_op jit(solution)/shard_map/ppermute | solution.py:501
  138.2 0.2 collective-permute-done.5.refs_6_
  138.4 4.4 %collective-permute-done.6.refs_7_ = bf16[680,128]{1,0:T(8,128)(2,1)S(1)} collective-permute-done((bf16[680,128]{1,0:T(8,128)(2,1)S(1)}, bf16[680,128]{1,0:T(8,128)(2,1)S(1)}, u32[]{:S(2)}, u32[]{:S(2)}) %collective-permute-start.6) | collective-permute-done | bytes 174112 | tf_op jit(solution)/shard_map/ppermute | solution.py:501
  142.8 1.3 attend.1.att_ref
  144.1 0.0 collective-permute-done.10.refs_12_
  144.1 4.5 %units.1 = bf16[8,336,128]{2,1,0:T(8,128)(2,1)} custom-call(s32[1]{0:T(128)} %bitcast.me_ref, bf16[3584,128]{1,0:T(8,128)(2,1)} %bitcast.11, bf16[3584,128]{1,0:T(8,128)(2,1)} %bitcast.12, bf16[8,80,128]{2,1,0:T(8,128)(2,1)S(1)} %attend.1.att_ref, bf16[680,128]{1,0:T(8,128)(2,1)S(1)} %get-tuple-element.14.refs_0_, ...), custom_call_target="tpu_custom_call" | custom-call | tf_op jit(solution)/shard_map/units/pallas_call | solution.py:138
  148.7 4.0 %all-to-all-start.1 = ((bf16[8,336,128]{2,1,0:T(8,128)(2,1)}), bf16[8,336,128]{2,1,0:T(8,128)(2,1)S(1)}, u32[]{:S(2)}, u32[]{:S(2)}) async-start(bf16[8,336,128]{2,1,0:T(8,128)(2,1)} %units.1), calls=%async_computation.1 | async-start | bytes 1376256 | tf_op jit(solution)/shard_map/all_to_all | solution.py:31
  152.6 0.3 columns.1.w_ref
  153.0 19.6 %all-to-all-done.1.u_ref.units_ref = bf16[8,336,128]{2,1,0:T(8,128)(2,1)S(1)} async-done(((bf16[8,336,128]{2,1,0:T(8,128)(2,1)}), bf16[8,336,128]{2,1,0:T(8,128)(2,1)S(1)}, u32[]{:S(2)}, u32[]{:S(2)}) %all-to-all-start.1) | async-done | bytes 688160 | tf_op jit(solution)/shard_map/all_to_all | solution.py:31
  172.6 1.4 down.1
  174.0 4.9 %all-to-all-start.2 = ((bf16[32,8,448]{2,1,0:T(8,128)(2,1)}), bf16[32,8,448]{2,1,0:T(8,128)(2,1)S(1)}, u32[]{:S(2)}, u32[]{:S(2)}) async-start(bf16[32,8,448]{2,1,0:T(8,128)(2,1)} %down.1), calls=%async_computation.2 | async-start | bytes 524288 | tf_op jit(solution)/shard_map/all_to_all | solution.py:31
  178.9 0.0 copy-start.3
  178.9 21.9 %all-to-all-done.2.ret_ref = bf16[32,8,448]{2,1,0:T(8,128)(2,1)S(1)} async-done(((bf16[32,8,448]{2,1,0:T(8,128)(2,1)}), bf16[32,8,448]{2,1,0:T(8,128)(2,1)S(1)}, u32[]{:S(2)}, u32[]{:S(2)}) %all-to-all-start.2) | async-done | bytes 229408 | tf_op jit(solution)/shard_map/all_to_all | solution.py:31
  200.8 1.1 close.1
  201.9 3.7 %all-to-all-start.3 = ((bf16[8,16,640]{2,1,0:T(8,128)(2,1)}), bf16[8,16,640]{2,1,0:T(8,128)(2,1)S(1)}, u32[]{:S(2)}, u32[]{:S(2)}) async-start(bf16[8,16,640]{2,1,0:T(8,128)(2,1)} %get-tuple-element.25), calls=%async_computation.3 | async-start | bytes 327680 | tf_op jit(solution)/shard_map/all_to_all | solution.py:31
  205.6 0.0 copy-start
  205.7 0.1 multiply_sine_fusion
  205.8 0.1 concatenate.3.table_ref
  205.9 8.9 %all-to-all-done.3.all_ref = bf16[8,16,640]{2,1,0:T(8,128)(2,1)S(1)} async-done(((bf16[8,16,640]{2,1,0:T(8,128)(2,1)}), bf16[8,16,640]{2,1,0:T(8,128)(2,1)S(1)}, u32[]{:S(2)}, u32[]{:S(2)}) %all-to-all-start.3) | async-done | bytes 163872 | tf_op jit(solution)/shard_map/all_to_all | solution.py:31
  214.8 1.1 merge.1
  (17 shorter events, 0.1 us)
Async XLA Ops:
  68.0 11.4 %collective-permute-start.7 = (bf16[128,896]{1,0:T(8,128)(2,1)S(1)}, bf16[128,896]{1,0:T(8,128)(2,1)S(1)}, u32[]{:S(2)}, u32[]{:S(2)}) collective-permute-start(bf16[128,896]{1,0:T(8,128)(2,1)S(1)} %rows.1.refs_8_), channel_id=1, source_target_pairs={{0,2},{2,4},{4,6},{6,8},{8,10},{10,12},{12,14},{14,0},{1,3},{3,5},... | collective-permute-start | bytes 688136 | tf_op jit(solution)/shard_map/ppermute | solution.py:501
  71.6 9.8 %collective-permute-start.11 = (bf16[128,896]{1,0:T(8,128)(2,1)S(1)}, bf16[128,896]{1,0:T(8,128)(2,1)S(1)}, u32[]{:S(2)}, u32[]{:S(2)}) collective-permute-start(bf16[128,896]{1,0:T(8,128)(2,1)S(1)} %rows.1.refs_8_), channel_id=1, source_target_pairs={{0,14},{2,0},{4,2},{6,4},{8,6},{10,8},{12,10},{14,12},{1,15},{3,1}... | collective-permute-start | bytes 688136 | tf_op jit(solution)/shard_map/ppermute | solution.py:501
  79.5 10.9 %collective-permute-start.8 = (bf16[128,896]{1,0:T(8,128)(2,1)S(1)}, bf16[128,896]{1,0:T(8,128)(2,1)S(1)}, u32[]{:S(2)}, u32[]{:S(2)}) collective-permute-start(bf16[128,896]{1,0:T(8,128)(2,1)S(1)} %collective-permute-done.7.refs_9_), channel_id=1, source_target_pairs={{0,2},{2,4},{4,6},{6,8},{8,10},{10,12},{12,14},{14,0},{1,3},{3,5},... | collective-permute-start | bytes 688136 | tf_op jit(solution)/shard_map/ppermute | solution.py:501
  81.4 11.3 %collective-permute-start.12 = (bf16[128,896]{1,0:T(8,128)(2,1)S(1)}, bf16[128,896]{1,0:T(8,128)(2,1)S(1)}, u32[]{:S(2)}, u32[]{:S(2)}) collective-permute-start(bf16[128,896]{1,0:T(8,128)(2,1)S(1)} %collective-permute-done.11.refs_16_), channel_id=1, source_target_pairs={{0,14},{2,0},{4,2},{6,4},{8,6},{10,8},{12,10},{14,12},{1,15},{3,1}... | collective-permute-start | bytes 688136 | tf_op jit(solution)/shard_map/ppermute | solution.py:501
  88.4 17.5 %collective-permute-start = (bf16[680,128]{1,0:T(8,128)(2,1)S(1)}, bf16[680,128]{1,0:T(8,128)(2,1)S(1)}, u32[]{:S(2)}, u32[]{:S(2)}) collective-permute-start(bf16[680,128]{1,0:T(8,128)(2,1)S(1)} %get-tuple-element.15), channel_id=1, source_target_pairs={{0,2},{2,4},{4,6},{6,8},{8,10},{10,12},{12,14},{14,0},{1,3},{3,5},... | collective-permute-start | bytes 522248 | tf_op jit(solution)/shard_map/ppermute | solution.py:501
  90.4 30.6 %collective-permute-start.9 = (bf16[128,896]{1,0:T(8,128)(2,1)S(1)}, bf16[128,896]{1,0:T(8,128)(2,1)S(1)}, u32[]{:S(2)}, u32[]{:S(2)}) collective-permute-start(bf16[128,896]{1,0:T(8,128)(2,1)S(1)} %collective-permute-done.8.refs_10_), channel_id=1, source_target_pairs={{0,2},{2,4},{4,6},{6,8},{8,10},{10,12},{12,14},{14,0},{1,3},{3,5},... | collective-permute-start | bytes 688136 | tf_op jit(solution)/shard_map/ppermute | solution.py:501
  92.7 36.3 %collective-permute-start.13 = (bf16[128,896]{1,0:T(8,128)(2,1)S(1)}, bf16[128,896]{1,0:T(8,128)(2,1)S(1)}, u32[]{:S(2)}, u32[]{:S(2)}) collective-permute-start(bf16[128,896]{1,0:T(8,128)(2,1)S(1)} %collective-permute-done.12.refs_15_), channel_id=1, source_target_pairs={{0,14},{2,0},{4,2},{6,4},{8,6},{10,8},{12,10},{14,12},{1,15},{3,1}... | collective-permute-start | bytes 688136 | tf_op jit(solution)/shard_map/ppermute | solution.py:501
  97.5 19.6 %collective-permute-start.1 = (bf16[680,128]{1,0:T(8,128)(2,1)S(1)}, bf16[680,128]{1,0:T(8,128)(2,1)S(1)}, u32[]{:S(2)}, u32[]{:S(2)}) collective-permute-start(bf16[680,128]{1,0:T(8,128)(2,1)S(1)} %get-tuple-element.16), channel_id=1, source_target_pairs={{0,4},{2,6},{4,8},{6,10},{8,12},{10,14},{12,0},{14,2},{1,5},{3,7},... | collective-permute-start | bytes 522248 | tf_op jit(solution)/shard_map/ppermute | solution.py:501
  102.5 28.5 %collective-permute-start.2 = (bf16[680,128]{1,0:T(8,128)(2,1)S(1)}, bf16[680,128]{1,0:T(8,128)(2,1)S(1)}, u32[]{:S(2)}, u32[]{:S(2)}) collective-permute-start(bf16[680,128]{1,0:T(8,128)(2,1)S(1)} %get-tuple-element.17), channel_id=1, source_target_pairs={{0,6},{2,8},{4,10},{6,12},{8,14},{10,0},{12,2},{14,4},{1,7},{3,9},... | collective-permute-start | bytes 522248 | tf_op jit(solution)/shard_map/ppermute | solution.py:501
  105.9 29.1 %collective-permute-start.3 = (bf16[680,128]{1,0:T(8,128)(2,1)S(1)}, bf16[680,128]{1,0:T(8,128)(2,1)S(1)}, u32[]{:S(2)}, u32[]{:S(2)}) collective-permute-start(bf16[680,128]{1,0:T(8,128)(2,1)S(1)} %get-tuple-element.18), channel_id=1, source_target_pairs={{0,8},{2,10},{4,12},{6,14},{8,0},{10,2},{12,4},{14,6},{1,9},{3,11}... | collective-permute-start | bytes 522248 | tf_op jit(solution)/shard_map/ppermute | solution.py:501
  117.1 21.1 %collective-permute-start.4 = (bf16[680,128]{1,0:T(8,128)(2,1)S(1)}, bf16[680,128]{1,0:T(8,128)(2,1)S(1)}, u32[]{:S(2)}, u32[]{:S(2)}) collective-permute-start(bf16[680,128]{1,0:T(8,128)(2,1)S(1)} %get-tuple-element.19), channel_id=1, source_target_pairs={{0,10},{2,12},{4,14},{6,0},{8,2},{10,4},{12,6},{14,8},{1,11},{3,13... | collective-permute-start | bytes 522248 | tf_op jit(solution)/shard_map/ppermute | solution.py:501
  121.0 17.4 %collective-permute-start.5 = (bf16[680,128]{1,0:T(8,128)(2,1)S(1)}, bf16[680,128]{1,0:T(8,128)(2,1)S(1)}, u32[]{:S(2)}, u32[]{:S(2)}) collective-permute-start(bf16[680,128]{1,0:T(8,128)(2,1)S(1)} %get-tuple-element.20), channel_id=1, source_target_pairs={{0,12},{2,14},{4,0},{6,2},{8,4},{10,6},{12,8},{14,10},{1,13},{3,15... | collective-permute-start | bytes 522248 | tf_op jit(solution)/shard_map/ppermute | solution.py:501
  129.0 13.8 %collective-permute-start.6 = (bf16[680,128]{1,0:T(8,128)(2,1)S(1)}, bf16[680,128]{1,0:T(8,128)(2,1)S(1)}, u32[]{:S(2)}, u32[]{:S(2)}) collective-permute-start(bf16[680,128]{1,0:T(8,128)(2,1)S(1)} %get-tuple-element.21), channel_id=1, source_target_pairs={{0,14},{2,0},{4,2},{6,4},{8,6},{10,8},{12,10},{14,12},{1,15},{3,1}... | collective-permute-start | bytes 522248 | tf_op jit(solution)/shard_map/ppermute | solution.py:501
  131.0 11.8 %copy-start.4 = (s32[16]{0:T(128)S(1)}, s32[16]{0:T(128)}, u32[]{:S(2)}) copy-start(s32[16]{0:T(128)} %len_ref.1) | copy-start | bytes 196
  131.0 13.1 %collective-permute-start.10 = (bf16[64,896]{1,0:T(8,128)(2,1)S(1)}, bf16[64,896]{1,0:T(8,128)(2,1)S(1)}, u32[]{:S(2)}, u32[]{:S(2)}) collective-permute-start(bf16[64,896]{1,0:T(8,128)(2,1)S(1)} %slice.8), channel_id=1, source_target_pairs={{0,2},{2,4},{4,6},{6,8},{8,10},{10,12},{12,14},{14,0},{1,3},{3,5},... | collective-permute-start | bytes 344072 | tf_op jit(solution)/shard_map/ppermute | solution.py:501
  135.0 9.1 %collective-permute-start.14 = (bf16[64,896]{1,0:T(8,128)(2,1)S(1)}, bf16[64,896]{1,0:T(8,128)(2,1)S(1)}, u32[]{:S(2)}, u32[]{:S(2)}) collective-permute-start(bf16[64,896]{1,0:T(8,128)(2,1)S(1)} %slice.9), channel_id=1, source_target_pairs={{0,14},{2,0},{4,2},{6,4},{8,6},{10,8},{12,10},{14,12},{1,15},{3,1}... | collective-permute-start | bytes 344072 | tf_op jit(solution)/shard_map/ppermute | solution.py:501
  148.7 23.9 %all-to-all-start.1 = ((bf16[8,336,128]{2,1,0:T(8,128)(2,1)}), bf16[8,336,128]{2,1,0:T(8,128)(2,1)S(1)}, u32[]{:S(2)}, u32[]{:S(2)}) async-start(bf16[8,336,128]{2,1,0:T(8,128)(2,1)} %units.1), calls=%async_computation.1 | async-start | bytes 1376256 | tf_op jit(solution)/shard_map/all_to_all | solution.py:31
  172.6 28.3 %copy-start.1 = (bf16[448,576]{1,0:T(8,128)(2,1)S(1)}, bf16[448,576]{1,0:T(8,128)(2,1)}, u32[]{:S(2)}) copy-start(bf16[448,576]{1,0:T(8,128)(2,1)} %wdkv_ref.1) | copy-start | bytes 1548292
  174.0 26.9 %copy-start.2 = (bf16[16,448]{1,0:T(8,128)(2,1)S(1)}, bf16[16,448]{1,0:T(8,128)(2,1)}, u32[]{:S(2)}) copy-start(bf16[16,448]{1,0:T(8,128)(2,1)} %hid_ref.1) | copy-start | bytes 43012
  174.0 26.9 %all-to-all-start.2 = ((bf16[32,8,448]{2,1,0:T(8,128)(2,1)}), bf16[32,8,448]{2,1,0:T(8,128)(2,1)S(1)}, u32[]{:S(2)}, u32[]{:S(2)}) async-start(bf16[32,8,448]{2,1,0:T(8,128)(2,1)} %down.1), calls=%async_computation.2 | async-start | bytes 524288 | tf_op jit(solution)/shard_map/all_to_all | solution.py:31
  178.9 22.0 %copy-start.3 = (f32[448]{0:T(512)S(1)}, f32[448]{0:T(512)}, u32[]{:S(2)}) copy-start(f32[448]{0:T(512)} %param.22) | copy-start | bytes 5380
  201.9 3.9 %copy-start.5 = (f32[512]{0:T(512)S(1)}, f32[512]{0:T(512)}, u32[]{:S(2)}) copy-start(f32[512]{0:T(512)} %param.24) | copy-start | bytes 6148
  201.9 12.9 %all-to-all-start.3 = ((bf16[8,16,640]{2,1,0:T(8,128)(2,1)}), bf16[8,16,640]{2,1,0:T(8,128)(2,1)S(1)}, u32[]{:S(2)}, u32[]{:S(2)}) async-start(bf16[8,16,640]{2,1,0:T(8,128)(2,1)} %get-tuple-element.25), calls=%async_computation.3 | async-start | bytes 327680 | tf_op jit(solution)/shard_map/all_to_all | solution.py:31
  205.6 9.2 %copy-start = (bf16[16,8,576]{2,1,0:T(8,128)(2,1)S(1)}, bf16[16,8,576]{2,1,0:T(8,128)(2,1)}, u32[]{:S(2)}) copy-start(bf16[16,8,576]{2,1,0:T(8,128)(2,1)} %q_ref.1) | copy-start | bytes 442372

commit v7 on v6

--- a/solution.py
+++ b/solution.py
@@ -96,16 +96,24 @@
     blocks, parts = refs[:peers], refs[peers : 2 * peers + 1]
     o_ref, wg_ref, wu_ref, n_ref, g_ref, u_ref, sems = refs[2 * peers + 1 :]
     copies = fetch((wg_hbm, wu_hbm), (wg_ref, wu_ref), sems)
-    half, double = parts[0].shape
-    rows, cols, middle = 2 * half, double // 2, peers // 2
+    _, rows, cols = n_ref.shape
+    middle, tiles = peers // 2, cols // 128
     square = jnp.zeros((rows, 1), f32)
     for k in range(peers):
         at = 0
-        for part in parts[k : k + 1] if k < middle else parts[k : k + 2] if k == middle else parts[k + 1 : k + 2]:
-            end = at + part.shape[0]
-            n_ref[k, at:end, :] = part[:, :cols]
-            n_ref[k, half + at : half + end, :] = part[:, cols:]
-            at = end
+        first = k if k <= middle else k + 1
+        for part in parts[first : first + (2 if k == middle else 1)]:
+            done = 0
+            while done < part.shape[0]:
+                tile, row = divmod(at, rows)
+                take = min(part.shape[0] - done, (rows if tile < tiles else rows // 2) - row)
+                piece = part[done : done + take, :]
+                if tile < tiles:
+                    n_ref[k, row : row + take, 128 * tile : 128 * (tile + 1)] = piece
+                else:
+                    n_ref[k, row : row + take, 128 * tiles :] = piece[:, :64]
+                    n_ref[k, rows // 2 + row : rows // 2 + row + take, 128 * tiles :] = piece[:, 64:]
+                at, done = at + take, done + take
         x = n_ref[k].astype(f32)
         square = square + jnp.sum(x * x, -1, keepdims=True)
     scale = lax.rsqrt(square / D + epsilon)
@@ -133,8 +141,8 @@
 
 def expert_units(me, parts, w_gate, w_up, attended, blocks):
     peers = len(blocks)
-    half, double = parts[0].shape
-    rows, cols, hid = 2 * half, double // 2, w_gate.shape[1]
+    cols, hid = w_gate.shape[0] // peers, w_gate.shape[1]
+    rows = parts[0].shape[0] * 128 // cols
     return pl.pallas_call(
         units_kernel,
         out_shape=shape((peers, rows + attended.shape[1], hid), bf16),
@@ -223,18 +231,21 @@
 
 
 def rows_kernel(x_ref, o_ref):
-    half, double = o_ref.shape
-    width = double // 2
-    x = x_ref[...].reshape(2 * half, width)
-    o_ref[:, :width] = x[:half]
-    o_ref[:, width:] = x[half:]
+    experts, cap, width = x_ref.shape
+    rows = experts * cap
+    x = x_ref[...].reshape(rows, width)
+    tiles = width // 128
+    for t in range(tiles):
+        o_ref[t * rows : (t + 1) * rows, :] = x[:, 128 * t : 128 * (t + 1)]
+    o_ref[tiles * rows :, :64] = x[: rows // 2, 128 * tiles :]
+    o_ref[tiles * rows :, 64:] = x[rows // 2 :, 128 * tiles :]
 
 
 def packed_rows(arrived):
     experts, cap, width = arrived.shape
     return pl.pallas_call(
         rows_kernel,
-        out_shape=shape((experts * cap // 2, 2 * width), bf16),
+        out_shape=shape((experts * cap * width // 128, 128), bf16),
         in_specs=[VMEM],
         out_specs=VMEM,
         compiler_params=PARAMS,

time: 217 us -> 217 us (level)
  no operation moved by 1% of the time
where the time goes in v7:
time: 217 us; the launch traced here: 216 us
  starting transfers between devices  69.6 us (32%)
  blocking collectives  66.2 us (31%)
  waiting for transfers between devices  66.2 us (31%)
  Pallas kernels  12.5 us (6%)
    all_to_all x1, blocking collectives, exchange(): return lax.all_to_all(x, axis, split_axis=0, concat_axis=0, tiled=True)  66.2 us
    ppermute x15, starting transfers between devices, moved(): return lax.ppermute(x, 'tp', [(i, (i + k) % peers) for i in range(peers)])  57 us
    all_to_all x3, waiting for transfers between devices, exchange(): return lax.all_to_all(x, axis, split_axis=0, concat_axis=0, tiled=True)  50.4 us
    ppermute x15, waiting for transfers between devices, moved(): return lax.ppermute(x, 'tp', [(i, (i + k) % peers) for i in range(peers)])  15.7 us
    all_to_all x3, starting transfers between devices, exchange(): return lax.all_to_all(x, axis, split_axis=0, concat_axis=0, tiled=True)  12.6 us
  transfers between devices with their start and end apart: 18, of which 7 were waited for; matrix products, arithmetic and copies ran while one was open for 0% of the time, Pallas kernels for 2%

profile of v7, /device:TPU:80, one launch (start us, length us, event | category | flops | bytes accessed | tf_op | source)
XLA Modules:
  0.0 215.7 jit_solution(15127707560167935744)
XLA Ops:
  0.6 1.1 route.1
  1.7 66.2 %all_to_all.20.x_ref = bf16[32,8,448]{2,1,0:T(8,128)(2,1)S(1)} all-to-all(bf16[32,8,448]{2,1,0:T(8,128)(2,1)S(1)} %get-tuple-element.22), channel_id=1, replica_groups=mesh['grp'=2,'ep'=16,'tp'=8,'mb'=2] {'ep','mb'}, dimensions={0} | all-to-all | bytes 458752 | tf_op jit(solution)/shard_map/all_to_all | solution.py:31
  67.9 0.1 rows.1.refs_8_
  68.0 3.6 %collective-permute-start.7 = (bf16[896,128]{1,0:T(8,128)(2,1)S(1)}, bf16[896,128]{1,0:T(8,128)(2,1)S(1)}, u32[]{:S(2)}, u32[]{:S(2)}) collective-permute-start(bf16[896,128]{1,0:T(8,128)(2,1)S(1)} %rows.1.refs_8_), channel_id=1, source_target_pairs={{0,2},{2,4},{4,6},{6,8},{8,10},{10,12},{12,14},{14,0},{1,3},{3,5},... | collective-permute-start | bytes 688136 | tf_op jit(solution)/shard_map/ppermute | solution.py:512
  71.6 4.1 %collective-permute-start.11 = (bf16[896,128]{1,0:T(8,128)(2,1)S(1)}, bf16[896,128]{1,0:T(8,128)(2,1)S(1)}, u32[]{:S(2)}, u32[]{:S(2)}) collective-permute-start(bf16[896,128]{1,0:T(8,128)(2,1)S(1)} %rows.1.refs_8_), channel_id=1, source_target_pairs={{0,14},{2,0},{4,2},{6,4},{8,6},{10,8},{12,10},{14,12},{1,15},{3,1}... | collective-permute-start | bytes 688136 | tf_op jit(solution)/shard_map/ppermute | solution.py:512
  75.8 3.7 %collective-permute-done.7.refs_9_ = bf16[896,128]{1,0:T(8,128)(2,1)S(1)} collective-permute-done((bf16[896,128]{1,0:T(8,128)(2,1)S(1)}, bf16[896,128]{1,0:T(8,128)(2,1)S(1)}, u32[]{:S(2)}, u32[]{:S(2)}) %collective-permute-start.7) | collective-permute-done | bytes 229408 | tf_op jit(solution)/shard_map/ppermute | solution.py:512
  79.5 1.9 collective-permute-start.8
  81.4 0.0 collective-permute-done.11.refs_16_
  81.4 5.2 %collective-permute-start.12 = (bf16[896,128]{1,0:T(8,128)(2,1)S(1)}, bf16[896,128]{1,0:T(8,128)(2,1)S(1)}, u32[]{:S(2)}, u32[]{:S(2)}) collective-permute-start(bf16[896,128]{1,0:T(8,128)(2,1)S(1)} %collective-permute-done.11.refs_16_), channel_id=1, source_target_pairs={{0,14},{2,0},{4,2},{6,4},{8,6},{10,8},{12,10},{14,12},{1,15},{3,1}... | collective-permute-start | bytes 688136 | tf_op jit(solution)/shard_map/ppermute | solution.py:512
  86.6 1.8 pack.1
  88.4 2.0 collective-permute-start
  90.4 0.0 collective-permute-done.8.refs_10_
  90.4 2.3 %collective-permute-start.9 = (bf16[896,128]{1,0:T(8,128)(2,1)S(1)}, bf16[896,128]{1,0:T(8,128)(2,1)S(1)}, u32[]{:S(2)}, u32[]{:S(2)}) collective-permute-start(bf16[896,128]{1,0:T(8,128)(2,1)S(1)} %collective-permute-done.8.refs_10_), channel_id=1, source_target_pairs={{0,2},{2,4},{4,6},{6,8},{8,10},{10,12},{12,14},{14,0},{1,3},{3,5},... | collective-permute-start | bytes 688136 | tf_op jit(solution)/shard_map/ppermute | solution.py:512
  92.7 0.0 collective-permute-done.12.refs_15_
  92.7 4.8 %collective-permute-start.13 = (bf16[896,128]{1,0:T(8,128)(2,1)S(1)}, bf16[896,128]{1,0:T(8,128)(2,1)S(1)}, u32[]{:S(2)}, u32[]{:S(2)}) collective-permute-start(bf16[896,128]{1,0:T(8,128)(2,1)S(1)} %collective-permute-done.12.refs_15_), channel_id=1, source_target_pairs={{0,14},{2,0},{4,2},{6,4},{8,6},{10,8},{12,10},{14,12},{1,15},{3,1}... | collective-permute-start | bytes 688136 | tf_op jit(solution)/shard_map/ppermute | solution.py:512
  97.5 5.0 %collective-permute-start.1 = (bf16[680,128]{1,0:T(8,128)(2,1)S(1)}, bf16[680,128]{1,0:T(8,128)(2,1)S(1)}, u32[]{:S(2)}, u32[]{:S(2)}) collective-permute-start(bf16[680,128]{1,0:T(8,128)(2,1)S(1)} %get-tuple-element.16), channel_id=1, source_target_pairs={{0,4},{2,6},{4,8},{6,10},{8,12},{10,14},{12,0},{14,2},{1,5},{3,7},... | collective-permute-start | bytes 522248 | tf_op jit(solution)/shard_map/ppermute | solution.py:512
  102.5 3.4 %collective-permute-start.2 = (bf16[680,128]{1,0:T(8,128)(2,1)S(1)}, bf16[680,128]{1,0:T(8,128)(2,1)S(1)}, u32[]{:S(2)}, u32[]{:S(2)}) collective-permute-start(bf16[680,128]{1,0:T(8,128)(2,1)S(1)} %get-tuple-element.17), channel_id=1, source_target_pairs={{0,6},{2,8},{4,10},{6,12},{8,14},{10,0},{12,2},{14,4},{1,7},{3,9},... | collective-permute-start | bytes 522248 | tf_op jit(solution)/shard_map/ppermute | solution.py:512
  105.9 0.0 collective-permute-done.refs_1_
  105.9 3.7 %collective-permute-start.3 = (bf16[680,128]{1,0:T(8,128)(2,1)S(1)}, bf16[680,128]{1,0:T(8,128)(2,1)S(1)}, u32[]{:S(2)}, u32[]{:S(2)}) collective-permute-start(bf16[680,128]{1,0:T(8,128)(2,1)S(1)} %get-tuple-element.18), channel_id=1, source_target_pairs={{0,8},{2,10},{4,12},{6,14},{8,0},{10,2},{12,4},{14,6},{1,9},{3,11}... | collective-permute-start | bytes 522248 | tf_op jit(solution)/shard_map/ppermute | solution.py:512
  109.7 7.4 %collective-permute-done.1.refs_2_ = bf16[680,128]{1,0:T(8,128)(2,1)S(1)} collective-permute-done((bf16[680,128]{1,0:T(8,128)(2,1)S(1)}, bf16[680,128]{1,0:T(8,128)(2,1)S(1)}, u32[]{:S(2)}, u32[]{:S(2)}) %collective-permute-start.1) | collective-permute-done | bytes 174112 | tf_op jit(solution)/shard_map/ppermute | solution.py:512
  117.1 3.9 %collective-permute-start.4 = (bf16[680,128]{1,0:T(8,128)(2,1)S(1)}, bf16[680,128]{1,0:T(8,128)(2,1)S(1)}, u32[]{:S(2)}, u32[]{:S(2)}) collective-permute-start(bf16[680,128]{1,0:T(8,128)(2,1)S(1)} %get-tuple-element.19), channel_id=1, source_target_pairs={{0,10},{2,12},{4,14},{6,0},{8,2},{10,4},{12,6},{14,8},{1,11},{3,13... | collective-permute-start | bytes 522248 | tf_op jit(solution)/shard_map/ppermute | solution.py:512
  121.0 8.0 %collective-permute-start.5 = (bf16[680,128]{1,0:T(8,128)(2,1)S(1)}, bf16[680,128]{1,0:T(8,128)(2,1)S(1)}, u32[]{:S(2)}, u32[]{:S(2)}) collective-permute-start(bf16[680,128]{1,0:T(8,128)(2,1)S(1)} %get-tuple-element.20), channel_id=1, source_target_pairs={{0,12},{2,14},{4,0},{6,2},{8,4},{10,6},{12,8},{14,10},{1,13},{3,15... | collective-permute-start | bytes 522248 | tf_op jit(solution)/shard_map/ppermute | solution.py:512
  129.0 0.0 collective-permute-done.13.refs_14_
  129.0 2.0 collective-permute-start.6
  131.0 0.0 copy-start.4
  131.0 4.0 %collective-permute-start.10 = (bf16[448,128]{1,0:T(8,128)(2,1)S(1)}, bf16[448,128]{1,0:T(8,128)(2,1)S(1)}, u32[]{:S(2)}, u32[]{:S(2)}) collective-permute-start(bf16[448,128]{1,0:T(8,128)(2,1)S(1)} %slice.8), channel_id=1, source_target_pairs={{0,2},{2,4},{4,6},{6,8},{8,10},{10,12},{12,14},{14,0},{1,3},{3,5},... | collective-permute-start | bytes 344072 | tf_op jit(solution)/shard_map/ppermute | solution.py:512
  135.0 0.0 collective-permute-done.3.refs_4_
  135.0 3.2 %collective-permute-start.14 = (bf16[448,128]{1,0:T(8,128)(2,1)S(1)}, bf16[448,128]{1,0:T(8,128)(2,1)S(1)}, u32[]{:S(2)}, u32[]{:S(2)}) collective-permute-start(bf16[448,128]{1,0:T(8,128)(2,1)S(1)} %slice.9), channel_id=1, source_target_pairs={{0,14},{2,0},{4,2},{6,4},{8,6},{10,8},{12,10},{14,12},{1,15},{3,1}... | collective-permute-start | bytes 344072 | tf_op jit(solution)/shard_map/ppermute | solution.py:512
  138.2 0.0 collective-permute-done.4.refs_5_
  138.2 0.2 collective-permute-done.5.refs_6_
  138.4 4.4 %collective-permute-done.6.refs_7_ = bf16[680,128]{1,0:T(8,128)(2,1)S(1)} collective-permute-done((bf16[680,128]{1,0:T(8,128)(2,1)S(1)}, bf16[680,128]{1,0:T(8,128)(2,1)S(1)}, u32[]{:S(2)}, u32[]{:S(2)}) %collective-permute-start.6) | collective-permute-done | bytes 174112 | tf_op jit(solution)/shard_map/ppermute | solution.py:512
  142.8 1.3 attend.1.att_ref
  144.1 0.0 collective-permute-done.14.refs_13_
  144.1 4.3 %units.1 = bf16[8,336,128]{2,1,0:T(8,128)(2,1)} custom-call(s32[1]{0:T(128)} %bitcast.me_ref, bf16[3584,128]{1,0:T(8,128)(2,1)} %bitcast.11, bf16[3584,128]{1,0:T(8,128)(2,1)} %bitcast.12, bf16[8,80,128]{2,1,0:T(8,128)(2,1)S(1)} %attend.1.att_ref, bf16[680,128]{1,0:T(8,128)(2,1)S(1)} %get-tuple-element.14.refs_0_, ...), custom_call_target="tpu_custom_call" | custom-call | tf_op jit(solution)/shard_map/units/pallas_call | solution.py:146
  148.5 4.0 %all-to-all-start.1 = ((bf16[8,336,128]{2,1,0:T(8,128)(2,1)}), bf16[8,336,128]{2,1,0:T(8,128)(2,1)S(1)}, u32[]{:S(2)}, u32[]{:S(2)}) async-start(bf16[8,336,128]{2,1,0:T(8,128)(2,1)} %units.1), calls=%async_computation.1 | async-start | bytes 1376256 | tf_op jit(solution)/shard_map/all_to_all | solution.py:31
  152.4 0.3 columns.1.w_ref
  152.8 19.6 %all-to-all-done.1.u_ref.units_ref = bf16[8,336,128]{2,1,0:T(8,128)(2,1)S(1)} async-done(((bf16[8,336,128]{2,1,0:T(8,128)(2,1)}), bf16[8,336,128]{2,1,0:T(8,128)(2,1)S(1)}, u32[]{:S(2)}, u32[]{:S(2)}) %all-to-all-start.1) | async-done | bytes 688160 | tf_op jit(solution)/shard_map/all_to_all | solution.py:31
  172.3 1.4 down.1
  173.7 4.9 %all-to-all-start.2 = ((bf16[32,8,448]{2,1,0:T(8,128)(2,1)}), bf16[32,8,448]{2,1,0:T(8,128)(2,1)S(1)}, u32[]{:S(2)}, u32[]{:S(2)}) async-start(bf16[32,8,448]{2,1,0:T(8,128)(2,1)} %down.1), calls=%async_computation.2 | async-start | bytes 524288 | tf_op jit(solution)/shard_map/all_to_all | solution.py:31
  178.7 0.0 copy-start.3
  178.7 21.9 %all-to-all-done.2.ret_ref = bf16[32,8,448]{2,1,0:T(8,128)(2,1)S(1)} async-done(((bf16[32,8,448]{2,1,0:T(8,128)(2,1)}), bf16[32,8,448]{2,1,0:T(8,128)(2,1)S(1)}, u32[]{:S(2)}, u32[]{:S(2)}) %all-to-all-start.2) | async-done | bytes 229408 | tf_op jit(solution)/shard_map/all_to_all | solution.py:31
  200.6 1.1 close.1
  201.7 3.7 %all-to-all-start.3 = ((bf16[8,16,640]{2,1,0:T(8,128)(2,1)}), bf16[8,16,640]{2,1,0:T(8,128)(2,1)S(1)}, u32[]{:S(2)}, u32[]{:S(2)}) async-start(bf16[8,16,640]{2,1,0:T(8,128)(2,1)} %get-tuple-element.25), calls=%async_computation.3 | async-start | bytes 327680 | tf_op jit(solution)/shard_map/all_to_all | solution.py:31
  205.4 0.0 copy-start
  205.5 0.1 multiply_sine_fusion
  205.6 0.1 concatenate.3.table_ref
  205.7 8.9 %all-to-all-done.3.all_ref = bf16[8,16,640]{2,1,0:T(8,128)(2,1)S(1)} async-done(((bf16[8,16,640]{2,1,0:T(8,128)(2,1)}), bf16[8,16,640]{2,1,0:T(8,128)(2,1)S(1)}, u32[]{:S(2)}, u32[]{:S(2)}) %all-to-all-start.3) | async-done | bytes 163872 | tf_op jit(solution)/shard_map/all_to_all | solution.py:31
  214.6 1.1 merge.1
  (17 shorter events, 0.1 us)
Async XLA Ops:
  68.0 11.4 %collective-permute-start.7 = (bf16[896,128]{1,0:T(8,128)(2,1)S(1)}, bf16[896,128]{1,0:T(8,128)(2,1)S(1)}, u32[]{:S(2)}, u32[]{:S(2)}) collective-permute-start(bf16[896,128]{1,0:T(8,128)(2,1)S(1)} %rows.1.refs_8_), channel_id=1, source_target_pairs={{0,2},{2,4},{4,6},{6,8},{8,10},{10,12},{12,14},{14,0},{1,3},{3,5},... | collective-permute-start | bytes 688136 | tf_op jit(solution)/shard_map/ppermute | solution.py:512
  71.6 9.8 %collective-permute-start.11 = (bf16[896,128]{1,0:T(8,128)(2,1)S(1)}, bf16[896,128]{1,0:T(8,128)(2,1)S(1)}, u32[]{:S(2)}, u32[]{:S(2)}) collective-permute-start(bf16[896,128]{1,0:T(8,128)(2,1)S(1)} %rows.1.refs_8_), channel_id=1, source_target_pairs={{0,14},{2,0},{4,2},{6,4},{8,6},{10,8},{12,10},{14,12},{1,15},{3,1}... | collective-permute-start | bytes 688136 | tf_op jit(solution)/shard_map/ppermute | solution.py:512
  79.5 10.9 %collective-permute-start.8 = (bf16[896,128]{1,0:T(8,128)(2,1)S(1)}, bf16[896,128]{1,0:T(8,128)(2,1)S(1)}, u32[]{:S(2)}, u32[]{:S(2)}) collective-permute-start(bf16[896,128]{1,0:T(8,128)(2,1)S(1)} %collective-permute-done.7.refs_9_), channel_id=1, source_target_pairs={{0,2},{2,4},{4,6},{6,8},{8,10},{10,12},{12,14},{14,0},{1,3},{3,5},... | collective-permute-start | bytes 688136 | tf_op jit(solution)/shard_map/ppermute | solution.py:512
  81.4 11.3 %collective-permute-start.12 = (bf16[896,128]{1,0:T(8,128)(2,1)S(1)}, bf16[896,128]{1,0:T(8,128)(2,1)S(1)}, u32[]{:S(2)}, u32[]{:S(2)}) collective-permute-start(bf16[896,128]{1,0:T(8,128)(2,1)S(1)} %collective-permute-done.11.refs_16_), channel_id=1, source_target_pairs={{0,14},{2,0},{4,2},{6,4},{8,6},{10,8},{12,10},{14,12},{1,15},{3,1}... | collective-permute-start | bytes 688136 | tf_op jit(solution)/shard_map/ppermute | solution.py:512
  88.4 17.5 %collective-permute-start = (bf16[680,128]{1,0:T(8,128)(2,1)S(1)}, bf16[680,128]{1,0:T(8,128)(2,1)S(1)}, u32[]{:S(2)}, u32[]{:S(2)}) collective-permute-start(bf16[680,128]{1,0:T(8,128)(2,1)S(1)} %get-tuple-element.15), channel_id=1, source_target_pairs={{0,2},{2,4},{4,6},{6,8},{8,10},{10,12},{12,14},{14,0},{1,3},{3,5},... | collective-permute-start | bytes 522248 | tf_op jit(solution)/shard_map/ppermute | solution.py:512
  90.4 30.6 %collective-permute-start.9 = (bf16[896,128]{1,0:T(8,128)(2,1)S(1)}, bf16[896,128]{1,0:T(8,128)(2,1)S(1)}, u32[]{:S(2)}, u32[]{:S(2)}) collective-permute-start(bf16[896,128]{1,0:T(8,128)(2,1)S(1)} %collective-permute-done.8.refs_10_), channel_id=1, source_target_pairs={{0,2},{2,4},{4,6},{6,8},{8,10},{10,12},{12,14},{14,0},{1,3},{3,5},... | collective-permute-start | bytes 688136 | tf_op jit(solution)/shard_map/ppermute | solution.py:512
  92.7 36.3 %collective-permute-start.13 = (bf16[896,128]{1,0:T(8,128)(2,1)S(1)}, bf16[896,128]{1,0:T(8,128)(2,1)S(1)}, u32[]{:S(2)}, u32[]{:S(2)}) collective-permute-start(bf16[896,128]{1,0:T(8,128)(2,1)S(1)} %collective-permute-done.12.refs_15_), channel_id=1, source_target_pairs={{0,14},{2,0},{4,2},{6,4},{8,6},{10,8},{12,10},{14,12},{1,15},{3,1}... | collective-permute-start | bytes 688136 | tf_op jit(solution)/shard_map/ppermute | solution.py:512
  97.5 19.6 %collective-permute-start.1 = (bf16[680,128]{1,0:T(8,128)(2,1)S(1)}, bf16[680,128]{1,0:T(8,128)(2,1)S(1)}, u32[]{:S(2)}, u32[]{:S(2)}) collective-permute-start(bf16[680,128]{1,0:T(8,128)(2,1)S(1)} %get-tuple-element.16), channel_id=1, source_target_pairs={{0,4},{2,6},{4,8},{6,10},{8,12},{10,14},{12,0},{14,2},{1,5},{3,7},... | collective-permute-start | bytes 522248 | tf_op jit(solution)/shard_map/ppermute | solution.py:512
  102.5 28.5 %collective-permute-start.2 = (bf16[680,128]{1,0:T(8,128)(2,1)S(1)}, bf16[680,128]{1,0:T(8,128)(2,1)S(1)}, u32[]{:S(2)}, u32[]{:S(2)}) collective-permute-start(bf16[680,128]{1,0:T(8,128)(2,1)S(1)} %get-tuple-element.17), channel_id=1, source_target_pairs={{0,6},{2,8},{4,10},{6,12},{8,14},{10,0},{12,2},{14,4},{1,7},{3,9},... | collective-permute-start | bytes 522248 | tf_op jit(solution)/shard_map/ppermute | solution.py:512
  105.9 29.1 %collective-permute-start.3 = (bf16[680,128]{1,0:T(8,128)(2,1)S(1)}, bf16[680,128]{1,0:T(8,128)(2,1)S(1)}, u32[]{:S(2)}, u32[]{:S(2)}) collective-permute-start(bf16[680,128]{1,0:T(8,128)(2,1)S(1)} %get-tuple-element.18), channel_id=1, source_target_pairs={{0,8},{2,10},{4,12},{6,14},{8,0},{10,2},{12,4},{14,6},{1,9},{3,11}... | collective-permute-start | bytes 522248 | tf_op jit(solution)/shard_map/ppermute | solution.py:512
  117.1 21.1 %collective-permute-start.4 = (bf16[680,128]{1,0:T(8,128)(2,1)S(1)}, bf16[680,128]{1,0:T(8,128)(2,1)S(1)}, u32[]{:S(2)}, u32[]{:S(2)}) collective-permute-start(bf16[680,128]{1,0:T(8,128)(2,1)S(1)} %get-tuple-element.19), channel_id=1, source_target_pairs={{0,10},{2,12},{4,14},{6,0},{8,2},{10,4},{12,6},{14,8},{1,11},{3,13... | collective-permute-start | bytes 522248 | tf_op jit(solution)/shard_map/ppermute | solution.py:512
  121.0 17.4 %collective-permute-start.5 = (bf16[680,128]{1,0:T(8,128)(2,1)S(1)}, bf16[680,128]{1,0:T(8,128)(2,1)S(1)}, u32[]{:S(2)}, u32[]{:S(2)}) collective-permute-start(bf16[680,128]{1,0:T(8,128)(2,1)S(1)} %get-tuple-element.20), channel_id=1, source_target_pairs={{0,12},{2,14},{4,0},{6,2},{8,4},{10,6},{12,8},{14,10},{1,13},{3,15... | collective-permute-start | bytes 522248 | tf_op jit(solution)/shard_map/ppermute | solution.py:512
  129.0 13.8 %collective-permute-start.6 = (bf16[680,128]{1,0:T(8,128)(2,1)S(1)}, bf16[680,128]{1,0:T(8,128)(2,1)S(1)}, u32[]{:S(2)}, u32[]{:S(2)}) collective-permute-start(bf16[680,128]{1,0:T(8,128)(2,1)S(1)} %get-tuple-element.21), channel_id=1, source_target_pairs={{0,14},{2,0},{4,2},{6,4},{8,6},{10,8},{12,10},{14,12},{1,15},{3,1}... | collective-permute-start | bytes 522248 | tf_op jit(solution)/shard_map/ppermute | solution.py:512
  131.0 11.8 %copy-start.4 = (s32[16]{0:T(128)S(1)}, s32[16]{0:T(128)}, u32[]{:S(2)}) copy-start(s32[16]{0:T(128)} %len_ref.1) | copy-start | bytes 196
  131.0 13.1 %collective-permute-start.10 = (bf16[448,128]{1,0:T(8,128)(2,1)S(1)}, bf16[448,128]{1,0:T(8,128)(2,1)S(1)}, u32[]{:S(2)}, u32[]{:S(2)}) collective-permute-start(bf16[448,128]{1,0:T(8,128)(2,1)S(1)} %slice.8), channel_id=1, source_target_pairs={{0,2},{2,4},{4,6},{6,8},{8,10},{10,12},{12,14},{14,0},{1,3},{3,5},... | collective-permute-start | bytes 344072 | tf_op jit(solution)/shard_map/ppermute | solution.py:512
  135.0 9.1 %collective-permute-start.14 = (bf16[448,128]{1,0:T(8,128)(2,1)S(1)}, bf16[448,128]{1,0:T(8,128)(2,1)S(1)}, u32[]{:S(2)}, u32[]{:S(2)}) collective-permute-start(bf16[448,128]{1,0:T(8,128)(2,1)S(1)} %slice.9), channel_id=1, source_target_pairs={{0,14},{2,0},{4,2},{6,4},{8,6},{10,8},{12,10},{14,12},{1,15},{3,1}... | collective-permute-start | bytes 344072 | tf_op jit(solution)/shard_map/ppermute | solution.py:512
  148.5 23.9 %all-to-all-start.1 = ((bf16[8,336,128]{2,1,0:T(8,128)(2,1)}), bf16[8,336,128]{2,1,0:T(8,128)(2,1)S(1)}, u32[]{:S(2)}, u32[]{:S(2)}) async-start(bf16[8,336,128]{2,1,0:T(8,128)(2,1)} %units.1), calls=%async_computation.1 | async-start | bytes 1376256 | tf_op jit(solution)/shard_map/all_to_all | solution.py:31
  172.3 28.3 %copy-start.1 = (bf16[448,576]{1,0:T(8,128)(2,1)S(1)}, bf16[448,576]{1,0:T(8,128)(2,1)}, u32[]{:S(2)}) copy-start(bf16[448,576]{1,0:T(8,128)(2,1)} %wdkv_ref.1) | copy-start | bytes 1548292
  173.7 26.9 %copy-start.2 = (bf16[16,448]{1,0:T(8,128)(2,1)S(1)}, bf16[16,448]{1,0:T(8,128)(2,1)}, u32[]{:S(2)}) copy-start(bf16[16,448]{1,0:T(8,128)(2,1)} %hid_ref.1) | copy-start | bytes 43012
  173.7 26.9 %all-to-all-start.2 = ((bf16[32,8,448]{2,1,0:T(8,128)(2,1)}), bf16[32,8,448]{2,1,0:T(8,128)(2,1)S(1)}, u32[]{:S(2)}, u32[]{:S(2)}) async-start(bf16[32,8,448]{2,1,0:T(8,128)(2,1)} %down.1), calls=%async_computation.2 | async-start | bytes 524288 | tf_op jit(solution)/shard_map/all_to_all | solution.py:31
  178.7 22.0 %copy-start.3 = (f32[448]{0:T(512)S(1)}, f32[448]{0:T(512)}, u32[]{:S(2)}) copy-start(f32[448]{0:T(512)} %param.22) | copy-start | bytes 5380
  201.7 3.9 %copy-start.5 = (f32[512]{0:T(512)S(1)}, f32[512]{0:T(512)}, u32[]{:S(2)}) copy-start(f32[512]{0:T(512)} %param.24) | copy-start | bytes 6148
  201.7 12.9 %all-to-all-start.3 = ((bf16[8,16,640]{2,1,0:T(8,128)(2,1)}), bf16[8,16,640]{2,1,0:T(8,128)(2,1)S(1)}, u32[]{:S(2)}, u32[]{:S(2)}) async-start(bf16[8,16,640]{2,1,0:T(8,128)(2,1)} %get-tuple-element.25), calls=%async_computation.3 | async-start | bytes 327680 | tf_op jit(solution)/shard_map/all_to_all | solution.py:31
  205.4 9.2 %copy-start = (bf16[16,8,576]{2,1,0:T(8,128)(2,1)S(1)}, bf16[16,8,576]{2,1,0:T(8,128)(2,1)}, u32[]{:S(2)}) copy-start(bf16[16,8,576]{2,1,0:T(8,128)(2,1)} %q_ref.1) | copy-start | bytes 442372

commit v8 on v7

--- a/solution.py
+++ b/solution.py
@@ -45,11 +45,7 @@
     return copies
 
 
-def route_kernel(ids_hbm, slots_hbm, aff_hbm, hid_hbm, send_ref, comb_ref, *refs):
-    ids_ref, slots_ref, aff_ref, hid_ref, sems = refs
-    copies = fetch((ids_hbm, slots_hbm, aff_hbm, hid_hbm), refs[:4], sems)
-    for copy in copies:
-        copy.wait()
+def route_into(ids_ref, slots_ref, aff_ref, hid_ref, send_ref, comb_ref):
     experts = send_ref.shape[0]
     top, tokens = ids_ref.shape
     rows = experts * CAP
@@ -69,21 +65,6 @@
     send_ref[...] = sent.reshape(send_ref.shape).astype(bf16)
 
 
-def route(expert_ids, slots, affinity, hidden, experts):
-    tokens, width = hidden.shape
-    inputs = (expert_ids.T, slots.T, affinity.T, hidden)
-    return pl.pallas_call(
-        route_kernel,
-        out_shape=(shape((experts, CAP, width), bf16), shape((experts * CAP, tokens), f32)),
-        in_specs=[HBM] * 4,
-        out_specs=(VMEM, VMEM),
-        scratch_shapes=[pltpu.VMEM(x.shape, x.dtype) for x in inputs]
-        + [pltpu.SemaphoreType.DMA((4,))],
-        compiler_params=PARAMS,
-        name="route",
-    )(*[in_hbm(x) for x in inputs])
-
-
 def gain_of(block, at, width):
     rows = block[at : at + 16, :].astype(f32)
     tiles = (width + 127) // 128
@@ -94,8 +75,9 @@
 def units_kernel(me_ref, wg_hbm, wu_hbm, att_ref, *refs):
     peers = att_ref.shape[0]
     blocks, parts = refs[:peers], refs[peers : 2 * peers + 1]
-    o_ref, wg_ref, wu_ref, n_ref, g_ref, u_ref, sems = refs[2 * peers + 1 :]
-    copies = fetch((wg_hbm, wu_hbm), (wg_ref, wu_ref), sems)
+    o_ref, w_ref, n_ref, h_ref, sems = refs[2 * peers + 1 :]
+    hid = wg_hbm.shape[1]
+    copies = fetch((wg_hbm, wu_hbm), (w_ref.at[:, :hid], w_ref.at[:, hid:]), sems)
     _, rows, cols = n_ref.shape
     middle, tiles = peers // 2, cols // 128
     square = jnp.zeros((rows, 1), f32)
@@ -116,25 +98,21 @@
                 at, done = at + take, done + take
         x = n_ref[k].astype(f32)
         square = square + jnp.sum(x * x, -1, keepdims=True)
-    scale = lax.rsqrt(square / D + epsilon)
-    copies[0].wait()
-    copies[1].wait()
-    for k in range(peers):
         j = lax.rem(me_ref[0] + (peers - k), peers)
         gain = jnp.concatenate(gain_of(blocks[k], blocks[k].shape[0] - 16, cols), 1)
-        normed = (n_ref[k].astype(f32) * scale * gain).astype(bf16)
+        if k == 0:
+            copies[0].wait()
+            copies[1].wait()
         part = pl.ds(pl.multiple_of(j * cols, 64), cols)
-        gate = jnp.dot(normed, wg_ref[part, :], preferred_element_type=f32)
-        up = jnp.dot(normed, wu_ref[part, :], preferred_element_type=f32)
+        both = jnp.dot((x * gain).astype(bf16), w_ref[part, :], preferred_element_type=f32)
         if k == 0:
-            g_ref[...] = gate
-            u_ref[...] = up
+            h_ref[...] = both
         else:
-            g_ref[...] += gate
-            u_ref[...] += up
+            h_ref[...] += both
         o_ref[j, rows:, :] = att_ref[k]
-    gate = g_ref[...]
-    units = (gate / (1.0 + jnp.exp(-gate)) * u_ref[...]).astype(bf16)
+    scale = lax.rsqrt(square / D + epsilon)
+    gate = h_ref[:, :hid] * scale
+    units = (gate / (1.0 + jnp.exp(-gate)) * (h_ref[:, hid:] * scale)).astype(bf16)
     for j in range(peers):
         o_ref[j, :rows, :] = units
 
@@ -149,11 +127,9 @@
         in_specs=[SMEM, HBM, HBM] + [VMEM] * (2 * peers + 2),
         out_specs=VMEM,
         scratch_shapes=[
-            pltpu.VMEM(w_gate.shape, bf16),
-            pltpu.VMEM(w_up.shape, bf16),
+            pltpu.VMEM((w_gate.shape[0], 2 * hid), bf16),
             pltpu.VMEM((peers, rows, cols), bf16),
-            pltpu.VMEM((rows, hid), f32),
-            pltpu.VMEM((rows, hid), f32),
+            pltpu.VMEM((rows, 2 * hid), f32),
             pltpu.SemaphoreType.DMA((2,)),
         ],
         compiler_params=PARAMS,
@@ -161,11 +137,12 @@
     )(me, in_hbm(w_gate), in_hbm(w_up), attended, *blocks, *parts)
 
 
-def pack_kernel(me_ref, wd_hbm, cache_hbm, q_hbm, gain_hbm, *refs):
-    outs, (wd_ref, cache_ref, q_ref, gain_ref, tiles_ref, keys_ref, sems) = refs[:-7], refs[-7:]
-    copies = fetch(
-        (wd_hbm, cache_hbm, q_hbm, gain_hbm), (wd_ref, cache_ref, q_ref, gain_ref), sems
-    )
+def pack_kernel(me_ref, *refs):
+    inputs, outs, scratch = refs[:8], refs[8:-11], refs[-11:]
+    copies = fetch(inputs, scratch[:8], scratch[10])
+    wd_ref, cache_ref, q_ref, gain_ref = scratch[:4]
+    tiles_ref, keys_ref = scratch[8:10]
+    outs, send_ref, comb_ref = outs[:-2], outs[-2], outs[-1]
     peers = len(outs)
     half, double = tiles_ref.shape[1:]
     width = double // 2
@@ -204,30 +181,33 @@
             outs[k][at : at + span + heads, :] = keys_ref[:, 128 * t : 128 * (t + 1)]
             at += span + heads
         outs[k][at : at + 16, :] = packed
-
-
-def pack(me, w_down, cache, queries, gain, peers):
+    for copy in copies[4:]:
+        copy.wait()
+    route_into(*scratch[4:8], send_ref, comb_ref)
+
+
+def pack(me, w_down, cache, queries, gain, expert_ids, slots, affinity, hidden, peers, experts):
     hid, width = w_down.shape[0], w_down.shape[1] // peers
     seqs, span, keys = cache.shape
     own, heads = seqs // peers, queries.shape[1]
     rows = hid * width // 128 + own * (span + heads) * keys // 128 + 16
-    return pl.pallas_call(
+    inputs = (w_down, cache, queries, gain, expert_ids.T, slots.T, affinity.T, hidden)
+    *blocks, send_rows, combine = pl.pallas_call(
         pack_kernel,
-        out_shape=tuple(shape((rows, 128), bf16) for _ in range(peers)),
-        in_specs=[SMEM] + [HBM] * 4,
-        out_specs=tuple(VMEM for _ in range(peers)),
-        scratch_shapes=[
-            pltpu.VMEM(w_down.shape, bf16),
-            pltpu.VMEM(cache.shape, bf16),
-            pltpu.VMEM(queries.shape, bf16),
-            pltpu.VMEM(gain.shape, f32),
+        out_shape=tuple(shape((rows, 128), bf16) for _ in range(peers))
+        + (shape((experts, CAP, width), bf16), shape((experts * CAP, seqs), f32)),
+        in_specs=[SMEM] + [HBM] * len(inputs),
+        out_specs=tuple(VMEM for _ in range(peers + 2)),
+        scratch_shapes=[pltpu.VMEM(x.shape, x.dtype) for x in inputs]
+        + [
             pltpu.VMEM((peers, hid // 2, 2 * width), bf16),
             pltpu.VMEM((span + heads, own * keys), bf16),
-            pltpu.SemaphoreType.DMA((4,)),
+            pltpu.SemaphoreType.DMA((len(inputs),)),
         ],
         compiler_params=PARAMS,
         name="pack",
-    )(me, in_hbm(w_down), in_hbm(cache), in_hbm(queries), in_hbm(gain))
+    )(me, *[in_hbm(x) for x in inputs])
+    return blocks, send_rows, combine
 
 
 def rows_kernel(x_ref, o_ref):
@@ -511,9 +491,20 @@
     def moved(x, k):
         return lax.ppermute(x, "tp", [(i, (i + k) % peers) for i in range(peers)])
 
-    send_rows, combine = route(expert_ids, slots, affinity, hidden, experts)
+    blocks, send_rows, combine = pack(
+        me,
+        w_down[0],
+        cache,
+        queries,
+        moe_gain[None],
+        expert_ids,
+        slots,
+        affinity,
+        hidden,
+        peers,
+        experts,
+    )
     arrived = exchange(send_rows, ("ep", "mb"))
-    blocks = list(pack(me, w_down[0], cache, queries, moe_gain[None], peers))
     for k in MOVES:
         blocks[k] = moved(blocks[k], k)
     parts = ring(packed_rows(arrived), moved, peers)

time: 217 us -> 216 us (level)
  waiting for transfers between devices: 66.2 us -> 69.6 us
    ppermute x15, waiting for transfers between devices: 15.7 us -> 18.5 us  [moved(): return lax.ppermute(x, 'tp', [(i, (i + k) % peers) for i in range(peers)])]
  transfers between devices with their start and end apart: 18 -> 18, of which waited for: 7 -> 8; matrix products, arithmetic and copies ran while one was open for 0% -> 0% of each run, Pallas kernels for 2% -> 1%
where the time goes in v8:
time: 216 us; the launch traced here: 215 us
  waiting for transfers between devices  69.6 us (32%)
  starting transfers between devices  67.5 us (31%)
  blocking collectives  66.2 us (31%)
  Pallas kernels  10.8 us (5%)
    all_to_all x1, blocking collectives, exchange(): return lax.all_to_all(x, axis, split_axis=0, concat_axis=0, tiled=True)  66.2 us
    ppermute x15, starting transfers between devices, moved(): return lax.ppermute(x, 'tp', [(i, (i + k) % peers) for i in range(peers)])  54.8 us
    all_to_all x3, waiting for transfers between devices, exchange(): return lax.all_to_all(x, axis, split_axis=0, concat_axis=0, tiled=True)  51.1 us
    ppermute x15, waiting for transfers between devices, moved(): return lax.ppermute(x, 'tp', [(i, (i + k) % peers) for i in range(peers)])  18.5 us
    all_to_all x3, starting transfers between devices, exchange(): return lax.all_to_all(x, axis, split_axis=0, concat_axis=0, tiled=True)  12.7 us
  transfers between devices with their start and end apart: 18, of which 8 were waited for; matrix products, arithmetic and copies ran while one was open for 0% of the time, Pallas kernels for 1%

profile of v8, /device:TPU:80, one launch (start us, length us, event | category | flops | bytes accessed | tf_op | source)
XLA Modules:
  0.0 215.3 jit_solution(9884859315191038684)
XLA Ops:
  0.6 2.1 pack.1
  2.7 66.2 %all_to_all.20.x_ref = bf16[32,8,448]{2,1,0:T(8,128)(2,1)S(1)} all-to-all(bf16[32,8,448]{2,1,0:T(8,128)(2,1)S(1)} %get-tuple-element.22), channel_id=1, replica_groups=mesh['grp'=2,'ep'=16,'tp'=8,'mb'=2] {'ep','mb'}, dimensions={0} | all-to-all | bytes 458752 | tf_op jit(solution)/shard_map/all_to_all | solution.py:31
  69.0 0.1 rows.1.refs_8_
  69.1 3.6 %collective-permute-start.7 = (bf16[896,128]{1,0:T(8,128)(2,1)S(1)}, bf16[896,128]{1,0:T(8,128)(2,1)S(1)}, u32[]{:S(2)}, u32[]{:S(2)}) collective-permute-start(bf16[896,128]{1,0:T(8,128)(2,1)S(1)} %rows.1.refs_8_), channel_id=1, source_target_pairs={{0,2},{2,4},{4,6},{6,8},{8,10},{10,12},{12,14},{14,0},{1,3},{3,5},... | collective-permute-start | bytes 688136 | tf_op jit(solution)/shard_map/ppermute | solution.py:492
  72.6 4.1 %collective-permute-start.11 = (bf16[896,128]{1,0:T(8,128)(2,1)S(1)}, bf16[896,128]{1,0:T(8,128)(2,1)S(1)}, u32[]{:S(2)}, u32[]{:S(2)}) collective-permute-start(bf16[896,128]{1,0:T(8,128)(2,1)S(1)} %rows.1.refs_8_), channel_id=1, source_target_pairs={{0,14},{2,0},{4,2},{6,4},{8,6},{10,8},{12,10},{14,12},{1,15},{3,1}... | collective-permute-start | bytes 688136 | tf_op jit(solution)/shard_map/ppermute | solution.py:492
  76.8 3.7 %collective-permute-done.7.refs_9_ = bf16[896,128]{1,0:T(8,128)(2,1)S(1)} collective-permute-done((bf16[896,128]{1,0:T(8,128)(2,1)S(1)}, bf16[896,128]{1,0:T(8,128)(2,1)S(1)}, u32[]{:S(2)}, u32[]{:S(2)}) %collective-permute-start.7) | collective-permute-done | bytes 229408 | tf_op jit(solution)/shard_map/ppermute | solution.py:492
  80.5 1.9 collective-permute-start.8
  82.5 0.0 collective-permute-done.11.refs_16_
  82.5 5.2 %collective-permute-start.12 = (bf16[896,128]{1,0:T(8,128)(2,1)S(1)}, bf16[896,128]{1,0:T(8,128)(2,1)S(1)}, u32[]{:S(2)}, u32[]{:S(2)}) collective-permute-start(bf16[896,128]{1,0:T(8,128)(2,1)S(1)} %collective-permute-done.11.refs_16_), channel_id=1, source_target_pairs={{0,14},{2,0},{4,2},{6,4},{8,6},{10,8},{12,10},{14,12},{1,15},{3,1}... | collective-permute-start | bytes 688136 | tf_op jit(solution)/shard_map/ppermute | solution.py:492
  87.6 2.0 collective-permute-start
  89.6 0.9 collective-permute-done.8.refs_10_
  90.5 1.9 collective-permute-start.9
  92.4 0.0 collective-permute-done.12.refs_15_
  92.4 5.2 %collective-permute-start.13 = (bf16[896,128]{1,0:T(8,128)(2,1)S(1)}, bf16[896,128]{1,0:T(8,128)(2,1)S(1)}, u32[]{:S(2)}, u32[]{:S(2)}) collective-permute-start(bf16[896,128]{1,0:T(8,128)(2,1)S(1)} %collective-permute-done.12.refs_15_), channel_id=1, source_target_pairs={{0,14},{2,0},{4,2},{6,4},{8,6},{10,8},{12,10},{14,12},{1,15},{3,1}... | collective-permute-start | bytes 688136 | tf_op jit(solution)/shard_map/ppermute | solution.py:492
  97.6 4.1 %collective-permute-start.1 = (bf16[680,128]{1,0:T(8,128)(2,1)S(1)}, bf16[680,128]{1,0:T(8,128)(2,1)S(1)}, u32[]{:S(2)}, u32[]{:S(2)}) collective-permute-start(bf16[680,128]{1,0:T(8,128)(2,1)S(1)} %get-tuple-element.16), channel_id=1, source_target_pairs={{0,4},{2,6},{4,8},{6,10},{8,12},{10,14},{12,0},{14,2},{1,5},{3,7},... | collective-permute-start | bytes 522248 | tf_op jit(solution)/shard_map/ppermute | solution.py:492
  101.7 3.4 %collective-permute-start.2 = (bf16[680,128]{1,0:T(8,128)(2,1)S(1)}, bf16[680,128]{1,0:T(8,128)(2,1)S(1)}, u32[]{:S(2)}, u32[]{:S(2)}) collective-permute-start(bf16[680,128]{1,0:T(8,128)(2,1)S(1)} %get-tuple-element.17), channel_id=1, source_target_pairs={{0,6},{2,8},{4,10},{6,12},{8,14},{10,0},{12,2},{14,4},{1,7},{3,9},... | collective-permute-start | bytes 522248 | tf_op jit(solution)/shard_map/ppermute | solution.py:492
  105.2 0.0 collective-permute-done.refs_1_
  105.2 3.7 %collective-permute-start.3 = (bf16[680,128]{1,0:T(8,128)(2,1)S(1)}, bf16[680,128]{1,0:T(8,128)(2,1)S(1)}, u32[]{:S(2)}, u32[]{:S(2)}) collective-permute-start(bf16[680,128]{1,0:T(8,128)(2,1)S(1)} %get-tuple-element.18), channel_id=1, source_target_pairs={{0,8},{2,10},{4,12},{6,14},{8,0},{10,2},{12,4},{14,6},{1,9},{3,11}... | collective-permute-start | bytes 522248 | tf_op jit(solution)/shard_map/ppermute | solution.py:492
  108.9 8.7 %collective-permute-done.1.refs_2_ = bf16[680,128]{1,0:T(8,128)(2,1)S(1)} collective-permute-done((bf16[680,128]{1,0:T(8,128)(2,1)S(1)}, bf16[680,128]{1,0:T(8,128)(2,1)S(1)}, u32[]{:S(2)}, u32[]{:S(2)}) %collective-permute-start.1) | collective-permute-done | bytes 174112 | tf_op jit(solution)/shard_map/ppermute | solution.py:492
  117.6 2.5 %collective-permute-start.4 = (bf16[680,128]{1,0:T(8,128)(2,1)S(1)}, bf16[680,128]{1,0:T(8,128)(2,1)S(1)}, u32[]{:S(2)}, u32[]{:S(2)}) collective-permute-start(bf16[680,128]{1,0:T(8,128)(2,1)S(1)} %get-tuple-element.19), channel_id=1, source_target_pairs={{0,10},{2,12},{4,14},{6,0},{8,2},{10,4},{12,6},{14,8},{1,11},{3,13... | collective-permute-start | bytes 522248 | tf_op jit(solution)/shard_map/ppermute | solution.py:492
  120.2 0.0 collective-permute-done.9.refs_11_
  120.2 8.1 %collective-permute-start.5 = (bf16[680,128]{1,0:T(8,128)(2,1)S(1)}, bf16[680,128]{1,0:T(8,128)(2,1)S(1)}, u32[]{:S(2)}, u32[]{:S(2)}) collective-permute-start(bf16[680,128]{1,0:T(8,128)(2,1)S(1)} %get-tuple-element.20), channel_id=1, source_target_pairs={{0,12},{2,14},{4,0},{6,2},{8,4},{10,6},{12,8},{14,10},{1,13},{3,15... | collective-permute-start | bytes 522248 | tf_op jit(solution)/shard_map/ppermute | solution.py:492
  128.3 0.0 collective-permute-done.13.refs_14_
  128.3 2.0 collective-permute-start.6
  130.3 0.0 copy-start.4
  130.3 0.0 collective-permute-done.2.refs_3_
  130.3 4.0 %collective-permute-start.10 = (bf16[448,128]{1,0:T(8,128)(2,1)S(1)}, bf16[448,128]{1,0:T(8,128)(2,1)S(1)}, u32[]{:S(2)}, u32[]{:S(2)}) collective-permute-start(bf16[448,128]{1,0:T(8,128)(2,1)S(1)} %slice.8), channel_id=1, source_target_pairs={{0,2},{2,4},{4,6},{6,8},{8,10},{10,12},{12,14},{14,0},{1,3},{3,5},... | collective-permute-start | bytes 344072 | tf_op jit(solution)/shard_map/ppermute | solution.py:492
  134.2 0.0 collective-permute-done.3.refs_4_
  134.3 3.2 %collective-permute-start.14 = (bf16[448,128]{1,0:T(8,128)(2,1)S(1)}, bf16[448,128]{1,0:T(8,128)(2,1)S(1)}, u32[]{:S(2)}, u32[]{:S(2)}) collective-permute-start(bf16[448,128]{1,0:T(8,128)(2,1)S(1)} %slice.9), channel_id=1, source_target_pairs={{0,14},{2,0},{4,2},{6,4},{8,6},{10,8},{12,10},{14,12},{1,15},{3,1}... | collective-permute-start | bytes 344072 | tf_op jit(solution)/shard_map/ppermute | solution.py:492
  137.4 0.5 collective-permute-done.5.refs_6_
  137.9 4.6 %collective-permute-done.6.refs_7_ = bf16[680,128]{1,0:T(8,128)(2,1)S(1)} collective-permute-done((bf16[680,128]{1,0:T(8,128)(2,1)S(1)}, bf16[680,128]{1,0:T(8,128)(2,1)S(1)}, u32[]{:S(2)}, u32[]{:S(2)}) %collective-permute-start.6) | collective-permute-done | bytes 174112 | tf_op jit(solution)/shard_map/ppermute | solution.py:492
  142.6 1.3 attend.1.att_ref
  143.9 0.0 collective-permute-done.10.refs_12_
  143.9 3.4 %units.1 = bf16[8,336,128]{2,1,0:T(8,128)(2,1)} custom-call(s32[1]{0:T(128)} %bitcast.me_ref, bf16[3584,128]{1,0:T(8,128)(2,1)} %bitcast.11, bf16[3584,128]{1,0:T(8,128)(2,1)} %bitcast.12, bf16[8,80,128]{2,1,0:T(8,128)(2,1)S(1)} %attend.1.att_ref, bf16[680,128]{1,0:T(8,128)(2,1)S(1)} %get-tuple-element.14.refs_0_, ...), custom_call_target="tpu_custom_call" | custom-call | tf_op jit(solution)/shard_map/units/pallas_call | solution.py:124
  147.4 3.9 %all-to-all-start.1 = ((bf16[8,336,128]{2,1,0:T(8,128)(2,1)}), bf16[8,336,128]{2,1,0:T(8,128)(2,1)S(1)}, u32[]{:S(2)}, u32[]{:S(2)}) async-start(bf16[8,336,128]{2,1,0:T(8,128)(2,1)} %units.1), calls=%async_computation.1 | async-start | bytes 1376256 | tf_op jit(solution)/shard_map/all_to_all | solution.py:31
  151.3 0.3 columns.1.w_ref
  151.6 19.5 %all-to-all-done.1.u_ref.units_ref = bf16[8,336,128]{2,1,0:T(8,128)(2,1)S(1)} async-done(((bf16[8,336,128]{2,1,0:T(8,128)(2,1)}), bf16[8,336,128]{2,1,0:T(8,128)(2,1)S(1)}, u32[]{:S(2)}, u32[]{:S(2)}) %all-to-all-start.1) | async-done | bytes 688160 | tf_op jit(solution)/shard_map/all_to_all | solution.py:31
  171.1 1.4 down.1
  172.5 5.0 %all-to-all-start.2 = ((bf16[32,8,448]{2,1,0:T(8,128)(2,1)}), bf16[32,8,448]{2,1,0:T(8,128)(2,1)S(1)}, u32[]{:S(2)}, u32[]{:S(2)}) async-start(bf16[32,8,448]{2,1,0:T(8,128)(2,1)} %down.1), calls=%async_computation.2 | async-start | bytes 524288 | tf_op jit(solution)/shard_map/all_to_all | solution.py:31
  177.5 0.0 copy-start.3
  177.5 22.0 %all-to-all-done.2.ret_ref = bf16[32,8,448]{2,1,0:T(8,128)(2,1)S(1)} async-done(((bf16[32,8,448]{2,1,0:T(8,128)(2,1)}), bf16[32,8,448]{2,1,0:T(8,128)(2,1)S(1)}, u32[]{:S(2)}, u32[]{:S(2)}) %all-to-all-start.2) | async-done | bytes 229408 | tf_op jit(solution)/shard_map/all_to_all | solution.py:31
  199.5 1.1 close.1
  200.6 3.7 %all-to-all-start.3 = ((bf16[8,16,640]{2,1,0:T(8,128)(2,1)}), bf16[8,16,640]{2,1,0:T(8,128)(2,1)S(1)}, u32[]{:S(2)}, u32[]{:S(2)}) async-start(bf16[8,16,640]{2,1,0:T(8,128)(2,1)} %get-tuple-element.25), calls=%async_computation.3 | async-start | bytes 327680 | tf_op jit(solution)/shard_map/all_to_all | solution.py:31
  204.3 0.0 copy-start
  204.3 0.1 multiply_sine_fusion
  204.5 0.1 concatenate.3.table_ref
  204.6 9.6 %all-to-all-done.3.all_ref = bf16[8,16,640]{2,1,0:T(8,128)(2,1)S(1)} async-done(((bf16[8,16,640]{2,1,0:T(8,128)(2,1)}), bf16[8,16,640]{2,1,0:T(8,128)(2,1)S(1)}, u32[]{:S(2)}, u32[]{:S(2)}) %all-to-all-start.3) | async-done | bytes 163872 | tf_op jit(solution)/shard_map/all_to_all | solution.py:31
  214.2 1.1 merge.1
  (16 shorter events, 0.1 us)
Async XLA Ops:
  69.1 11.4 %collective-permute-start.7 = (bf16[896,128]{1,0:T(8,128)(2,1)S(1)}, bf16[896,128]{1,0:T(8,128)(2,1)S(1)}, u32[]{:S(2)}, u32[]{:S(2)}) collective-permute-start(bf16[896,128]{1,0:T(8,128)(2,1)S(1)} %rows.1.refs_8_), channel_id=1, source_target_pairs={{0,2},{2,4},{4,6},{6,8},{8,10},{10,12},{12,14},{14,0},{1,3},{3,5},... | collective-permute-start | bytes 688136 | tf_op jit(solution)/shard_map/ppermute | solution.py:492
  72.6 9.8 %collective-permute-start.11 = (bf16[896,128]{1,0:T(8,128)(2,1)S(1)}, bf16[896,128]{1,0:T(8,128)(2,1)S(1)}, u32[]{:S(2)}, u32[]{:S(2)}) collective-permute-start(bf16[896,128]{1,0:T(8,128)(2,1)S(1)} %rows.1.refs_8_), channel_id=1, source_target_pairs={{0,14},{2,0},{4,2},{6,4},{8,6},{10,8},{12,10},{14,12},{1,15},{3,1}... | collective-permute-start | bytes 688136 | tf_op jit(solution)/shard_map/ppermute | solution.py:492
  80.5 10.0 %collective-permute-start.8 = (bf16[896,128]{1,0:T(8,128)(2,1)S(1)}, bf16[896,128]{1,0:T(8,128)(2,1)S(1)}, u32[]{:S(2)}, u32[]{:S(2)}) collective-permute-start(bf16[896,128]{1,0:T(8,128)(2,1)S(1)} %collective-permute-done.7.refs_9_), channel_id=1, source_target_pairs={{0,2},{2,4},{4,6},{6,8},{8,10},{10,12},{12,14},{14,0},{1,3},{3,5},... | collective-permute-start | bytes 688136 | tf_op jit(solution)/shard_map/ppermute | solution.py:492
  82.5 10.0 %collective-permute-start.12 = (bf16[896,128]{1,0:T(8,128)(2,1)S(1)}, bf16[896,128]{1,0:T(8,128)(2,1)S(1)}, u32[]{:S(2)}, u32[]{:S(2)}) collective-permute-start(bf16[896,128]{1,0:T(8,128)(2,1)S(1)} %collective-permute-done.11.refs_16_), channel_id=1, source_target_pairs={{0,14},{2,0},{4,2},{6,4},{8,6},{10,8},{12,10},{14,12},{1,15},{3,1}... | collective-permute-start | bytes 688136 | tf_op jit(solution)/shard_map/ppermute | solution.py:492
  87.6 17.5 %collective-permute-start = (bf16[680,128]{1,0:T(8,128)(2,1)S(1)}, bf16[680,128]{1,0:T(8,128)(2,1)S(1)}, u32[]{:S(2)}, u32[]{:S(2)}) collective-permute-start(bf16[680,128]{1,0:T(8,128)(2,1)S(1)} %get-tuple-element.15), channel_id=1, source_target_pairs={{0,2},{2,4},{4,6},{6,8},{8,10},{10,12},{12,14},{14,0},{1,3},{3,5},... | collective-permute-start | bytes 522248 | tf_op jit(solution)/shard_map/ppermute | solution.py:492
  90.5 29.7 %collective-permute-start.9 = (bf16[896,128]{1,0:T(8,128)(2,1)S(1)}, bf16[896,128]{1,0:T(8,128)(2,1)S(1)}, u32[]{:S(2)}, u32[]{:S(2)}) collective-permute-start(bf16[896,128]{1,0:T(8,128)(2,1)S(1)} %collective-permute-done.8.refs_10_), channel_id=1, source_target_pairs={{0,2},{2,4},{4,6},{6,8},{8,10},{10,12},{12,14},{14,0},{1,3},{3,5},... | collective-permute-start | bytes 688136 | tf_op jit(solution)/shard_map/ppermute | solution.py:492
  92.4 35.8 %collective-permute-start.13 = (bf16[896,128]{1,0:T(8,128)(2,1)S(1)}, bf16[896,128]{1,0:T(8,128)(2,1)S(1)}, u32[]{:S(2)}, u32[]{:S(2)}) collective-permute-start(bf16[896,128]{1,0:T(8,128)(2,1)S(1)} %collective-permute-done.12.refs_15_), channel_id=1, source_target_pairs={{0,14},{2,0},{4,2},{6,4},{8,6},{10,8},{12,10},{14,12},{1,15},{3,1}... | collective-permute-start | bytes 688136 | tf_op jit(solution)/shard_map/ppermute | solution.py:492
  97.6 20.0 %collective-permute-start.1 = (bf16[680,128]{1,0:T(8,128)(2,1)S(1)}, bf16[680,128]{1,0:T(8,128)(2,1)S(1)}, u32[]{:S(2)}, u32[]{:S(2)}) collective-permute-start(bf16[680,128]{1,0:T(8,128)(2,1)S(1)} %get-tuple-element.16), channel_id=1, source_target_pairs={{0,4},{2,6},{4,8},{6,10},{8,12},{10,14},{12,0},{14,2},{1,5},{3,7},... | collective-permute-start | bytes 522248 | tf_op jit(solution)/shard_map/ppermute | solution.py:492
  101.7 28.5 %collective-permute-start.2 = (bf16[680,128]{1,0:T(8,128)(2,1)S(1)}, bf16[680,128]{1,0:T(8,128)(2,1)S(1)}, u32[]{:S(2)}, u32[]{:S(2)}) collective-permute-start(bf16[680,128]{1,0:T(8,128)(2,1)S(1)} %get-tuple-element.17), channel_id=1, source_target_pairs={{0,6},{2,8},{4,10},{6,12},{8,14},{10,0},{12,2},{14,4},{1,7},{3,9},... | collective-permute-start | bytes 522248 | tf_op jit(solution)/shard_map/ppermute | solution.py:492
  105.2 29.1 %collective-permute-start.3 = (bf16[680,128]{1,0:T(8,128)(2,1)S(1)}, bf16[680,128]{1,0:T(8,128)(2,1)S(1)}, u32[]{:S(2)}, u32[]{:S(2)}) collective-permute-start(bf16[680,128]{1,0:T(8,128)(2,1)S(1)} %get-tuple-element.18), channel_id=1, source_target_pairs={{0,8},{2,10},{4,12},{6,14},{8,0},{10,2},{12,4},{14,6},{1,9},{3,11}... | collective-permute-start | bytes 522248 | tf_op jit(solution)/shard_map/ppermute | solution.py:492
  117.6 19.8 %collective-permute-start.4 = (bf16[680,128]{1,0:T(8,128)(2,1)S(1)}, bf16[680,128]{1,0:T(8,128)(2,1)S(1)}, u32[]{:S(2)}, u32[]{:S(2)}) collective-permute-start(bf16[680,128]{1,0:T(8,128)(2,1)S(1)} %get-tuple-element.19), channel_id=1, source_target_pairs={{0,10},{2,12},{4,14},{6,0},{8,2},{10,4},{12,6},{14,8},{1,11},{3,13... | collective-permute-start | bytes 522248 | tf_op jit(solution)/shard_map/ppermute | solution.py:492
  120.2 17.8 %collective-permute-start.5 = (bf16[680,128]{1,0:T(8,128)(2,1)S(1)}, bf16[680,128]{1,0:T(8,128)(2,1)S(1)}, u32[]{:S(2)}, u32[]{:S(2)}) collective-permute-start(bf16[680,128]{1,0:T(8,128)(2,1)S(1)} %get-tuple-element.20), channel_id=1, source_target_pairs={{0,12},{2,14},{4,0},{6,2},{8,4},{10,6},{12,8},{14,10},{1,13},{3,15... | collective-permute-start | bytes 522248 | tf_op jit(solution)/shard_map/ppermute | solution.py:492
  128.3 14.3 %collective-permute-start.6 = (bf16[680,128]{1,0:T(8,128)(2,1)S(1)}, bf16[680,128]{1,0:T(8,128)(2,1)S(1)}, u32[]{:S(2)}, u32[]{:S(2)}) collective-permute-start(bf16[680,128]{1,0:T(8,128)(2,1)S(1)} %get-tuple-element.21), channel_id=1, source_target_pairs={{0,14},{2,0},{4,2},{6,4},{8,6},{10,8},{12,10},{14,12},{1,15},{3,1}... | collective-permute-start | bytes 522248 | tf_op jit(solution)/shard_map/ppermute | solution.py:492
  130.3 12.3 %copy-start.4 = (s32[16]{0:T(128)S(1)}, s32[16]{0:T(128)}, u32[]{:S(2)}) copy-start(s32[16]{0:T(128)} %len_ref.1) | copy-start | bytes 196
  130.3 13.6 %collective-permute-start.10 = (bf16[448,128]{1,0:T(8,128)(2,1)S(1)}, bf16[448,128]{1,0:T(8,128)(2,1)S(1)}, u32[]{:S(2)}, u32[]{:S(2)}) collective-permute-start(bf16[448,128]{1,0:T(8,128)(2,1)S(1)} %slice.8), channel_id=1, source_target_pairs={{0,2},{2,4},{4,6},{6,8},{8,10},{10,12},{12,14},{14,0},{1,3},{3,5},... | collective-permute-start | bytes 344072 | tf_op jit(solution)/shard_map/ppermute | solution.py:492
  134.3 9.7 %collective-permute-start.14 = (bf16[448,128]{1,0:T(8,128)(2,1)S(1)}, bf16[448,128]{1,0:T(8,128)(2,1)S(1)}, u32[]{:S(2)}, u32[]{:S(2)}) collective-permute-start(bf16[448,128]{1,0:T(8,128)(2,1)S(1)} %slice.9), channel_id=1, source_target_pairs={{0,14},{2,0},{4,2},{6,4},{8,6},{10,8},{12,10},{14,12},{1,15},{3,1}... | collective-permute-start | bytes 344072 | tf_op jit(solution)/shard_map/ppermute | solution.py:492
  147.4 23.7 %all-to-all-start.1 = ((bf16[8,336,128]{2,1,0:T(8,128)(2,1)}), bf16[8,336,128]{2,1,0:T(8,128)(2,1)S(1)}, u32[]{:S(2)}, u32[]{:S(2)}) async-start(bf16[8,336,128]{2,1,0:T(8,128)(2,1)} %units.1), calls=%async_computation.1 | async-start | bytes 1376256 | tf_op jit(solution)/shard_map/all_to_all | solution.py:31
  171.1 28.4 %copy-start.1 = (bf16[448,576]{1,0:T(8,128)(2,1)S(1)}, bf16[448,576]{1,0:T(8,128)(2,1)}, u32[]{:S(2)}) copy-start(bf16[448,576]{1,0:T(8,128)(2,1)} %wdkv_ref.1) | copy-start | bytes 1548292
  172.5 27.0 %copy-start.2 = (bf16[16,448]{1,0:T(8,128)(2,1)S(1)}, bf16[16,448]{1,0:T(8,128)(2,1)}, u32[]{:S(2)}) copy-start(bf16[16,448]{1,0:T(8,128)(2,1)} %hid_ref.1) | copy-start | bytes 43012
  172.5 27.0 %all-to-all-start.2 = ((bf16[32,8,448]{2,1,0:T(8,128)(2,1)}), bf16[32,8,448]{2,1,0:T(8,128)(2,1)S(1)}, u32[]{:S(2)}, u32[]{:S(2)}) async-start(bf16[32,8,448]{2,1,0:T(8,128)(2,1)} %down.1), calls=%async_computation.2 | async-start | bytes 524288 | tf_op jit(solution)/shard_map/all_to_all | solution.py:31
  177.5 22.0 %copy-start.3 = (f32[448]{0:T(512)S(1)}, f32[448]{0:T(512)}, u32[]{:S(2)}) copy-start(f32[448]{0:T(512)} %param.22) | copy-start | bytes 5380
  200.6 3.9 %copy-start.5 = (f32[512]{0:T(512)S(1)}, f32[512]{0:T(512)}, u32[]{:S(2)}) copy-start(f32[512]{0:T(512)} %param.24) | copy-start | bytes 6148
  200.6 13.6 %all-to-all-start.3 = ((bf16[8,16,640]{2,1,0:T(8,128)(2,1)}), bf16[8,16,640]{2,1,0:T(8,128)(2,1)S(1)}, u32[]{:S(2)}, u32[]{:S(2)}) async-start(bf16[8,16,640]{2,1,0:T(8,128)(2,1)} %get-tuple-element.25), calls=%async_computation.3 | async-start | bytes 327680 | tf_op jit(solution)/shard_map/all_to_all | solution.py:31
  204.3 9.9 %copy-start = (bf16[16,8,576]{2,1,0:T(8,128)(2,1)S(1)}, bf16[16,8,576]{2,1,0:T(8,128)(2,1)}, u32[]{:S(2)}) copy-start(bf16[16,8,576]{2,1,0:T(8,128)(2,1)} %q_ref.1) | copy-start | bytes 442372

commit v9 on v8

--- a/solution.py
+++ b/solution.py
@@ -72,12 +72,31 @@
     return [total[q : q + 1, : min(128, width - 128 * q)] for q in range(tiles)]
 
 
-def units_kernel(me_ref, wg_hbm, wu_hbm, att_ref, *refs):
+def beside_kernel(wg_hbm, wu_hbm, o_ref, sems):
+    hid = wg_hbm.shape[1]
+    copies = fetch((wg_hbm, wu_hbm), (o_ref.at[:, :hid], o_ref.at[:, hid:]), sems)
+    for copy in copies:
+        copy.wait()
+
+
+def beside(w_gate, w_up):
+    rows, hid = w_gate.shape
+    return pl.pallas_call(
+        beside_kernel,
+        out_shape=shape((rows, 2 * hid), bf16),
+        in_specs=[HBM, HBM],
+        out_specs=VMEM,
+        scratch_shapes=[pltpu.SemaphoreType.DMA((2,))],
+        compiler_params=PARAMS,
+        name="beside",
+    )(in_hbm(w_gate), in_hbm(w_up))
+
+
+def units_kernel(me_ref, w_ref, att_ref, *refs):
     peers = att_ref.shape[0]
     blocks, parts = refs[:peers], refs[peers : 2 * peers + 1]
-    o_ref, w_ref, n_ref, h_ref, sems = refs[2 * peers + 1 :]
-    hid = wg_hbm.shape[1]
-    copies = fetch((wg_hbm, wu_hbm), (w_ref.at[:, :hid], w_ref.at[:, hid:]), sems)
+    o_ref, n_ref, h_ref = refs[2 * peers + 1 :]
+    hid = w_ref.shape[1] // 2
     _, rows, cols = n_ref.shape
     middle, tiles = peers // 2, cols // 128
     square = jnp.zeros((rows, 1), f32)
@@ -100,9 +119,6 @@
         square = square + jnp.sum(x * x, -1, keepdims=True)
         j = lax.rem(me_ref[0] + (peers - k), peers)
         gain = jnp.concatenate(gain_of(blocks[k], blocks[k].shape[0] - 16, cols), 1)
-        if k == 0:
-            copies[0].wait()
-            copies[1].wait()
         part = pl.ds(pl.multiple_of(j * cols, 64), cols)
         both = jnp.dot((x * gain).astype(bf16), w_ref[part, :], preferred_element_type=f32)
         if k == 0:
@@ -117,24 +133,22 @@
         o_ref[j, :rows, :] = units
 
 
-def expert_units(me, parts, w_gate, w_up, attended, blocks):
+def expert_units(me, parts, weights, attended, blocks):
     peers = len(blocks)
-    cols, hid = w_gate.shape[0] // peers, w_gate.shape[1]
+    cols, hid = weights.shape[0] // peers, weights.shape[1] // 2
     rows = parts[0].shape[0] * 128 // cols
     return pl.pallas_call(
         units_kernel,
         out_shape=shape((peers, rows + attended.shape[1], hid), bf16),
-        in_specs=[SMEM, HBM, HBM] + [VMEM] * (2 * peers + 2),
+        in_specs=[SMEM] + [VMEM] * (2 * peers + 3),
         out_specs=VMEM,
         scratch_shapes=[
-            pltpu.VMEM((w_gate.shape[0], 2 * hid), bf16),
             pltpu.VMEM((peers, rows, cols), bf16),
             pltpu.VMEM((rows, 2 * hid), f32),
-            pltpu.SemaphoreType.DMA((2,)),
         ],
         compiler_params=PARAMS,
         name="units",
-    )(me, in_hbm(w_gate), in_hbm(w_up), attended, *blocks, *parts)
+    )(me, weights, attended, *blocks, *parts)
 
 
 def pack_kernel(me_ref, *refs):
@@ -510,7 +524,7 @@
     parts = ring(packed_rows(arrived), moved, peers)
     span, heads, keys = cache.shape[1], queries.shape[1], queries.shape[2]
     attended = attend(me, lengths, blocks, seqs // peers, span, heads, keys)
-    units = expert_units(me, parts, w_gate[0], w_up[0], attended, blocks)
+    units = expert_units(me, parts, beside(w_gate[0], w_up[0]), attended, blocks)
     all_units = exchange(units, "tp")
     columns = columns_of(blocks, w_down.shape[1], width)
     output = expert_down(me, all_units, columns, experts)

time: 216 us -> 214 us (level)
  transfers between devices with their start and end apart: 18 -> 18, of which waited for: 8 -> 7; matrix products, arithmetic and copies ran while one was open for 0% -> 0% of each run, Pallas kernels for 1% -> 1%
where the time goes in v9:
time: 214 us
  waiting for transfers between devices  68 us (32%)
  starting transfers between devices  67.2 us (31%)
  blocking collectives  66.2 us (31%)
  Pallas kernels  10.8 us (5%)
    all_to_all x1, blocking collectives, exchange(): return lax.all_to_all(x, axis, split_axis=0, concat_axis=0, tiled=True)  66.2 us
    ppermute x15, starting transfers between devices, moved(): return lax.ppermute(x, 'tp', [(i, (i + k) % peers) for i in range(peers)])  54.8 us
    all_to_all x3, waiting for transfers between devices, exchange(): return lax.all_to_all(x, axis, split_axis=0, concat_axis=0, tiled=True)  51 us
    ppermute x15, waiting for transfers between devices, moved(): return lax.ppermute(x, 'tp', [(i, (i + k) % peers) for i in range(peers)])  17 us
    all_to_all x3, starting transfers between devices, exchange(): return lax.all_to_all(x, axis, split_axis=0, concat_axis=0, tiled=True)  12.4 us
  transfers between devices with their start and end apart: 18, of which 7 were waited for; matrix products, arithmetic and copies ran while one was open for 0% of the time, Pallas kernels for 1%

profile of v9, /device:TPU:80, one launch (start us, length us, event | category | flops | bytes accessed | tf_op | source)
XLA Modules:
  0.0 213.6 jit_solution(7810550100067738717)
XLA Ops:
  0.6 2.1 pack.1
  2.7 66.2 %all_to_all.20.x_ref = bf16[32,8,448]{2,1,0:T(8,128)(2,1)S(1)} all-to-all(bf16[32,8,448]{2,1,0:T(8,128)(2,1)S(1)} %get-tuple-element.22), channel_id=1, replica_groups=mesh['grp'=2,'ep'=16,'tp'=8,'mb'=2] {'ep','mb'}, dimensions={0} | all-to-all | bytes 458752 | tf_op jit(solution)/shard_map/all_to_all | solution.py:31
  69.0 0.1 rows.1.refs_8_
  69.1 3.6 %collective-permute-start.7 = (bf16[896,128]{1,0:T(8,128)(2,1)S(1)}, bf16[896,128]{1,0:T(8,128)(2,1)S(1)}, u32[]{:S(2)}, u32[]{:S(2)}) collective-permute-start(bf16[896,128]{1,0:T(8,128)(2,1)S(1)} %rows.1.refs_8_), channel_id=1, source_target_pairs={{0,2},{2,4},{4,6},{6,8},{8,10},{10,12},{12,14},{14,0},{1,3},{3,5},... | collective-permute-start | bytes 688136 | tf_op jit(solution)/shard_map/ppermute | solution.py:506
  72.6 4.1 %collective-permute-start.11 = (bf16[896,128]{1,0:T(8,128)(2,1)S(1)}, bf16[896,128]{1,0:T(8,128)(2,1)S(1)}, u32[]{:S(2)}, u32[]{:S(2)}) collective-permute-start(bf16[896,128]{1,0:T(8,128)(2,1)S(1)} %rows.1.refs_8_), channel_id=1, source_target_pairs={{0,14},{2,0},{4,2},{6,4},{8,6},{10,8},{12,10},{14,12},{1,15},{3,1}... | collective-permute-start | bytes 688136 | tf_op jit(solution)/shard_map/ppermute | solution.py:506
  76.8 3.7 %collective-permute-done.7.refs_9_ = bf16[896,128]{1,0:T(8,128)(2,1)S(1)} collective-permute-done((bf16[896,128]{1,0:T(8,128)(2,1)S(1)}, bf16[896,128]{1,0:T(8,128)(2,1)S(1)}, u32[]{:S(2)}, u32[]{:S(2)}) %collective-permute-start.7) | collective-permute-done | bytes 229408 | tf_op jit(solution)/shard_map/ppermute | solution.py:506
  80.5 1.9 collective-permute-start.8
  82.5 0.0 collective-permute-done.11.refs_16_
  82.5 5.2 %collective-permute-start.12 = (bf16[896,128]{1,0:T(8,128)(2,1)S(1)}, bf16[896,128]{1,0:T(8,128)(2,1)S(1)}, u32[]{:S(2)}, u32[]{:S(2)}) collective-permute-start(bf16[896,128]{1,0:T(8,128)(2,1)S(1)} %collective-permute-done.11.refs_16_), channel_id=1, source_target_pairs={{0,14},{2,0},{4,2},{6,4},{8,6},{10,8},{12,10},{14,12},{1,15},{3,1}... | collective-permute-start | bytes 688136 | tf_op jit(solution)/shard_map/ppermute | solution.py:506
  87.6 2.0 collective-permute-start
  89.6 0.9 collective-permute-done.8.refs_10_
  90.5 1.9 collective-permute-start.9
  92.4 5.2 %collective-permute-start.13 = (bf16[896,128]{1,0:T(8,128)(2,1)S(1)}, bf16[896,128]{1,0:T(8,128)(2,1)S(1)}, u32[]{:S(2)}, u32[]{:S(2)}) collective-permute-start(bf16[896,128]{1,0:T(8,128)(2,1)S(1)} %collective-permute-done.12.refs_15_), channel_id=1, source_target_pairs={{0,14},{2,0},{4,2},{6,4},{8,6},{10,8},{12,10},{14,12},{1,15},{3,1}... | collective-permute-start | bytes 688136 | tf_op jit(solution)/shard_map/ppermute | solution.py:506
  97.6 4.1 %collective-permute-start.1 = (bf16[680,128]{1,0:T(8,128)(2,1)S(1)}, bf16[680,128]{1,0:T(8,128)(2,1)S(1)}, u32[]{:S(2)}, u32[]{:S(2)}) collective-permute-start(bf16[680,128]{1,0:T(8,128)(2,1)S(1)} %get-tuple-element.16), channel_id=1, source_target_pairs={{0,4},{2,6},{4,8},{6,10},{8,12},{10,14},{12,0},{14,2},{1,5},{3,7},... | collective-permute-start | bytes 522248 | tf_op jit(solution)/shard_map/ppermute | solution.py:506
  101.7 3.4 %collective-permute-start.2 = (bf16[680,128]{1,0:T(8,128)(2,1)S(1)}, bf16[680,128]{1,0:T(8,128)(2,1)S(1)}, u32[]{:S(2)}, u32[]{:S(2)}) collective-permute-start(bf16[680,128]{1,0:T(8,128)(2,1)S(1)} %get-tuple-element.17), channel_id=1, source_target_pairs={{0,6},{2,8},{4,10},{6,12},{8,14},{10,0},{12,2},{14,4},{1,7},{3,9},... | collective-permute-start | bytes 522248 | tf_op jit(solution)/shard_map/ppermute | solution.py:506
  105.2 3.7 %collective-permute-start.3 = (bf16[680,128]{1,0:T(8,128)(2,1)S(1)}, bf16[680,128]{1,0:T(8,128)(2,1)S(1)}, u32[]{:S(2)}, u32[]{:S(2)}) collective-permute-start(bf16[680,128]{1,0:T(8,128)(2,1)S(1)} %get-tuple-element.18), channel_id=1, source_target_pairs={{0,8},{2,10},{4,12},{6,14},{8,0},{10,2},{12,4},{14,6},{1,9},{3,11}... | collective-permute-start | bytes 522248 | tf_op jit(solution)/shard_map/ppermute | solution.py:506
  108.9 8.7 %collective-permute-done.1.refs_2_ = bf16[680,128]{1,0:T(8,128)(2,1)S(1)} collective-permute-done((bf16[680,128]{1,0:T(8,128)(2,1)S(1)}, bf16[680,128]{1,0:T(8,128)(2,1)S(1)}, u32[]{:S(2)}, u32[]{:S(2)}) %collective-permute-start.1) | collective-permute-done | bytes 174112 | tf_op jit(solution)/shard_map/ppermute | solution.py:506
  117.6 2.5 %collective-permute-start.4 = (bf16[680,128]{1,0:T(8,128)(2,1)S(1)}, bf16[680,128]{1,0:T(8,128)(2,1)S(1)}, u32[]{:S(2)}, u32[]{:S(2)}) collective-permute-start(bf16[680,128]{1,0:T(8,128)(2,1)S(1)} %get-tuple-element.19), channel_id=1, source_target_pairs={{0,10},{2,12},{4,14},{6,0},{8,2},{10,4},{12,6},{14,8},{1,11},{3,13... | collective-permute-start | bytes 522248 | tf_op jit(solution)/shard_map/ppermute | solution.py:506
  120.2 0.0 collective-permute-done.9.refs_11_
  120.2 8.1 %collective-permute-start.5 = (bf16[680,128]{1,0:T(8,128)(2,1)S(1)}, bf16[680,128]{1,0:T(8,128)(2,1)S(1)}, u32[]{:S(2)}, u32[]{:S(2)}) collective-permute-start(bf16[680,128]{1,0:T(8,128)(2,1)S(1)} %get-tuple-element.20), channel_id=1, source_target_pairs={{0,12},{2,14},{4,0},{6,2},{8,4},{10,6},{12,8},{14,10},{1,13},{3,15... | collective-permute-start | bytes 522248 | tf_op jit(solution)/shard_map/ppermute | solution.py:506
  128.3 0.0 collective-permute-done.13.refs_14_
  128.3 2.0 collective-permute-start.6
  130.3 0.0 collective-permute-done.2.refs_3_
  130.3 4.0 %collective-permute-start.10 = (bf16[448,128]{1,0:T(8,128)(2,1)S(1)}, bf16[448,128]{1,0:T(8,128)(2,1)S(1)}, u32[]{:S(2)}, u32[]{:S(2)}) collective-permute-start(bf16[448,128]{1,0:T(8,128)(2,1)S(1)} %slice.8), channel_id=1, source_target_pairs={{0,2},{2,4},{4,6},{6,8},{8,10},{10,12},{12,14},{14,0},{1,3},{3,5},... | collective-permute-start | bytes 344072 | tf_op jit(solution)/shard_map/ppermute | solution.py:506
  134.2 3.2 %collective-permute-start.14 = (bf16[448,128]{1,0:T(8,128)(2,1)S(1)}, bf16[448,128]{1,0:T(8,128)(2,1)S(1)}, u32[]{:S(2)}, u32[]{:S(2)}) collective-permute-start(bf16[448,128]{1,0:T(8,128)(2,1)S(1)} %slice.9), channel_id=1, source_target_pairs={{0,14},{2,0},{4,2},{6,4},{8,6},{10,8},{12,10},{14,12},{1,15},{3,1}... | collective-permute-start | bytes 344072 | tf_op jit(solution)/shard_map/ppermute | solution.py:506
  137.4 0.0 copy-start.4
  137.4 1.5 beside.1.w_ref
  138.9 0.0 collective-permute-done.5.refs_6_
  138.9 3.7 %collective-permute-done.6.refs_7_ = bf16[680,128]{1,0:T(8,128)(2,1)S(1)} collective-permute-done((bf16[680,128]{1,0:T(8,128)(2,1)S(1)}, bf16[680,128]{1,0:T(8,128)(2,1)S(1)}, u32[]{:S(2)}, u32[]{:S(2)}) %collective-permute-start.6) | collective-permute-done | bytes 174112 | tf_op jit(solution)/shard_map/ppermute | solution.py:506
  142.6 1.3 attend.1.att_ref
  143.9 2.0 units.1
  145.9 3.9 %all-to-all-start.1 = ((bf16[8,336,128]{2,1,0:T(8,128)(2,1)}), bf16[8,336,128]{2,1,0:T(8,128)(2,1)S(1)}, u32[]{:S(2)}, u32[]{:S(2)}) async-start(bf16[8,336,128]{2,1,0:T(8,128)(2,1)} %units.1), calls=%async_computation.1 | async-start | bytes 1376256 | tf_op jit(solution)/shard_map/all_to_all | solution.py:31
  149.8 0.3 columns.1.w_ref
  150.2 0.0 copy-start.1
  150.2 0.0 copy-start.2
  150.2 0.0 copy-start.3
  150.2 0.0 copy-start.5
  150.2 0.0 copy-start
  150.2 19.4 %all-to-all-done.1.u_ref.units_ref = bf16[8,336,128]{2,1,0:T(8,128)(2,1)S(1)} async-done(((bf16[8,336,128]{2,1,0:T(8,128)(2,1)}), bf16[8,336,128]{2,1,0:T(8,128)(2,1)S(1)}, u32[]{:S(2)}, u32[]{:S(2)}) %all-to-all-start.1) | async-done | bytes 688160 | tf_op jit(solution)/shard_map/all_to_all | solution.py:31
  169.6 1.4 down.1
  171.0 4.9 %all-to-all-start.2 = ((bf16[32,8,448]{2,1,0:T(8,128)(2,1)}), bf16[32,8,448]{2,1,0:T(8,128)(2,1)S(1)}, u32[]{:S(2)}, u32[]{:S(2)}) async-start(bf16[32,8,448]{2,1,0:T(8,128)(2,1)} %down.1), calls=%async_computation.2 | async-start | bytes 524288 | tf_op jit(solution)/shard_map/all_to_all | solution.py:31
  175.9 22.0 %all-to-all-done.2.ret_ref = bf16[32,8,448]{2,1,0:T(8,128)(2,1)S(1)} async-done(((bf16[32,8,448]{2,1,0:T(8,128)(2,1)}), bf16[32,8,448]{2,1,0:T(8,128)(2,1)S(1)}, u32[]{:S(2)}, u32[]{:S(2)}) %all-to-all-start.2) | async-done | bytes 229408 | tf_op jit(solution)/shard_map/all_to_all | solution.py:31
  197.9 1.1 close.1
  199.0 3.6 %all-to-all-start.3 = ((bf16[8,16,640]{2,1,0:T(8,128)(2,1)}), bf16[8,16,640]{2,1,0:T(8,128)(2,1)S(1)}, u32[]{:S(2)}, u32[]{:S(2)}) async-start(bf16[8,16,640]{2,1,0:T(8,128)(2,1)} %get-tuple-element.25), calls=%async_computation.3 | async-start | bytes 327680 | tf_op jit(solution)/shard_map/all_to_all | solution.py:31
  202.6 0.1 multiply_sine_fusion
  202.7 0.1 concatenate.3.table_ref
  202.8 9.6 %all-to-all-done.3.all_ref = bf16[8,16,640]{2,1,0:T(8,128)(2,1)S(1)} async-done(((bf16[8,16,640]{2,1,0:T(8,128)(2,1)}), bf16[8,16,640]{2,1,0:T(8,128)(2,1)S(1)}, u32[]{:S(2)}, u32[]{:S(2)}) %all-to-all-start.3) | async-done | bytes 163872 | tf_op jit(solution)/shard_map/all_to_all | solution.py:31
  212.4 1.1 merge.1
  (17 shorter events, 0.1 us)
Async XLA Ops:
  69.1 11.4 %collective-permute-start.7 = (bf16[896,128]{1,0:T(8,128)(2,1)S(1)}, bf16[896,128]{1,0:T(8,128)(2,1)S(1)}, u32[]{:S(2)}, u32[]{:S(2)}) collective-permute-start(bf16[896,128]{1,0:T(8,128)(2,1)S(1)} %rows.1.refs_8_), channel_id=1, source_target_pairs={{0,2},{2,4},{4,6},{6,8},{8,10},{10,12},{12,14},{14,0},{1,3},{3,5},... | collective-permute-start | bytes 688136 | tf_op jit(solution)/shard_map/ppermute | solution.py:506
  72.6 9.8 %collective-permute-start.11 = (bf16[896,128]{1,0:T(8,128)(2,1)S(1)}, bf16[896,128]{1,0:T(8,128)(2,1)S(1)}, u32[]{:S(2)}, u32[]{:S(2)}) collective-permute-start(bf16[896,128]{1,0:T(8,128)(2,1)S(1)} %rows.1.refs_8_), channel_id=1, source_target_pairs={{0,14},{2,0},{4,2},{6,4},{8,6},{10,8},{12,10},{14,12},{1,15},{3,1}... | collective-permute-start | bytes 688136 | tf_op jit(solution)/shard_map/ppermute | solution.py:506
  80.5 10.0 %collective-permute-start.8 = (bf16[896,128]{1,0:T(8,128)(2,1)S(1)}, bf16[896,128]{1,0:T(8,128)(2,1)S(1)}, u32[]{:S(2)}, u32[]{:S(2)}) collective-permute-start(bf16[896,128]{1,0:T(8,128)(2,1)S(1)} %collective-permute-done.7.refs_9_), channel_id=1, source_target_pairs={{0,2},{2,4},{4,6},{6,8},{8,10},{10,12},{12,14},{14,0},{1,3},{3,5},... | collective-permute-start | bytes 688136 | tf_op jit(solution)/shard_map/ppermute | solution.py:506
  82.5 10.0 %collective-permute-start.12 = (bf16[896,128]{1,0:T(8,128)(2,1)S(1)}, bf16[896,128]{1,0:T(8,128)(2,1)S(1)}, u32[]{:S(2)}, u32[]{:S(2)}) collective-permute-start(bf16[896,128]{1,0:T(8,128)(2,1)S(1)} %collective-permute-done.11.refs_16_), channel_id=1, source_target_pairs={{0,14},{2,0},{4,2},{6,4},{8,6},{10,8},{12,10},{14,12},{1,15},{3,1}... | collective-permute-start | bytes 688136 | tf_op jit(solution)/shard_map/ppermute | solution.py:506
  87.6 17.5 %collective-permute-start = (bf16[680,128]{1,0:T(8,128)(2,1)S(1)}, bf16[680,128]{1,0:T(8,128)(2,1)S(1)}, u32[]{:S(2)}, u32[]{:S(2)}) collective-permute-start(bf16[680,128]{1,0:T(8,128)(2,1)S(1)} %get-tuple-element.15), channel_id=1, source_target_pairs={{0,2},{2,4},{4,6},{6,8},{8,10},{10,12},{12,14},{14,0},{1,3},{3,5},... | collective-permute-start | bytes 522248 | tf_op jit(solution)/shard_map/ppermute | solution.py:506
  90.5 29.7 %collective-permute-start.9 = (bf16[896,128]{1,0:T(8,128)(2,1)S(1)}, bf16[896,128]{1,0:T(8,128)(2,1)S(1)}, u32[]{:S(2)}, u32[]{:S(2)}) collective-permute-start(bf16[896,128]{1,0:T(8,128)(2,1)S(1)} %collective-permute-done.8.refs_10_), channel_id=1, source_target_pairs={{0,2},{2,4},{4,6},{6,8},{8,10},{10,12},{12,14},{14,0},{1,3},{3,5},... | collective-permute-start | bytes 688136 | tf_op jit(solution)/shard_map/ppermute | solution.py:506
  92.4 35.8 %collective-permute-start.13 = (bf16[896,128]{1,0:T(8,128)(2,1)S(1)}, bf16[896,128]{1,0:T(8,128)(2,1)S(1)}, u32[]{:S(2)}, u32[]{:S(2)}) collective-permute-start(bf16[896,128]{1,0:T(8,128)(2,1)S(1)} %collective-permute-done.12.refs_15_), channel_id=1, source_target_pairs={{0,14},{2,0},{4,2},{6,4},{8,6},{10,8},{12,10},{14,12},{1,15},{3,1}... | collective-permute-start | bytes 688136 | tf_op jit(solution)/shard_map/ppermute | solution.py:506
  97.6 20.0 %collective-permute-start.1 = (bf16[680,128]{1,0:T(8,128)(2,1)S(1)}, bf16[680,128]{1,0:T(8,128)(2,1)S(1)}, u32[]{:S(2)}, u32[]{:S(2)}) collective-permute-start(bf16[680,128]{1,0:T(8,128)(2,1)S(1)} %get-tuple-element.16), channel_id=1, source_target_pairs={{0,4},{2,6},{4,8},{6,10},{8,12},{10,14},{12,0},{14,2},{1,5},{3,7},... | collective-permute-start | bytes 522248 | tf_op jit(solution)/shard_map/ppermute | solution.py:506
  101.7 28.5 %collective-permute-start.2 = (bf16[680,128]{1,0:T(8,128)(2,1)S(1)}, bf16[680,128]{1,0:T(8,128)(2,1)S(1)}, u32[]{:S(2)}, u32[]{:S(2)}) collective-permute-start(bf16[680,128]{1,0:T(8,128)(2,1)S(1)} %get-tuple-element.17), channel_id=1, source_target_pairs={{0,6},{2,8},{4,10},{6,12},{8,14},{10,0},{12,2},{14,4},{1,7},{3,9},... | collective-permute-start | bytes 522248 | tf_op jit(solution)/shard_map/ppermute | solution.py:506
  105.2 29.0 %collective-permute-start.3 = (bf16[680,128]{1,0:T(8,128)(2,1)S(1)}, bf16[680,128]{1,0:T(8,128)(2,1)S(1)}, u32[]{:S(2)}, u32[]{:S(2)}) collective-permute-start(bf16[680,128]{1,0:T(8,128)(2,1)S(1)} %get-tuple-element.18), channel_id=1, source_target_pairs={{0,8},{2,10},{4,12},{6,14},{8,0},{10,2},{12,4},{14,6},{1,9},{3,11}... | collective-permute-start | bytes 522248 | tf_op jit(solution)/shard_map/ppermute | solution.py:506
  117.6 21.3 %collective-permute-start.4 = (bf16[680,128]{1,0:T(8,128)(2,1)S(1)}, bf16[680,128]{1,0:T(8,128)(2,1)S(1)}, u32[]{:S(2)}, u32[]{:S(2)}) collective-permute-start(bf16[680,128]{1,0:T(8,128)(2,1)S(1)} %get-tuple-element.19), channel_id=1, source_target_pairs={{0,10},{2,12},{4,14},{6,0},{8,2},{10,4},{12,6},{14,8},{1,11},{3,13... | collective-permute-start | bytes 522248 | tf_op jit(solution)/shard_map/ppermute | solution.py:506
  120.2 18.8 %collective-permute-start.5 = (bf16[680,128]{1,0:T(8,128)(2,1)S(1)}, bf16[680,128]{1,0:T(8,128)(2,1)S(1)}, u32[]{:S(2)}, u32[]{:S(2)}) collective-permute-start(bf16[680,128]{1,0:T(8,128)(2,1)S(1)} %get-tuple-element.20), channel_id=1, source_target_pairs={{0,12},{2,14},{4,0},{6,2},{8,4},{10,6},{12,8},{14,10},{1,13},{3,15... | collective-permute-start | bytes 522248 | tf_op jit(solution)/shard_map/ppermute | solution.py:506
  128.3 14.3 %collective-permute-start.6 = (bf16[680,128]{1,0:T(8,128)(2,1)S(1)}, bf16[680,128]{1,0:T(8,128)(2,1)S(1)}, u32[]{:S(2)}, u32[]{:S(2)}) collective-permute-start(bf16[680,128]{1,0:T(8,128)(2,1)S(1)} %get-tuple-element.21), channel_id=1, source_target_pairs={{0,14},{2,0},{4,2},{6,4},{8,6},{10,8},{12,10},{14,12},{1,15},{3,1}... | collective-permute-start | bytes 522248 | tf_op jit(solution)/shard_map/ppermute | solution.py:506
  130.3 13.7 %collective-permute-start.10 = (bf16[448,128]{1,0:T(8,128)(2,1)S(1)}, bf16[448,128]{1,0:T(8,128)(2,1)S(1)}, u32[]{:S(2)}, u32[]{:S(2)}) collective-permute-start(bf16[448,128]{1,0:T(8,128)(2,1)S(1)} %slice.8), channel_id=1, source_target_pairs={{0,2},{2,4},{4,6},{6,8},{8,10},{10,12},{12,14},{14,0},{1,3},{3,5},... | collective-permute-start | bytes 344072 | tf_op jit(solution)/shard_map/ppermute | solution.py:506
  134.2 9.7 %collective-permute-start.14 = (bf16[448,128]{1,0:T(8,128)(2,1)S(1)}, bf16[448,128]{1,0:T(8,128)(2,1)S(1)}, u32[]{:S(2)}, u32[]{:S(2)}) collective-permute-start(bf16[448,128]{1,0:T(8,128)(2,1)S(1)} %slice.9), channel_id=1, source_target_pairs={{0,14},{2,0},{4,2},{6,4},{8,6},{10,8},{12,10},{14,12},{1,15},{3,1}... | collective-permute-start | bytes 344072 | tf_op jit(solution)/shard_map/ppermute | solution.py:506
  137.4 5.2 %copy-start.4 = (s32[16]{0:T(128)S(1)}, s32[16]{0:T(128)}, u32[]{:S(2)}) copy-start(s32[16]{0:T(128)} %len_ref.1) | copy-start | bytes 196
  145.9 23.7 %all-to-all-start.1 = ((bf16[8,336,128]{2,1,0:T(8,128)(2,1)}), bf16[8,336,128]{2,1,0:T(8,128)(2,1)S(1)}, u32[]{:S(2)}, u32[]{:S(2)}) async-start(bf16[8,336,128]{2,1,0:T(8,128)(2,1)} %units.1), calls=%async_computation.1 | async-start | bytes 1376256 | tf_op jit(solution)/shard_map/all_to_all | solution.py:31
  150.2 47.7 %copy-start.1 = (bf16[448,576]{1,0:T(8,128)(2,1)S(1)}, bf16[448,576]{1,0:T(8,128)(2,1)}, u32[]{:S(2)}) copy-start(bf16[448,576]{1,0:T(8,128)(2,1)} %wdkv_ref.1) | copy-start | bytes 1548292
  150.2 47.7 %copy-start.2 = (bf16[16,448]{1,0:T(8,128)(2,1)S(1)}, bf16[16,448]{1,0:T(8,128)(2,1)}, u32[]{:S(2)}) copy-start(bf16[16,448]{1,0:T(8,128)(2,1)} %hid_ref.1) | copy-start | bytes 43012
  150.2 47.7 %copy-start.3 = (f32[448]{0:T(512)S(1)}, f32[448]{0:T(512)}, u32[]{:S(2)}) copy-start(f32[448]{0:T(512)} %param.22) | copy-start | bytes 5380
  150.2 52.5 %copy-start.5 = (f32[512]{0:T(512)S(1)}, f32[512]{0:T(512)}, u32[]{:S(2)}) copy-start(f32[512]{0:T(512)} %param.24) | copy-start | bytes 6148
  150.2 62.2 %copy-start = (bf16[16,8,576]{2,1,0:T(8,128)(2,1)S(1)}, bf16[16,8,576]{2,1,0:T(8,128)(2,1)}, u32[]{:S(2)}) copy-start(bf16[16,8,576]{2,1,0:T(8,128)(2,1)} %q_ref.1) | copy-start | bytes 442372
  171.0 26.9 %all-to-all-start.2 = ((bf16[32,8,448]{2,1,0:T(8,128)(2,1)}), bf16[32,8,448]{2,1,0:T(8,128)(2,1)S(1)}, u32[]{:S(2)}, u32[]{:S(2)}) async-start(bf16[32,8,448]{2,1,0:T(8,128)(2,1)} %down.1), calls=%async_computation.2 | async-start | bytes 524288 | tf_op jit(solution)/shard_map/all_to_all | solution.py:31
  199.0 13.5 %all-to-all-start.3 = ((bf16[8,16,640]{2,1,0:T(8,128)(2,1)}), bf16[8,16,640]{2,1,0:T(8,128)(2,1)S(1)}, u32[]{:S(2)}, u32[]{:S(2)}) async-start(bf16[8,16,640]{2,1,0:T(8,128)(2,1)} %get-tuple-element.25), calls=%async_computation.3 | async-start | bytes 327680 | tf_op jit(solution)/shard_map/all_to_all | solution.py:31
